TPU v7x, 256 devices: a whole 4x4x8 slice. The times are simulated.
256 devices in a mesh: seq: 32 (over z, y), tp: 8 (over x, core).
Axes of the slice: x: 4, y: 4, z: 8, core: 2. Of those that a mesh axis runs over, the one named last changes fastest.
Arguments:
- query_act: bfloat16 [8192, 4096], P('seq', 'tp'), may hold values from -6 to 6
- key_act: bfloat16 [8192, 1024], P('seq', 'tp'), may hold values from -6 to 6
- value_act: bfloat16 [8192, 1024], P('seq', 'tp'), may hold values from -6 to 6
- attn_out: bfloat16 [8192, 4096], P('seq', 'tp'), may hold values from -6 to 6
- out_grad: bfloat16 [8192, 4096], P('seq', 'tp'), may hold values from -6 to 6
- log_sum: float32 [32, 8192], P('tp', 'seq'), as said below
- positions: int32 [8192], P('seq'), may hold values from 0 to 8191, as said below
- w_query: bfloat16 [4096, 4096], P(None, 'tp'), may hold values from -0.09375 to 0.09375
- w_key: bfloat16 [4096, 1024], P(None, 'tp'), may hold values from -0.09375 to 0.09375
- w_value: bfloat16 [4096, 1024], P(None, 'tp'), may hold values from -0.09375 to 0.09375
Outputs:
- input_grad: bfloat16 [8192, 4096], P('seq', 'tp')
Inputs may be any that keep to these rules, and one draw needn't show every extreme that they name: The rows of one index of seq are two runs of 128 consecutive positions, each run starting at a multiple of 128; all rows together hold every position 0 to 8191 once. log_sum[h, t] lies within 0.5 of log(positions[t] + 1) + 0.5.
All inputs are finite; a program needn't handle non-finite values.
Results may differ from a plain program's by a relative error of at most 0.0057.
Values may be sent and summed in bfloat16 or wider, within the bound.
No kernel may reach another device: no remote copies, remote signals or barrier semaphores. Data moves between devices by JAX's collectives and lax.ppermute only.
A program may use at most 64 MiB of HBM per device.

v0:
```python
import functools

import jax
import jax.numpy as jnp
from jax import lax
from jax.experimental import pallas as pl
from jax.experimental.pallas import tpu as pltpu
from jax.sharding import PartitionSpec as P


HEADS = 32
KV_HEADS = 8
HEAD_DIM = 128
REPEAT = HEADS // KV_HEADS
HALF = HEAD_DIM // 2
CHUNK = 128
ROWS = 256
NZ, NY, NX, NC = 8, 4, 4, 2
LOG2E = 1.4426950408889634
SCALE = HEAD_DIM**-0.5
BF = jnp.bfloat16
F32 = jnp.float32
PIECE = CHUNK + 16
UNROLL = 2
MIB = 1024 * 1024
PREP_LIMIT = 60 * MIB


def dot(a, b, dims, precision=None):
    return lax.dot_general(
        a, b, (dims, ((), ())), preferred_element_type=F32, precision=precision
    )


NN = ((1,), (0,))
NT = ((1,), (1,))


def move_z(value, steps):
    pairs = [
        (z * NY + y, ((z + steps) % NZ) * NY + y) for z in range(NZ) for y in range(NY)
    ]
    return lax.ppermute(value, "seq", pairs)


def move_y(value, steps):
    pairs = [
        (z * NY + y, z * NY + (y + steps) % NY) for z in range(NZ) for y in range(NY)
    ]
    return lax.ppermute(value, "seq", pairs)


def move_x(value, steps):
    pairs = [
        (x * NC + c, ((x + steps) % NX) * NC + c) for x in range(NX) for c in range(NC)
    ]
    return lax.ppermute(value, "tp", pairs)


def swap_core(value):
    pairs = [(x * NC + c, x * NC + 1 - c) for x in range(NX) for c in range(NC)]
    return lax.ppermute(value, "tp", pairs)


def split3(value):
    high = value.astype(BF)
    rest = value - high.astype(F32)
    mid = rest.astype(BF)
    low = (rest - mid.astype(F32)).astype(BF)
    return high, mid, low


def prep_kernel(pos_hbm, q_hbm, do_hbm, o_hbm, lse_hbm, k_hbm, v_hbm, pack_ref, kv_ref, *scratch):
    pos_ref, o_ref, lse_ref, sems = scratch
    copies = [
        pltpu.make_async_copy(pos_hbm, pos_ref, sems.at[0]),
        pltpu.make_async_copy(lse_hbm, lse_ref, sems.at[1]),
        pltpu.make_async_copy(o_hbm, o_ref, sems.at[2]),
        pltpu.make_async_copy(k_hbm, kv_ref.at[0:ROWS, 0:128], sems.at[3]),
        pltpu.make_async_copy(v_hbm, kv_ref.at[0:ROWS, 128:256], sems.at[4]),
    ]
    for c in range(2):
        rows = slice(c * CHUNK, c * CHUNK + CHUNK)
        into = slice(c * PIECE, c * PIECE + CHUNK)
        copies.append(
            pltpu.make_async_copy(do_hbm.at[rows], pack_ref.at[into, 512:1024], sems.at[5 + c])
        )
        copies.append(
            pltpu.make_async_copy(q_hbm.at[rows], pack_ref.at[into, 0:512], sems.at[7 + c])
        )
    for copy in copies:
        copy.start()
    for copy in copies:
        copy.wait()
    ones = jnp.ones((8, HEAD_DIM), F32)
    index = lax.broadcasted_iota(jnp.int32, (16, 256), 0)
    first = (pos_ref[0] // CHUNK).astype(F32)
    second = (pos_ref[CHUNK] // CHUNK).astype(F32)
    kv_ref[ROWS : ROWS + 16, :] = jnp.where(index == 0, first, second).astype(BF)
    for c in range(2):
        base = c * PIECE
        rows = slice(c * CHUNK, c * CHUNK + CHUNK)
        deltas = []
        for h in range(REPEAT):
            dout = pack_ref[base : base + CHUNK, 512 + h * 128 : 640 + h * 128].astype(F32)
            prod = dout * o_ref[rows, h * 128 : h * 128 + 128].astype(F32)
            deltas.append(dot(ones, prod, NT, lax.Precision.HIGHEST)[0:1])
        lse_row = jnp.concatenate([lse_ref[h : h + 1, rows] for h in range(REPEAT)], axis=1)
        delta_row = jnp.concatenate(deltas, axis=1)
        row = jnp.concatenate([lse_row * LOG2E, delta_row * SCALE], axis=1)
        parts = [part.astype(F32) for part in split3(row)]
        parts.append(jnp.full((1, 1024), second if c else first, F32))
        block = jnp.concatenate(parts + [jnp.zeros((12, 1024), F32)], axis=0)
        pack_ref[base + CHUNK : base + PIECE, :] = block.astype(BF)


def attn_kernel(q_sizes, nkv, has_dq, has_dkv, layout, *refs):
    refs = list(refs)

    def take(count):
        out = refs[:count]
        del refs[:count]
        return out

    packs = take(len(q_sizes))
    kvs = take(nkv)
    dq_ins = take(sum(has_dq))
    dkv_ins = take(sum(has_dkv))
    nblocks = sum(q_sizes) // 2
    dq_outs = take(nblocks)
    dkv_outs = take(len(layout))
    qc, doc, ks, vs, kts, rowc, dq_acc, dk_acc, dv_acc, qst, kst, ln, l1, l2, lt1, lt2 = refs
    nq = 2 * nblocks
    nk = 2 * nkv

    n = 0
    for ref, size in zip(packs, q_sizes):
        for c in range(size):
            base = c * PIECE
            meta = ref[base + CHUNK : base + PIECE, :].astype(F32)
            row = meta[0:1] + meta[1:2] + meta[2:3]
            rowc[n] = jnp.broadcast_to(row, (8, 1024))
            qst[n] = jnp.max(meta[3:4, 0:128]).astype(jnp.int32)
            for h in range(REPEAT):
                rows = slice(h * 128, h * 128 + 128)
                qc[n, rows, :] = ref[base : base + CHUNK, h * 128 : h * 128 + 128]
                doc[n, rows, :] = ref[base : base + CHUNK, 512 + h * 128 : 640 + h * 128]
            n += 1
    for j in range(nkv):
        meta = kvs[j][ROWS : ROWS + 16, :].astype(F32)
        for c in range(2):
            rows = slice(c * 128, c * 128 + 128)
            kst[2 * j + c] = jnp.max(meta[c : c + 1, 0:128]).astype(jnp.int32)
            ks[2 * j + c] = kvs[j][rows, 0:128]
            vs[2 * j + c] = kvs[j][rows, 128:256]
            kts[2 * j + c] = kvs[j][rows, 0:128].T
    at = 0
    for b in range(nblocks):
        for c in range(2):
            for h in range(REPEAT):
                lanes = slice(h * 128, h * 128 + 128)
                if has_dq[b]:
                    dq_acc[2 * b + c, :, lanes] = dq_ins[at][lanes, c * 128 : c * 128 + 128]
                else:
                    dq_acc[2 * b + c, :, lanes] = jnp.zeros((128, 128), F32)
        at += has_dq[b]
    at = 0
    for j in range(nkv):
        for c in range(2):
            rows = slice(c * 128, c * 128 + 128)
            if has_dkv[j]:
                dk_acc[2 * j + c] = dkv_ins[at][rows, 0:128]
                dv_acc[2 * j + c] = dkv_ins[at][rows, 128:256]
            else:
                dk_acc[2 * j + c] = jnp.zeros((128, 128), F32)
                dv_acc[2 * j + c] = jnp.zeros((128, 128), F32)
        at += has_dkv[j]

    def per_query(n, tiles):
        def per_key(c, state):
            tiles, odd = state
            gap = (qst[n] - kst[c]) * CHUNK
            seen = gap >= 0

            @pl.when(seen & (odd == 0))
            def _():
                ln[tiles] = n
                l1[tiles] = c
                l2[tiles] = c
                lt1[tiles] = gap
                lt2[tiles] = -100000

            @pl.when(seen & (odd == 1))
            def _():
                l2[tiles] = c
                lt2[tiles] = gap

            step = seen.astype(jnp.int32)
            return tiles + (step & odd), odd ^ step

        tiles, odd = lax.fori_loop(0, nk, per_key, (tiles, jnp.int32(0)), unroll=True)
        return tiles + odd

    tiles = lax.fori_loop(0, nq, per_query, jnp.int32(0))
    for extra in range(UNROLL - 1):
        ln[tiles + extra] = 0
        l1[tiles + extra] = 0
        l2[tiles + extra] = 0
        lt1[tiles + extra] = -100000
        lt2[tiles + extra] = -100000

    line = lax.broadcasted_iota(jnp.int32, (128, 256), 0)
    lane = lax.broadcasted_iota(jnp.int32, (128, 256), 1) & 127
    diff = line - lane

    def load(t):
        n, c1, c2 = ln[t], l1[t], l2[t]
        k = jnp.concatenate([ks[c1], ks[c2]], axis=0)
        v = jnp.concatenate([vs[c1], vs[c2]], axis=0)
        return n, c1, c2, k, v, (lt1[t], lt2[t])

    def opening(unit):
        (n, _, _, k, v, _), half = unit
        lanes = slice(half * 256, half * 256 + 256)
        return dot(k, qc[n, lanes, :], NT), dot(v, doc[n, lanes, :], NT)

    def middle(unit, found):
        (n, _, _, _, _, mask), half = unit
        scores = found[0] * (SCALE * LOG2E) - rowc[n, 0:1, half * 256 : half * 256 + 256]
        probs = jnp.exp2(scores)
        probs = jnp.concatenate(
            [
                jnp.where(diff <= mask[0], probs[0:128], 0.0),
                jnp.where(diff <= mask[1], probs[128:256], 0.0),
            ],
            axis=0,
        )
        dprob = found[1] * SCALE - rowc[n, 0:1, 512 + half * 256 : 768 + half * 256]
        return probs.astype(BF), (probs * dprob).astype(BF)

    def closing(unit, made, sums):
        (n, c1, c2, _, _, _), half = unit
        lanes = slice(half * 256, half * 256 + 256)
        probs, dscore = made
        dv = dot(probs, doc[n, lanes, :], NN)
        dk = dot(dscore, qc[n, lanes, :], NN)
        kt = jnp.concatenate([kts[c1], kts[c2]], axis=1)
        dq_acc[n, :, lanes] += dot(kt, dscore, NN)
        if half == 0:
            return dk, dv
        dk = dk + sums[0]
        dv = dv + sums[1]
        dk_acc[c1] += dk[0:128]
        dv_acc[c1] += dv[0:128]
        dk_acc[c2] += dk[128:256]
        dv_acc[c2] += dv[128:256]
        return None

    def turn(i, carry):
        units = []
        for step in range(UNROLL):
            info = load(i * UNROLL + step)
            units += [(info, 0), (info, 1)]
        found = {0: opening(units[0])}
        sums = None
        made = {}
        for at in range(len(units) + 1):
            if at + 1 < len(units):
                found[at + 1] = opening(units[at + 1])
            if at < len(units):
                made[at] = middle(units[at], found.pop(at))
            if at >= 1:
                sums = closing(units[at - 1], made.pop(at - 1), sums)
        return carry

    lax.fori_loop(0, (tiles + UNROLL - 1) // UNROLL, turn, 0)

    for b in range(nblocks):
        for c in range(2):
            for h in range(REPEAT):
                rows = slice(h * 128, h * 128 + 128)
                dq_outs[b][rows, c * 128 : c * 128 + 128] = dq_acc[2 * b + c, :, rows].astype(
                    dq_outs[b].dtype
                )
    for ref, held in zip(dkv_outs, layout):
        for at, c in enumerate(held):
            rows = slice(at * 128, at * 128 + 128)
            ref[rows, 0:128] = dk_acc[c].astype(ref.dtype)
            ref[rows, 128:256] = dv_acc[c].astype(ref.dtype)


def attend(packs, kvs, dq_ins, dkv_ins, dq_types, dkv_types, layout=None):
    layout = layout or tuple((2 * j, 2 * j + 1) for j in range(len(kvs)))
    sizes = tuple(p.shape[0] // PIECE for p in packs)
    nq = sum(sizes)
    nk = 2 * len(kvs)
    has_dq = tuple(int(g is not None) for g in dq_ins)
    has_dkv = tuple(int(g is not None) for g in dkv_ins)
    operands = list(packs) + list(kvs) + [g for g in list(dq_ins) + list(dkv_ins) if g is not None]
    most = nq * ((nk + 1) // 2) + UNROLL
    return pl.pallas_call(
        functools.partial(attn_kernel, sizes, len(kvs), has_dq, has_dkv, layout),
        out_shape=tuple(whole((512, ROWS), t) for t in dq_types)
        + tuple(whole((128 * len(held), 256), t) for held, t in zip(layout, dkv_types)),
        in_specs=[VM] * len(operands),
        out_specs=(VM,) * (len(dq_types) + len(dkv_types)),
        scratch_shapes=[
            pltpu.VMEM((nq, 512, 128), BF),
            pltpu.VMEM((nq, 512, 128), BF),
            pltpu.VMEM((nk, 128, 128), BF),
            pltpu.VMEM((nk, 128, 128), BF),
            pltpu.VMEM((nk, 128, 128), BF),
            pltpu.VMEM((nq, 8, 1024), F32),
            pltpu.VMEM((nq, 128, 512), F32),
            pltpu.VMEM((nk, 128, 128), F32),
            pltpu.VMEM((nk, 128, 128), F32),
            pltpu.SMEM((nq,), jnp.int32),
            pltpu.SMEM((nk,), jnp.int32),
        ]
        + [pltpu.SMEM((most,), jnp.int32)] * 5,
        compiler_params=pltpu.CompilerParams(vmem_limit_bytes=28 * MIB),
        cost_estimate=pl.CostEstimate(
            flops=nq * nk * 85_000_000, bytes_accessed=4_000_000, transcendentals=nq * nk * 65536
        ),
    )(*operands)


def rotate(value, cosine, sine):
    first = value[0:HALF]
    second = value[HALF : 2 * HALF]
    return jnp.concatenate(
        [first * cosine + second * sine, second * cosine - first * sine], axis=0
    )


def project(x, weights, i, other):
    tp = lax.axis_index("tp")
    core = tp % NC
    block = NC * lax.rem(tp // NC + i, NX) + (1 - core if other else core)
    rows = pl.ds(pl.multiple_of(block * 512, 512), 512)
    w_query, w_key, w_value = (ref[rows, :] for ref in weights)
    return (
        dot(w_query, x[0:512, :], NN)
        + dot(w_key, x[512:640, :], NN)
        + dot(w_value, x[640:768, :], NN)
    )


def send_kernel(*refs):
    dqs = refs[0:4]
    dkvs = refs[4:9]
    cos_ref, sin_ref, wq_ref, wk_ref, wv_ref, x_out, out_ref = refs[9:]
    cosine = cos_ref[...]
    sine = sin_ref[...]
    for head in range(REPEAT):
        rows = slice(head * 128, head * 128 + 128)
        total = dqs[0][rows, :]
        for ref in dqs[1:]:
            total = total + ref[rows, :].astype(F32)
        x_out[rows, :] = rotate(total, cosine, sine).astype(BF)
    total = dkvs[0][...]
    for ref in dkvs[1:]:
        total = total + ref[...].astype(F32)
    x_out[512:640, :] = rotate(total[:, 0:128].T, cosine, sine).astype(BF)
    x_out[640:768, :] = total[:, 128:256].T.astype(BF)
    for i in range(NX):
        out_ref[i] = project(x_out, (wq_ref, wk_ref, wv_ref), i, True).astype(BF)


def keep_kernel(x_ref, wq_ref, wk_ref, wv_ref, out_ref):
    for i in range(NX):
        out_ref[i] = project(x_ref, (wq_ref, wk_ref, wv_ref), i, False)


def merge_kernel(up1, down1, up2, down2, from_up, from_down, *outs):
    outs[0][...] = (up1[...] + from_up[0:256, :].astype(F32)).astype(BF)
    outs[1][...] = (down1[...] + from_down[0:256, :].astype(F32)).astype(BF)
    outs[2][0:128, :] = (up2[0:128, :] + from_up[256:384, :].astype(F32)).astype(BF)
    outs[2][128:256, :] = up2[128:256, :].astype(BF)
    outs[3][0:128, :] = down2[0:128, :].astype(BF)
    outs[3][128:256, :] = (down2[128:256, :] + from_down[256:384, :].astype(F32)).astype(BF)


def final_kernel(own_ref, a_ref, b_ref, c_ref, out_ref):
    total = own_ref[...] + a_ref[...].astype(F32) + b_ref[...].astype(F32) + c_ref[...].astype(F32)
    out_ref[...] = total.T.astype(BF)


def whole(shape, dtype):
    return jax.ShapeDtypeStruct(shape, dtype)


VM = pl.BlockSpec(memory_space=pltpu.VMEM)
HB = pl.BlockSpec(memory_space=pltpu.HBM)


def layer(
    query_act, key_act, value_act, attn_out, out_grad, log_sum, positions, w_query, w_key, w_value
):
    pack, kv = pl.pallas_call(
        prep_kernel,
        out_shape=(whole((2 * PIECE, 1024), BF), whole((ROWS + 16, 256), BF)),
        in_specs=[HB] * 7,
        out_specs=(VM, VM),
        scratch_shapes=[
            pltpu.SMEM((ROWS,), jnp.int32),
            pltpu.VMEM((ROWS, 512), BF),
            pltpu.VMEM((REPEAT, ROWS), F32),
            pltpu.SemaphoreType.DMA((9,)),
        ],
        compiler_params=pltpu.CompilerParams(vmem_limit_bytes=PREP_LIMIT),
    )(positions, query_act, out_grad, attn_out, log_sum, key_act, value_act)

    left = move_y(pack, 1)
    right = move_y(pack, -1)
    up1 = move_z(kv, 1)
    down1 = move_z(kv, -1)
    up2 = move_z(up1, 1)
    down2 = move_z(down1, -1)
    up3 = move_z(up2, 1)
    down3 = move_z(down2, -1)
    up4 = move_z(up3, 1)
    far0 = move_y(left[0:PIECE], 1)
    far1 = move_y(right[PIECE : 2 * PIECE], -1)

    near = [kv, up1, down1, up2, down2]
    own = attend([pack], near, [None], [None] * 5, [F32], [F32] * 5)
    side = attend([left, right], near, [None] * 2, list(own[1:]), [F32] * 2, [F32] * 5)
    outer = attend(
        [pack, left, right, far0, far1],
        [up3, down3, up4],
        [own[0], side[0], side[1], None],
        [None] * 3,
        [F32, BF, BF, F32],
        [BF] * 2,
        ((0, 1, 4), (2, 3, 5)),
    )
    back_up = move_z(outer[4], -2)
    back_down = move_z(outer[5], 2)
    last = attend([far0, far1], near, [outer[3]], list(side[2:]), [BF], [F32] * 5)
    dqs = [outer[0], move_y(outer[1], -1), move_y(outer[2], 1), move_y(last[0], 2)]
    merged = pl.pallas_call(
        merge_kernel,
        out_shape=(whole((ROWS, 256), BF),) * 4,
        in_specs=[VM] * 6,
        out_specs=(VM,) * 4,
        compiler_params=pltpu.CompilerParams(vmem_limit_bytes=8 * MIB),
    )(*last[2:6], back_up, back_down)
    dkvs = [last[1]] + [move_z(part, steps) for part, steps in zip(merged, (-1, 1, -2, 2))]

    freqs = 500000.0 ** (-(jnp.arange(HALF, dtype=F32) * 2.0 / HEAD_DIM))
    angles = freqs[:, None] * positions.astype(F32)[None, :]
    cosine = jnp.cos(angles)
    sine = jnp.sin(angles)

    grads, to_send = pl.pallas_call(
        send_kernel,
        out_shape=(whole((768, ROWS), BF), whole((NX, 512, ROWS), BF)),
        in_specs=[VM] * 14,
        out_specs=(VM, VM),
        compiler_params=pltpu.CompilerParams(vmem_limit_bytes=20 * MIB),
    )(*dqs, *dkvs, cosine, sine, w_query, w_key, w_value)
    got = swap_core(to_send)
    kept = pl.pallas_call(
        keep_kernel,
        out_shape=whole((NX, 512, ROWS), F32),
        in_specs=[VM] * 4,
        out_specs=VM,
        compiler_params=pltpu.CompilerParams(vmem_limit_bytes=20 * MIB),
        cost_estimate=pl.CostEstimate(
            flops=800_000_000, bytes_accessed=4_000_000, transcendentals=0
        ),
    )(grads, w_query, w_key, w_value)
    parts = [kept[i] + got[i].astype(F32) for i in range(4)]
    came = [move_x(parts[i].astype(BF), i) for i in (1, 3, 2)]
    return pl.pallas_call(
        final_kernel,
        out_shape=whole((ROWS, 512), BF),
        in_specs=[VM] * 4,
        out_specs=VM,
        compiler_params=pltpu.CompilerParams(vmem_limit_bytes=8 * MIB),
    )(parts[0], *came)


def solution(mesh):
    return jax.shard_map(
        layer,
        mesh=mesh,
        in_specs=(
            P("seq", "tp"),
            P("seq", "tp"),
            P("seq", "tp"),
            P("seq", "tp"),
            P("seq", "tp"),
            P("tp", "seq"),
            P("seq"),
            P(None, "tp"),
            P(None, "tp"),
            P(None, "tp"),
        ),
        out_specs=P("seq", "tp"),
        check_vma=False,
    )
```

profile of v0, /device:TPU:8, one launch (start us, length us, event | category | flops | bytes accessed | tf_op | source)
XLA Modules:
  0.0 104.0 jit_solution(11186552002937777846)
XLA Ops:
  0.0 3.1 %shard_map.100 = (bf16[288,1024]{1,0:T(8,128)(2,1)}, bf16[272,256]{1,0:T(8,128)(2,1)}) custom-call(s32[256]{0:T(256)} %pos_hbm.1, bf16[256,512]{1,0:T(8,128)(2,1)} %q_hbm.1, bf16[256,512]{1,0:T(8,128)(2,1)} %do_hbm.1, bf16[256,512]{1,0:T(8,128)(2,1)} %o_hbm.1, f32[4,256]{1,0:T(4,128)} %lse_hbm.1, bf16[256,128]{1,0:T(8,128)(2,1)} %k_hbm.1, bf16[256,128]{1,0:T(8,128)(2,1)} %v_hbm.1), custom_call_target="tpu_custom_call" | custom-call | tf_op jit(solution)/shard_map/pallas_call | solution.py:400
  3.1 1.7 %collective-permute-start = (bf16[288,1024]{1,0:T(8,128)(2,1)}, bf16[288,1024]{1,0:T(8,128)(2,1)S(1)}, u32[]{:S(2)}, u32[]{:S(2)}) collective-permute-start(bf16[288,1024]{1,0:T(8,128)(2,1)} %get-tuple-element.38.refs_0_), channel_id=1, source_target_pairs={{0,8},{8,16},{16,24},{24,0},{32,40},{40,48},{48,56},{56,32},{64,72... | collective-permute-start | bytes 1769480 | tf_op jit(solution)/shard_map/ppermute | solution.py:50
  4.7 0.7 collective-permute-start.1
  5.4 1.7 %collective-permute-start.4 = (bf16[272,256]{1,0:T(8,128)(2,1)}, bf16[272,256]{1,0:T(8,128)(2,1)S(1)}, u32[]{:S(2)}, u32[]{:S(2)}) collective-permute-start(bf16[272,256]{1,0:T(8,128)(2,1)} %get-tuple-element.39.refs_1_.refs_2_), channel_id=1, source_target_pairs={{0,32},{8,40},{16,48},{24,56},{32,64},{40,72},{48,80},{56,88},{64,... | collective-permute-start | bytes 417800 | tf_op jit(solution)/shard_map/ppermute | solution.py:43
  7.1 3.9 %collective-permute-start.7 = (bf16[272,256]{1,0:T(8,128)(2,1)}, bf16[272,256]{1,0:T(8,128)(2,1)S(1)}, u32[]{:S(2)}, u32[]{:S(2)}) collective-permute-start(bf16[272,256]{1,0:T(8,128)(2,1)} %get-tuple-element.39.refs_1_.refs_2_), channel_id=1, source_target_pairs={{0,224},{8,232},{16,240},{24,248},{32,0},{40,8},{48,16},{56,24},{6... | collective-permute-start | bytes 417800 | tf_op jit(solution)/shard_map/ppermute | solution.py:43
  11.0 3.3 %collective-permute-done.4.refs_2_.refs_3_ = bf16[272,256]{1,0:T(8,128)(2,1)S(1)} collective-permute-done((bf16[272,256]{1,0:T(8,128)(2,1)}, bf16[272,256]{1,0:T(8,128)(2,1)S(1)}, u32[]{:S(2)}, u32[]{:S(2)}) %collective-permute-start.4) | collective-permute-done | bytes 139296 | tf_op jit(solution)/shard_map/ppermute | solution.py:43
  14.4 3.2 %collective-permute-start.8 = (bf16[272,256]{1,0:T(8,128)(2,1)S(1)}, bf16[272,256]{1,0:T(8,128)(2,1)S(1)}, u32[]{:S(2)}, u32[]{:S(2)}) collective-permute-start(bf16[272,256]{1,0:T(8,128)(2,1)S(1)} %collective-permute-done.7.refs_3_.refs_4_), channel_id=1, source_target_pairs={{0,224},{8,232},{16,240},{24,248},{32,0},{40,8},{48,16},{56,24},{6... | collective-permute-start | bytes 417800 | tf_op jit(solution)/shard_map/ppermute | solution.py:43
  17.6 3.0 %collective-permute-done.5.refs_4_.refs_5_ = bf16[272,256]{1,0:T(8,128)(2,1)S(1)} collective-permute-done((bf16[272,256]{1,0:T(8,128)(2,1)S(1)}, bf16[272,256]{1,0:T(8,128)(2,1)S(1)}, u32[]{:S(2)}, u32[]{:S(2)}) %collective-permute-start.5) | collective-permute-done | bytes 139296 | tf_op jit(solution)/shard_map/ppermute | solution.py:43
  20.6 3.2 %collective-permute-start.9 = (bf16[272,256]{1,0:T(8,128)(2,1)S(1)}, bf16[272,256]{1,0:T(8,128)(2,1)S(1)}, u32[]{:S(2)}, u32[]{:S(2)}) collective-permute-start(bf16[272,256]{1,0:T(8,128)(2,1)S(1)} %collective-permute-done.8.refs_5_.refs_6_), channel_id=1, source_target_pairs={{0,224},{8,232},{16,240},{24,248},{32,0},{40,8},{48,16},{56,24},{6... | collective-permute-start | bytes 417800 | tf_op jit(solution)/shard_map/ppermute | solution.py:43
  23.9 1.1 %copy-done.3 = bf16[288,1024]{1,0:T(8,128)(2,1)S(1)} copy-done((bf16[288,1024]{1,0:T(8,128)(2,1)S(1)}, bf16[288,1024]{1,0:T(8,128)(2,1)}, u32[]{:S(2)}) %copy-start.3) | copy-done | bytes 589848
  24.9 0.9 copy-done.5
  25.8 3.2 %shard_map.101 = (f32[512,256]{1,0:T(8,128)S(1)}, f32[256,256]{1,0:T(8,128)S(1)}, f32[256,256]{1,0:T(8,128)S(1)}, f32[256,256]{1,0:T(8,128)S(1)}, f32[256,256]{1,0:T(8,128)S(1)}, /*index=5*/f32[256,256]{1,0:T(8,128)S(1)}) custom-call(bf16[288,1024]{1,0:T(8,128)(2,1)S(1)} %copy-done.3, bf16[272,256]{1,0:T(8,128)(2,1)S(1)} %copy-done.5, ...), custom_call_target="tpu_custom_call" | custom-call | flops 1700000000 | bytes 4000000 | tf_op jit(solution)/shard_map/pallas_call | solution.py:301
  29.1 0.1 collective-permute-start.10
  29.2 2.5 %collective-permute-start.2 = (bf16[144,1024]{1,0:T(8,128)(2,1)S(1)}, bf16[144,1024]{1,0:T(8,128)(2,1)S(1)}, u32[]{:S(2)}, u32[]{:S(2)}) collective-permute-start(bf16[144,1024]{1,0:T(8,128)(2,1)S(1)} %slice.40), channel_id=1, source_target_pairs={{0,8},{8,16},{16,24},{24,0},{32,40},{40,48},{48,56},{56,32},{64,72... | collective-permute-start | bytes 884744 | tf_op jit(solution)/shard_map/ppermute | solution.py:50
  31.7 0.1 collective-permute-start.3
  31.8 7.0 %shard_map.102 = (f32[512,256]{1,0:T(8,128)S(1)}, f32[512,256]{1,0:T(8,128)S(1)}, f32[256,256]{1,0:T(8,128)S(1)}, f32[256,256]{1,0:T(8,128)S(1)}, f32[256,256]{1...) custom-call(bf16[288,1024]{1,0:T(8,128)(2,1)S(1)} %collective-permute-done.refs_0_.refs_1_, ...), custom_call_target="tpu_custom_call" | custom-call | flops 3400000000 | bytes 4000000 | tf_op jit(solution)/shard_map/pallas_call | solution.py:301
  38.9 7.1 %shard_map.103 = (f32[512,256]{1,0:T(8,128)S(1)}, bf16[512,256]{1,0:T(8,128)(2,1)S(1)}, bf16[512,256]{1,0:T(8,128)(2,1)S(1)}, f32[512,256]{1,0:T(8,128)S(1)}, bf...) custom-call(bf16[288,1024]{1,0:T(8,128)(2,1)S(1)} %copy-done.4, ...), custom_call_target="tpu_custom_call" | custom-call | flops 4080000000 | bytes 4000000 | tf_op jit(solution)/shard_map/pallas_call | solution.py:301
  45.9 0.0 copy-start.7
  46.0 0.0 copy-start
  46.0 3.2 %shard_map.104 = (bf16[512,256]{1,0:T(8,128)(2,1)S(1)}, f32[256,256]{1,0:T(8,128)S(1)}, f32[256,256]{1,0:T(8,128)S(1)}, f32[256,256]{1,0:T(8,128)S(1)}, f32[256,256]{1,0:T(8,128)S(1)}, /*index=5*/f32[256,256]{1,0:T(8,128)S(1)}) custom-call(bf16[144,1024]{1,0:T(8,128)(2,1)S(1)} %collective-permute-done.2.refs_3_.refs_0_, ...), custom_call_target="tpu_custom_call" | custom-call | flops 1700000000 | bytes 4000000 | tf_op jit(solution)/shard_map/pallas_call | solution.py:301
  49.2 0.0 copy-start.1
  49.2 2.4 %collective-permute-start.13 = (bf16[512,256]{1,0:T(8,128)(2,1)S(1)}, bf16[512,256]{1,0:T(8,128)(2,1)S(1)}, u32[]{:S(2)}, u32[]{:S(2)}) collective-permute-start(bf16[512,256]{1,0:T(8,128)(2,1)S(1)} %get-tuple-element.57), channel_id=1, source_target_pairs={{0,16},{8,24},{16,0},{24,8},{32,48},{40,56},{48,32},{56,40},{64,80... | collective-permute-start | bytes 786440 | tf_op jit(solution)/shard_map/ppermute | solution.py:50
  51.6 1.2 %collective-permute-start.11 = (bf16[512,256]{1,0:T(8,128)(2,1)S(1)}, bf16[512,256]{1,0:T(8,128)(2,1)S(1)}, u32[]{:S(2)}, u32[]{:S(2)}) collective-permute-start(bf16[512,256]{1,0:T(8,128)(2,1)S(1)} %get-tuple-element.49), channel_id=1, source_target_pairs={{0,24},{8,0},{16,8},{24,16},{32,56},{40,32},{48,40},{56,48},{64,88... | collective-permute-start | bytes 786440 | tf_op jit(solution)/shard_map/ppermute | solution.py:50
  52.8 2.3 %collective-permute-start.14 = (bf16[384,256]{1,0:T(8,128)(2,1)S(1)}, bf16[384,256]{1,0:T(8,128)(2,1)S(1)}, u32[]{:S(2)}, u32[]{:S(2)}) collective-permute-start(bf16[384,256]{1,0:T(8,128)(2,1)S(1)} %get-tuple-element.63), channel_id=1, source_target_pairs={{0,192},{8,200},{16,208},{24,216},{32,224},{40,232},{48,240},{56,2... | collective-permute-start | bytes 589832 | tf_op jit(solution)/shard_map/ppermute | solution.py:43
  55.1 0.7 collective-permute-start.15
  55.7 1.4 %collective-permute-start.12 = (bf16[512,256]{1,0:T(8,128)(2,1)S(1)}, bf16[512,256]{1,0:T(8,128)(2,1)S(1)}, u32[]{:S(2)}, u32[]{:S(2)}) collective-permute-start(bf16[512,256]{1,0:T(8,128)(2,1)S(1)} %get-tuple-element.50), channel_id=1, source_target_pairs={{0,8},{8,16},{16,24},{24,0},{32,40},{40,48},{48,56},{56,32},{64,72... | collective-permute-start | bytes 786440 | tf_op jit(solution)/shard_map/ppermute | solution.py:50
  57.1 3.1 %collective-permute-done.14.from_up = bf16[384,256]{1,0:T(8,128)(2,1)S(1)} collective-permute-done((bf16[384,256]{1,0:T(8,128)(2,1)S(1)}, bf16[384,256]{1,0:T(8,128)(2,1)S(1)}, u32[]{:S(2)}, u32[]{:S(2)}) %collective-permute-start.14) | collective-permute-done | bytes 196640 | tf_op jit(solution)/shard_map/ppermute | solution.py:43
  60.2 4.7 %collective-permute-done.15.from_down = bf16[384,256]{1,0:T(8,128)(2,1)S(1)} collective-permute-done((bf16[384,256]{1,0:T(8,128)(2,1)S(1)}, bf16[384,256]{1,0:T(8,128)(2,1)S(1)}, u32[]{:S(2)}, u32[]{:S(2)}) %collective-permute-start.15) | collective-permute-done | bytes 196640 | tf_op jit(solution)/shard_map/ppermute | solution.py:43
  64.9 0.1 shard_map.105
  65.0 3.7 %collective-permute-start.16 = (bf16[256,256]{1,0:T(8,128)(2,1)S(1)}, bf16[256,256]{1,0:T(8,128)(2,1)S(1)}, u32[]{:S(2)}, u32[]{:S(2)}) collective-permute-start(bf16[256,256]{1,0:T(8,128)(2,1)S(1)} %get-tuple-element.65), channel_id=1, source_target_pairs={{0,224},{8,232},{16,240},{24,248},{32,0},{40,8},{48,16},{56,24},{6... | collective-permute-start | bytes 393224 | tf_op jit(solution)/shard_map/ppermute | solution.py:43
  68.7 0.2 collective-permute-start.17
  68.9 4.8 %collective-permute-start.18 = (bf16[256,256]{1,0:T(8,128)(2,1)S(1)}, bf16[256,256]{1,0:T(8,128)(2,1)S(1)}, u32[]{:S(2)}, u32[]{:S(2)}) collective-permute-start(bf16[256,256]{1,0:T(8,128)(2,1)S(1)} %get-tuple-element.67), channel_id=1, source_target_pairs={{0,192},{8,200},{16,208},{24,216},{32,224},{40,232},{48,240},{56,2... | collective-permute-start | bytes 393224 | tf_op jit(solution)/shard_map/ppermute | solution.py:43
  73.7 0.3 multiply_sine_fusion
  74.1 1.8 %collective-permute-done.17.refs_6_ = bf16[256,256]{1,0:T(8,128)(2,1)S(1)} collective-permute-done((bf16[256,256]{1,0:T(8,128)(2,1)S(1)}, bf16[256,256]{1,0:T(8,128)(2,1)S(1)}, u32[]{:S(2)}, u32[]{:S(2)}) %collective-permute-start.17) | collective-permute-done | bytes 131104 | tf_op jit(solution)/shard_map/ppermute | solution.py:43
  75.8 0.9 collective-permute-done.18.refs_7_
  76.7 5.5 %collective-permute-done.19.refs_8_ = bf16[256,256]{1,0:T(8,128)(2,1)S(1)} collective-permute-done((bf16[256,256]{1,0:T(8,128)(2,1)S(1)}, bf16[256,256]{1,0:T(8,128)(2,1)S(1)}, u32[]{:S(2)}, u32[]{:S(2)}) %collective-permute-start.19) | collective-permute-done | bytes 131104 | tf_op jit(solution)/shard_map/ppermute | solution.py:43
  82.2 1.4 %shard_map.106 = (bf16[768,256]{1,0:T(8,128)(2,1)S(1)}, bf16[4,512,256]{2,1,0:T(8,128)(2,1)S(1)}) custom-call(f32[512,256]{1,0:T(8,128)S(1)} %get-tuple-element.48.refs_0_, bf16[512,256]{1,0:T(8,128)(2,1)S(1)} %collective-permute-done.11.refs_1_, bf16[512,256]{1,0:T(8,128)(2,1)S(1)} %collective-permute-done.12.refs_2_, ...), custom_call_target="tpu_custom_call" | custom-call | tf_op jit(solution)/shard_map/pallas_call | solution.py:456
  83.6 0.3 collective-permute-start.20
  84.0 1.2 %shard_map.107 = f32[4,512,256]{2,1,0:T(8,128)S(1)} custom-call(bf16[768,256]{1,0:T(8,128)(2,1)S(1)} %get-tuple-element.69.x_ref, bf16[4096,512]{1,0:T(8,128)(2,1)S(1)} %copy-done, bf16[4096,128]{1,0:T(8,128)(2,1)S(1)} %copy-done.1, bf16[4096,128]{1,0:T(8,128)(2,1)S(1)} %copy-done.2), custom_call_target="tpu_custom_call" | custom-call | flops 800000000 | bytes 4000000 | tf_op jit(solution)/shard_map/pallas_call | solution.py:464
  85.2 1.4 %collective-permute-done.20 = bf16[4,512,256]{2,1,0:T(8,128)(2,1)S(1)} collective-permute-done((bf16[4,512,256]{2,1,0:T(8,128)(2,1)S(1)}, bf16[4,512,256]{2,1,0:T(8,128)(2,1)S(1)}, u32[]{:S(2)}, u32[]{:S(2)}) %collective-permute-start.20) | collective-permute-done | bytes 1048608 | tf_op jit(solution)/shard_map/ppermute | solution.py:62
  86.6 0.2 fusion.6
  86.8 1.6 %collective-permute-start.21 = (bf16[512,256]{1,0:T(8,128)(2,1)S(1)}, bf16[512,256]{1,0:T(8,128)(2,1)S(1)}, u32[]{:S(2)}, u32[]{:S(2)}) collective-permute-start(bf16[512,256]{1,0:T(8,128)(2,1)S(1)} %get-tuple-element.73), channel_id=1, source_target_pairs={{0,2},{1,3},{2,4},{3,5},{4,6},{5,7},{6,0},{7,1},{8,10},{9,11},{10,... | collective-permute-start | bytes 786440 | tf_op jit(solution)/shard_map/ppermute | solution.py:57
  88.4 1.7 %collective-permute-start.22 = (bf16[512,256]{1,0:T(8,128)(2,1)S(1)}, bf16[512,256]{1,0:T(8,128)(2,1)S(1)}, u32[]{:S(2)}, u32[]{:S(2)}) collective-permute-start(bf16[512,256]{1,0:T(8,128)(2,1)S(1)} %get-tuple-element.72), channel_id=1, source_target_pairs={{0,6},{1,7},{2,0},{3,1},{4,2},{5,3},{6,4},{7,5},{8,14},{9,15},{10,... | collective-permute-start | bytes 786440 | tf_op jit(solution)/shard_map/ppermute | solution.py:57
  90.2 1.8 %collective-permute-start.23 = (bf16[512,256]{1,0:T(8,128)(2,1)S(1)}, bf16[512,256]{1,0:T(8,128)(2,1)S(1)}, u32[]{:S(2)}, u32[]{:S(2)}) collective-permute-start(bf16[512,256]{1,0:T(8,128)(2,1)S(1)} %get-tuple-element.71), channel_id=1, source_target_pairs={{0,4},{1,5},{2,6},{3,7},{4,0},{5,1},{6,2},{7,3},{8,12},{9,13},{10,... | collective-permute-start | bytes 786440 | tf_op jit(solution)/shard_map/ppermute | solution.py:57
  91.9 4.5 %collective-permute-done.21.a_ref = bf16[512,256]{1,0:T(8,128)(2,1)S(1)} collective-permute-done((bf16[512,256]{1,0:T(8,128)(2,1)S(1)}, bf16[512,256]{1,0:T(8,128)(2,1)S(1)}, u32[]{:S(2)}, u32[]{:S(2)}) %collective-permute-start.21) | collective-permute-done | bytes 262176 | tf_op jit(solution)/shard_map/ppermute | solution.py:57
  96.5 4.9 %collective-permute-done.22.b_ref = bf16[512,256]{1,0:T(8,128)(2,1)S(1)} collective-permute-done((bf16[512,256]{1,0:T(8,128)(2,1)S(1)}, bf16[512,256]{1,0:T(8,128)(2,1)S(1)}, u32[]{:S(2)}, u32[]{:S(2)}) %collective-permute-start.22) | collective-permute-done | bytes 262176 | tf_op jit(solution)/shard_map/ppermute | solution.py:57
  101.4 1.7 %collective-permute-done.23.c_ref = bf16[512,256]{1,0:T(8,128)(2,1)S(1)} collective-permute-done((bf16[512,256]{1,0:T(8,128)(2,1)S(1)}, bf16[512,256]{1,0:T(8,128)(2,1)S(1)}, u32[]{:S(2)}, u32[]{:S(2)}) %collective-permute-start.23) | collective-permute-done | bytes 262176 | tf_op jit(solution)/shard_map/ppermute | solution.py:57
  103.1 0.9 shard_map.108
  (31 shorter events, 0.1 us)
Async XLA Ops:
  3.1 26.1 %collective-permute-start = (bf16[288,1024]{1,0:T(8,128)(2,1)}, bf16[288,1024]{1,0:T(8,128)(2,1)S(1)}, u32[]{:S(2)}, u32[]{:S(2)}) collective-permute-start(bf16[288,1024]{1,0:T(8,128)(2,1)} %get-tuple-element.38.refs_0_), channel_id=1, source_target_pairs={{0,8},{8,16},{16,24},{24,0},{32,40},{40,48},{48,56},{56,32},{64,72... | collective-permute-start | bytes 1769480 | tf_op jit(solution)/shard_map/ppermute | solution.py:50
  4.7 26.9 %collective-permute-start.1 = (bf16[288,1024]{1,0:T(8,128)(2,1)}, bf16[288,1024]{1,0:T(8,128)(2,1)S(1)}, u32[]{:S(2)}, u32[]{:S(2)}) collective-permute-start(bf16[288,1024]{1,0:T(8,128)(2,1)} %get-tuple-element.38.refs_0_), channel_id=1, source_target_pairs={{0,24},{8,0},{16,8},{24,16},{32,56},{40,32},{48,40},{56,48},{64,88... | collective-permute-start | bytes 1769480 | tf_op jit(solution)/shard_map/ppermute | solution.py:50
  5.4 9.0 %collective-permute-start.4 = (bf16[272,256]{1,0:T(8,128)(2,1)}, bf16[272,256]{1,0:T(8,128)(2,1)S(1)}, u32[]{:S(2)}, u32[]{:S(2)}) collective-permute-start(bf16[272,256]{1,0:T(8,128)(2,1)} %get-tuple-element.39.refs_1_.refs_2_), channel_id=1, source_target_pairs={{0,32},{8,40},{16,48},{24,56},{32,64},{40,72},{48,80},{56,88},{64,... | collective-permute-start | bytes 417800 | tf_op jit(solution)/shard_map/ppermute | solution.py:43
  7.1 7.3 %collective-permute-start.7 = (bf16[272,256]{1,0:T(8,128)(2,1)}, bf16[272,256]{1,0:T(8,128)(2,1)S(1)}, u32[]{:S(2)}, u32[]{:S(2)}) collective-permute-start(bf16[272,256]{1,0:T(8,128)(2,1)} %get-tuple-element.39.refs_1_.refs_2_), channel_id=1, source_target_pairs={{0,224},{8,232},{16,240},{24,248},{32,0},{40,8},{48,16},{56,24},{6... | collective-permute-start | bytes 417800 | tf_op jit(solution)/shard_map/ppermute | solution.py:43
  14.3 6.3 %collective-permute-start.5 = (bf16[272,256]{1,0:T(8,128)(2,1)S(1)}, bf16[272,256]{1,0:T(8,128)(2,1)S(1)}, u32[]{:S(2)}, u32[]{:S(2)}) collective-permute-start(bf16[272,256]{1,0:T(8,128)(2,1)S(1)} %collective-permute-done.4.refs_2_.refs_3_), channel_id=1, source_target_pairs={{0,32},{8,40},{16,48},{24,56},{32,64},{40,72},{48,80},{56,88},{64,... | collective-permute-start | bytes 417800 | tf_op jit(solution)/shard_map/ppermute | solution.py:43
  14.4 6.3 %collective-permute-start.8 = (bf16[272,256]{1,0:T(8,128)(2,1)S(1)}, bf16[272,256]{1,0:T(8,128)(2,1)S(1)}, u32[]{:S(2)}, u32[]{:S(2)}) collective-permute-start(bf16[272,256]{1,0:T(8,128)(2,1)S(1)} %collective-permute-done.7.refs_3_.refs_4_), channel_id=1, source_target_pairs={{0,224},{8,232},{16,240},{24,248},{32,0},{40,8},{48,16},{56,24},{6... | collective-permute-start | bytes 417800 | tf_op jit(solution)/shard_map/ppermute | solution.py:43
  20.6 8.4 %collective-permute-start.6 = (bf16[272,256]{1,0:T(8,128)(2,1)S(1)}, bf16[272,256]{1,0:T(8,128)(2,1)S(1)}, u32[]{:S(2)}, u32[]{:S(2)}) collective-permute-start(bf16[272,256]{1,0:T(8,128)(2,1)S(1)} %collective-permute-done.5.refs_4_.refs_5_), channel_id=1, source_target_pairs={{0,32},{8,40},{16,48},{24,56},{32,64},{40,72},{48,80},{56,88},{64,... | collective-permute-start | bytes 417800 | tf_op jit(solution)/shard_map/ppermute | solution.py:43
  20.6 18.2 %collective-permute-start.9 = (bf16[272,256]{1,0:T(8,128)(2,1)S(1)}, bf16[272,256]{1,0:T(8,128)(2,1)S(1)}, u32[]{:S(2)}, u32[]{:S(2)}) collective-permute-start(bf16[272,256]{1,0:T(8,128)(2,1)S(1)} %collective-permute-done.8.refs_5_.refs_6_), channel_id=1, source_target_pairs={{0,224},{8,232},{16,240},{24,248},{32,0},{40,8},{48,16},{56,24},{6... | collective-permute-start | bytes 417800 | tf_op jit(solution)/shard_map/ppermute | solution.py:43
  23.9 1.1 %copy-start.3 = (bf16[288,1024]{1,0:T(8,128)(2,1)S(1)}, bf16[288,1024]{1,0:T(8,128)(2,1)}, u32[]{:S(2)}) copy-start(bf16[288,1024]{1,0:T(8,128)(2,1)} %get-tuple-element.38.refs_0_) | copy-start | bytes 1769476
  24.9 0.9 copy-start.5
  25.8 6.0 %copy-start.6 = (bf16[272,256]{1,0:T(8,128)(2,1)S(1)}, bf16[272,256]{1,0:T(8,128)(2,1)}, u32[]{:S(2)}) copy-start(bf16[272,256]{1,0:T(8,128)(2,1)} %get-tuple-element.39.refs_1_.refs_2_) | copy-start | bytes 417796
  29.1 9.8 %collective-permute-start.10 = (bf16[272,256]{1,0:T(8,128)(2,1)S(1)}, bf16[272,256]{1,0:T(8,128)(2,1)S(1)}, u32[]{:S(2)}, u32[]{:S(2)}) collective-permute-start(bf16[272,256]{1,0:T(8,128)(2,1)S(1)} %collective-permute-done.6.refs_5_), channel_id=1, source_target_pairs={{0,32},{8,40},{16,48},{24,56},{32,64},{40,72},{48,80},{56,88},{64,... | collective-permute-start | bytes 417800 | tf_op jit(solution)/shard_map/ppermute | solution.py:43
  29.2 9.6 %collective-permute-start.2 = (bf16[144,1024]{1,0:T(8,128)(2,1)S(1)}, bf16[144,1024]{1,0:T(8,128)(2,1)S(1)}, u32[]{:S(2)}, u32[]{:S(2)}) collective-permute-start(bf16[144,1024]{1,0:T(8,128)(2,1)S(1)} %slice.40), channel_id=1, source_target_pairs={{0,8},{8,16},{16,24},{24,0},{32,40},{40,48},{48,56},{56,32},{64,72... | collective-permute-start | bytes 884744 | tf_op jit(solution)/shard_map/ppermute | solution.py:50
  31.7 7.1 %collective-permute-start.3 = (bf16[144,1024]{1,0:T(8,128)(2,1)S(1)}, bf16[144,1024]{1,0:T(8,128)(2,1)S(1)}, u32[]{:S(2)}, u32[]{:S(2)}) collective-permute-start(bf16[144,1024]{1,0:T(8,128)(2,1)S(1)} %slice.41), channel_id=1, source_target_pairs={{0,24},{8,0},{16,8},{24,16},{32,56},{40,32},{48,40},{56,48},{64,88... | collective-permute-start | bytes 884744 | tf_op jit(solution)/shard_map/ppermute | solution.py:50
  31.8 7.1 %copy-start.4 = (bf16[288,1024]{1,0:T(8,128)(2,1)S(1)}, bf16[288,1024]{1,0:T(8,128)(2,1)}, u32[]{:S(2)}) copy-start(bf16[288,1024]{1,0:T(8,128)(2,1)} %get-tuple-element.38.refs_0_) | copy-start | bytes 1769476
  45.9 11.2 %copy-start.7 = (s32[256]{0:T(256)S(1)}, s32[256]{0:T(256)}, u32[]{:S(2)}) copy-start(s32[256]{0:T(256)} %pos_hbm.1) | copy-start | bytes 3076
  46.0 36.3 %copy-start = (bf16[4096,512]{1,0:T(8,128)(2,1)S(1)}, bf16[4096,512]{1,0:T(8,128)(2,1)}, u32[]{:S(2)}) copy-start(bf16[4096,512]{1,0:T(8,128)(2,1)} %wq_ref.1) | copy-start | bytes 12582916
  46.0 36.2 %copy-start.2 = (bf16[4096,128]{1,0:T(8,128)(2,1)S(1)}, bf16[4096,128]{1,0:T(8,128)(2,1)}, u32[]{:S(2)}) copy-start(bf16[4096,128]{1,0:T(8,128)(2,1)} %wv_ref.1) | copy-start | bytes 3145732
  49.2 33.0 %copy-start.1 = (bf16[4096,128]{1,0:T(8,128)(2,1)S(1)}, bf16[4096,128]{1,0:T(8,128)(2,1)}, u32[]{:S(2)}) copy-start(bf16[4096,128]{1,0:T(8,128)(2,1)} %wk_ref.1) | copy-start | bytes 3145732
  49.2 19.7 %collective-permute-start.13 = (bf16[512,256]{1,0:T(8,128)(2,1)S(1)}, bf16[512,256]{1,0:T(8,128)(2,1)S(1)}, u32[]{:S(2)}, u32[]{:S(2)}) collective-permute-start(bf16[512,256]{1,0:T(8,128)(2,1)S(1)} %get-tuple-element.57), channel_id=1, source_target_pairs={{0,16},{8,24},{16,0},{24,8},{32,48},{40,56},{48,32},{56,40},{64,80... | collective-permute-start | bytes 786440 | tf_op jit(solution)/shard_map/ppermute | solution.py:50
  51.6 22.1 %collective-permute-start.11 = (bf16[512,256]{1,0:T(8,128)(2,1)S(1)}, bf16[512,256]{1,0:T(8,128)(2,1)S(1)}, u32[]{:S(2)}, u32[]{:S(2)}) collective-permute-start(bf16[512,256]{1,0:T(8,128)(2,1)S(1)} %get-tuple-element.49), channel_id=1, source_target_pairs={{0,24},{8,0},{16,8},{24,16},{32,56},{40,32},{48,40},{56,48},{64,88... | collective-permute-start | bytes 786440 | tf_op jit(solution)/shard_map/ppermute | solution.py:50
  52.8 7.4 %collective-permute-start.14 = (bf16[384,256]{1,0:T(8,128)(2,1)S(1)}, bf16[384,256]{1,0:T(8,128)(2,1)S(1)}, u32[]{:S(2)}, u32[]{:S(2)}) collective-permute-start(bf16[384,256]{1,0:T(8,128)(2,1)S(1)} %get-tuple-element.63), channel_id=1, source_target_pairs={{0,192},{8,200},{16,208},{24,216},{32,224},{40,232},{48,240},{56,2... | collective-permute-start | bytes 589832 | tf_op jit(solution)/shard_map/ppermute | solution.py:43
  55.1 9.8 %collective-permute-start.15 = (bf16[384,256]{1,0:T(8,128)(2,1)S(1)}, bf16[384,256]{1,0:T(8,128)(2,1)S(1)}, u32[]{:S(2)}, u32[]{:S(2)}) collective-permute-start(bf16[384,256]{1,0:T(8,128)(2,1)S(1)} %get-tuple-element.64), channel_id=1, source_target_pairs={{0,64},{8,72},{16,80},{24,88},{32,96},{40,104},{48,112},{56,120},{... | collective-permute-start | bytes 589832 | tf_op jit(solution)/shard_map/ppermute | solution.py:43
  55.7 18.3 %collective-permute-start.12 = (bf16[512,256]{1,0:T(8,128)(2,1)S(1)}, bf16[512,256]{1,0:T(8,128)(2,1)S(1)}, u32[]{:S(2)}, u32[]{:S(2)}) collective-permute-start(bf16[512,256]{1,0:T(8,128)(2,1)S(1)} %get-tuple-element.50), channel_id=1, source_target_pairs={{0,8},{8,16},{16,24},{24,0},{32,40},{40,48},{48,56},{56,32},{64,72... | collective-permute-start | bytes 786440 | tf_op jit(solution)/shard_map/ppermute | solution.py:50
  65.0 9.1 %collective-permute-start.16 = (bf16[256,256]{1,0:T(8,128)(2,1)S(1)}, bf16[256,256]{1,0:T(8,128)(2,1)S(1)}, u32[]{:S(2)}, u32[]{:S(2)}) collective-permute-start(bf16[256,256]{1,0:T(8,128)(2,1)S(1)} %get-tuple-element.65), channel_id=1, source_target_pairs={{0,224},{8,232},{16,240},{24,248},{32,0},{40,8},{48,16},{56,24},{6... | collective-permute-start | bytes 393224 | tf_op jit(solution)/shard_map/ppermute | solution.py:43
  68.7 7.1 %collective-permute-start.17 = (bf16[256,256]{1,0:T(8,128)(2,1)S(1)}, bf16[256,256]{1,0:T(8,128)(2,1)S(1)}, u32[]{:S(2)}, u32[]{:S(2)}) collective-permute-start(bf16[256,256]{1,0:T(8,128)(2,1)S(1)} %get-tuple-element.66), channel_id=1, source_target_pairs={{0,32},{8,40},{16,48},{24,56},{32,64},{40,72},{48,80},{56,88},{64,... | collective-permute-start | bytes 393224 | tf_op jit(solution)/shard_map/ppermute | solution.py:43
  68.9 7.8 %collective-permute-start.18 = (bf16[256,256]{1,0:T(8,128)(2,1)S(1)}, bf16[256,256]{1,0:T(8,128)(2,1)S(1)}, u32[]{:S(2)}, u32[]{:S(2)}) collective-permute-start(bf16[256,256]{1,0:T(8,128)(2,1)S(1)} %get-tuple-element.67), channel_id=1, source_target_pairs={{0,192},{8,200},{16,208},{24,216},{32,224},{40,232},{48,240},{56,2... | collective-permute-start | bytes 393224 | tf_op jit(solution)/shard_map/ppermute | solution.py:43
  73.7 8.5 %collective-permute-start.19 = (bf16[256,256]{1,0:T(8,128)(2,1)S(1)}, bf16[256,256]{1,0:T(8,128)(2,1)S(1)}, u32[]{:S(2)}, u32[]{:S(2)}) collective-permute-start(bf16[256,256]{1,0:T(8,128)(2,1)S(1)} %get-tuple-element.68), channel_id=1, source_target_pairs={{0,64},{8,72},{16,80},{24,88},{32,96},{40,104},{48,112},{56,120},{... | collective-permute-start | bytes 393224 | tf_op jit(solution)/shard_map/ppermute | solution.py:43
  83.6 3.0 %collective-permute-start.20 = (bf16[4,512,256]{2,1,0:T(8,128)(2,1)S(1)}, bf16[4,512,256]{2,1,0:T(8,128)(2,1)S(1)}, u32[]{:S(2)}, u32[]{:S(2)}) collective-permute-start(bf16[4,512,256]{2,1,0:T(8,128)(2,1)S(1)} %get-tuple-element.70), channel_id=1, source_target_pairs={{0,1},{1,0},{2,3},{3,2},{4,5},{5,4},{6,7},{7,6},{8,9},{9,8},{10,11... | collective-permute-start | bytes 3145736 | tf_op jit(solution)/shard_map/ppermute | solution.py:62
  86.8 9.6 %collective-permute-start.21 = (bf16[512,256]{1,0:T(8,128)(2,1)S(1)}, bf16[512,256]{1,0:T(8,128)(2,1)S(1)}, u32[]{:S(2)}, u32[]{:S(2)}) collective-permute-start(bf16[512,256]{1,0:T(8,128)(2,1)S(1)} %get-tuple-element.73), channel_id=1, source_target_pairs={{0,2},{1,3},{2,4},{3,5},{4,6},{5,7},{6,0},{7,1},{8,10},{9,11},{10,... | collective-permute-start | bytes 786440 | tf_op jit(solution)/shard_map/ppermute | solution.py:57
  88.4 13.0 %collective-permute-start.22 = (bf16[512,256]{1,0:T(8,128)(2,1)S(1)}, bf16[512,256]{1,0:T(8,128)(2,1)S(1)}, u32[]{:S(2)}, u32[]{:S(2)}) collective-permute-start(bf16[512,256]{1,0:T(8,128)(2,1)S(1)} %get-tuple-element.72), channel_id=1, source_target_pairs={{0,6},{1,7},{2,0},{3,1},{4,2},{5,3},{6,4},{7,5},{8,14},{9,15},{10,... | collective-permute-start | bytes 786440 | tf_op jit(solution)/shard_map/ppermute | solution.py:57
  90.2 12.9 %collective-permute-start.23 = (bf16[512,256]{1,0:T(8,128)(2,1)S(1)}, bf16[512,256]{1,0:T(8,128)(2,1)S(1)}, u32[]{:S(2)}, u32[]{:S(2)}) collective-permute-start(bf16[512,256]{1,0:T(8,128)(2,1)S(1)} %get-tuple-element.71), channel_id=1, source_target_pairs={{0,4},{1,5},{2,6},{3,7},{4,0},{5,1},{6,2},{7,3},{8,12},{9,13},{10,... | collective-permute-start | bytes 786440 | tf_op jit(solution)/shard_map/ppermute | solution.py:57
where the time goes:
time: 104 us
  starting transfers between devices  39.1 us (38%)
  waiting for transfers between devices  34.8 us (33%)
  Pallas kernels  27.2 us (26%)
  local copies, waits for them, and re-layouts  2.04 us (2%)
    ppermute x13, starting transfers between devices, move_z(): return lax.ppermute(value, 'seq', pairs)  23.8 us
    ppermute x13, waiting for transfers between devices, move_z(): return lax.ppermute(value, 'seq', pairs)  22.3 us
    pallas_call x4, Pallas kernels, attend(): pl.pallas_call(functools.partial(attn_kernel, sizes, len(kvs), has_dq, ha...  20.5 us
    ppermute x3, waiting for transfers between devices, move_x(): return lax.ppermute(value, 'tp', pairs)  11.1 us
    ppermute x7, starting transfers between devices, move_y(): return lax.ppermute(value, 'seq', pairs)  9.86 us
    ppermute x3, starting transfers between devices, move_x(): return lax.ppermute(value, 'tp', pairs)  5.1 us
    pallas_call x1, Pallas kernels, layer(): pl.pallas_call(prep_kernel, out_shape=(whole((2 * PIECE, 1024), BF), whol...  3.06 us
  transfers between devices with their start and end apart: 24, of which 11 were waited for; matrix products, arithmetic and copies ran while one was open for 0% of the time, Pallas kernels for 11%

commit v1 on v0

--- a/solution.py
+++ b/solution.py
@@ -23,7 +23,7 @@
 PIECE = CHUNK + 16
 UNROLL = 2
 MIB = 1024 * 1024
-PREP_LIMIT = 60 * MIB
+PREP_LIMIT = 63 * MIB
 
 
 def dot(a, b, dims, precision=None):
@@ -114,6 +114,11 @@
         pack_ref[base + CHUNK : base + PIECE, :] = block.astype(BF)
 
 
+def stage_kernel(pack_ref, kv_ref, pack_out, kv_out):
+    pack_out[...] = pack_ref[...]
+    kv_out[...] = kv_ref[...]
+
+
 def attn_kernel(q_sizes, nkv, has_dq, has_dkv, layout, *refs):
     refs = list(refs)
 
@@ -129,7 +134,7 @@
     nblocks = sum(q_sizes) // 2
     dq_outs = take(nblocks)
     dkv_outs = take(len(layout))
-    qc, doc, ks, vs, kts, rowc, dq_acc, dk_acc, dv_acc, qst, kst, ln, l1, l2, lt1, lt2 = refs
+    qc, doc, ks, vs, kts, rowc, dq_acc, dk_acc, dv_acc, qst, kst, ln, lc, lg = refs
     nq = 2 * nblocks
     nk = 2 * nkv
 
@@ -176,48 +181,34 @@
                 dv_acc[2 * j + c] = jnp.zeros((128, 128), F32)
         at += has_dkv[j]
 
-    def per_query(n, tiles):
-        def per_key(c, state):
-            tiles, odd = state
-            gap = (qst[n] - kst[c]) * CHUNK
-            seen = gap >= 0
-
-            @pl.when(seen & (odd == 0))
-            def _():
-                ln[tiles] = n
-                l1[tiles] = c
-                l2[tiles] = c
-                lt1[tiles] = gap
-                lt2[tiles] = -100000
-
-            @pl.when(seen & (odd == 1))
-            def _():
-                l2[tiles] = c
-                lt2[tiles] = gap
-
-            step = seen.astype(jnp.int32)
-            return tiles + (step & odd), odd ^ step
-
-        tiles, odd = lax.fori_loop(0, nk, per_key, (tiles, jnp.int32(0)), unroll=True)
-        return tiles + odd
-
-    tiles = lax.fori_loop(0, nq, per_query, jnp.int32(0))
-    for extra in range(UNROLL - 1):
-        ln[tiles + extra] = 0
-        l1[tiles + extra] = 0
-        l2[tiles + extra] = 0
-        lt1[tiles + extra] = -100000
-        lt2[tiles + extra] = -100000
+    def per_query(n, count):
+        place = qst[n]
+        for c in range(nk):
+            gap = (place - kst[c]) * CHUNK
+            ln[count] = n
+            lc[count] = c
+            lg[count] = gap
+            count = count + (gap >= 0).astype(jnp.int32)
+        ln[count] = n
+        lc[count] = 0
+        lg[count] = -100000
+        return count + (count & 1)
+
+    count = lax.fori_loop(0, nq, per_query, jnp.int32(0))
+    for extra in range(2 * UNROLL - 2):
+        ln[count + extra] = 0
+        lc[count + extra] = 0
+        lg[count + extra] = -100000
 
     line = lax.broadcasted_iota(jnp.int32, (128, 256), 0)
     lane = lax.broadcasted_iota(jnp.int32, (128, 256), 1) & 127
     diff = line - lane
 
     def load(t):
-        n, c1, c2 = ln[t], l1[t], l2[t]
+        n, c1, c2 = ln[2 * t], lc[2 * t], lc[2 * t + 1]
         k = jnp.concatenate([ks[c1], ks[c2]], axis=0)
         v = jnp.concatenate([vs[c1], vs[c2]], axis=0)
-        return n, c1, c2, k, v, (lt1[t], lt2[t])
+        return n, c1, c2, k, v, (lg[2 * t], lg[2 * t + 1])
 
     def opening(unit):
         (n, _, _, k, v, _), half = unit
@@ -273,7 +264,7 @@
                 sums = closing(units[at - 1], made.pop(at - 1), sums)
         return carry
 
-    lax.fori_loop(0, (tiles + UNROLL - 1) // UNROLL, turn, 0)
+    lax.fori_loop(0, (count + 2 * UNROLL - 1) // (2 * UNROLL), turn, 0)
 
     for b in range(nblocks):
         for c in range(2):
@@ -297,7 +288,7 @@
     has_dq = tuple(int(g is not None) for g in dq_ins)
     has_dkv = tuple(int(g is not None) for g in dkv_ins)
     operands = list(packs) + list(kvs) + [g for g in list(dq_ins) + list(dkv_ins) if g is not None]
-    most = nq * ((nk + 1) // 2) + UNROLL
+    most = nq * (nk + 1) + 2 * UNROLL
     return pl.pallas_call(
         functools.partial(attn_kernel, sizes, len(kvs), has_dq, has_dkv, layout),
         out_shape=tuple(whole((512, ROWS), t) for t in dq_types)
@@ -317,7 +308,7 @@
             pltpu.SMEM((nq,), jnp.int32),
             pltpu.SMEM((nk,), jnp.int32),
         ]
-        + [pltpu.SMEM((most,), jnp.int32)] * 5,
+        + [pltpu.SMEM((most,), jnp.int32)] * 3,
         compiler_params=pltpu.CompilerParams(vmem_limit_bytes=28 * MIB),
         cost_estimate=pl.CostEstimate(
             flops=nq * nk * 85_000_000, bytes_accessed=4_000_000, transcendentals=nq * nk * 65536
@@ -415,14 +406,21 @@
     right = move_y(pack, -1)
     up1 = move_z(kv, 1)
     down1 = move_z(kv, -1)
-    up2 = move_z(up1, 1)
-    down2 = move_z(down1, -1)
+    up2 = move_z(kv, 2)
+    down2 = move_z(kv, -2)
     up3 = move_z(up2, 1)
     down3 = move_z(down2, -1)
-    up4 = move_z(up3, 1)
+    up4 = move_z(up2, 2)
     far0 = move_y(left[0:PIECE], 1)
     far1 = move_y(right[PIECE : 2 * PIECE], -1)
 
+    pack, kv = pl.pallas_call(
+        stage_kernel,
+        out_shape=(whole(pack.shape, BF), whole(kv.shape, BF)),
+        in_specs=[VM] * 2,
+        out_specs=(VM, VM),
+        compiler_params=pltpu.CompilerParams(vmem_limit_bytes=8 * MIB),
+    )(pack, kv)
     near = [kv, up1, down1, up2, down2]
     own = attend([pack], near, [None], [None] * 5, [F32], [F32] * 5)
     side = attend([left, right], near, [None] * 2, list(own[1:]), [F32] * 2, [F32] * 5)
@@ -446,7 +444,7 @@
         out_specs=(VM,) * 4,
         compiler_params=pltpu.CompilerParams(vmem_limit_bytes=8 * MIB),
     )(*last[2:6], back_up, back_down)
-    dkvs = [last[1]] + [move_z(part, steps) for part, steps in zip(merged, (-1, 1, -2, 2))]
+    dkvs = [last[1]] + [move_z(merged[i], steps) for i, steps in ((2, -2), (3, 2), (0, -1), (1, 1))]
 
     freqs = 500000.0 ** (-(jnp.arange(HALF, dtype=F32) * 2.0 / HEAD_DIM))
     angles = freqs[:, None] * positions.astype(F32)[None, :]
@@ -472,7 +470,7 @@
         ),
     )(grads, w_query, w_key, w_value)
     parts = [kept[i] + got[i].astype(F32) for i in range(4)]
-    came = [move_x(parts[i].astype(BF), i) for i in (1, 3, 2)]
+    came = [move_x(parts[i].astype(BF), i) for i in (2, 1, 3)]
     return pl.pallas_call(
         final_kernel,
         out_shape=whole((ROWS, 512), BF),

time: 104 us -> 102 us (0.981)
  the two profiles are of different devices: /device:TPU:8 before, /device:TPU:1 now
where the time goes in v1:
time: 102 us
  starting transfers between devices  46 us (45%)
  Pallas kernels  27.5 us (27%)
  waiting for transfers between devices  25.3 us (25%)
  local copies, waits for them, and re-layouts  2.04 us (2%)
    ppermute x13, starting transfers between devices, move_z(): return lax.ppermute(value, 'seq', pairs)  29.2 us
    pallas_call x4, Pallas kernels, attend(): pl.pallas_call(functools.partial(attn_kernel, sizes, len(kvs), has_dq, ha...  20.8 us
    ppermute x13, waiting for transfers between devices, move_z(): return lax.ppermute(value, 'seq', pairs)  14.3 us
    ppermute x3, waiting for transfers between devices, move_x(): return lax.ppermute(value, 'tp', pairs)  9.92 us
    ppermute x7, starting transfers between devices, move_y(): return lax.ppermute(value, 'seq', pairs)  8.17 us
    ppermute x3, starting transfers between devices, move_x(): return lax.ppermute(value, 'tp', pairs)  5.52 us
    pallas_call x1, Pallas kernels, layer(): pl.pallas_call(prep_kernel, out_shape=(whole((2 * PIECE, 1024), BF), whol...  3.04 us
    ppermute x1, starting transfers between devices, swap_core(): return lax.ppermute(value, 'tp', pairs)  3.04 us
  transfers between devices with their start and end apart: 24, of which 9 were waited for; matrix products, arithmetic and copies ran while one was open for 0% of the time, Pallas kernels for 10%

profile of v1, /device:TPU:1, one launch (start us, length us, event | category | flops | bytes accessed | tf_op | source)
XLA Modules:
  0.0 101.6 jit_solution(1564617161495157992)
XLA Ops:
  0.0 3.0 %shard_map.100 = (bf16[288,1024]{1,0:T(8,128)(2,1)}, bf16[272,256]{1,0:T(8,128)(2,1)}) custom-call(s32[256]{0:T(256)} %pos_hbm.1, bf16[256,512]{1,0:T(8,128)(2,1)} %q_hbm.1, bf16[256,512]{1,0:T(8,128)(2,1)} %do_hbm.1, bf16[256,512]{1,0:T(8,128)(2,1)} %o_hbm.1, f32[4,256]{1,0:T(4,128)} %lse_hbm.1, bf16[256,128]{1,0:T(8,128)(2,1)} %k_hbm.1, bf16[256,128]{1,0:T(8,128)(2,1)} %v_hbm.1), custom_call_target="tpu_custom_call" | custom-call | tf_op jit(solution)/shard_map/pallas_call | solution.py:391
  3.0 2.2 %collective-permute-start = (bf16[288,1024]{1,0:T(8,128)(2,1)}, bf16[288,1024]{1,0:T(8,128)(2,1)S(1)}, u32[]{:S(2)}, u32[]{:S(2)}) collective-permute-start(bf16[288,1024]{1,0:T(8,128)(2,1)} %get-tuple-element.40.pack_ref), channel_id=1, source_target_pairs={{0,8},{8,16},{16,24},{24,0},{32,40},{40,48},{48,56},{56,32},{64,72... | collective-permute-start | bytes 1769480 | tf_op jit(solution)/shard_map/ppermute | solution.py:50
  5.2 1.5 %collective-permute-start.1 = (bf16[288,1024]{1,0:T(8,128)(2,1)}, bf16[288,1024]{1,0:T(8,128)(2,1)S(1)}, u32[]{:S(2)}, u32[]{:S(2)}) collective-permute-start(bf16[288,1024]{1,0:T(8,128)(2,1)} %get-tuple-element.40.pack_ref), channel_id=1, source_target_pairs={{0,24},{8,0},{16,8},{24,16},{32,56},{40,32},{48,40},{56,48},{64,88... | collective-permute-start | bytes 1769480 | tf_op jit(solution)/shard_map/ppermute | solution.py:50
  6.8 3.0 %collective-permute-start.4 = (bf16[272,256]{1,0:T(8,128)(2,1)}, bf16[272,256]{1,0:T(8,128)(2,1)S(1)}, u32[]{:S(2)}, u32[]{:S(2)}) collective-permute-start(bf16[272,256]{1,0:T(8,128)(2,1)} %get-tuple-element.41.kv_ref), channel_id=1, source_target_pairs={{0,64},{8,72},{16,80},{24,88},{32,96},{40,104},{48,112},{56,120},{... | collective-permute-start | bytes 417800 | tf_op jit(solution)/shard_map/ppermute | solution.py:43
  9.8 3.0 %collective-permute-start.6 = (bf16[272,256]{1,0:T(8,128)(2,1)}, bf16[272,256]{1,0:T(8,128)(2,1)S(1)}, u32[]{:S(2)}, u32[]{:S(2)}) collective-permute-start(bf16[272,256]{1,0:T(8,128)(2,1)} %get-tuple-element.41.kv_ref), channel_id=1, source_target_pairs={{0,192},{8,200},{16,208},{24,216},{32,224},{40,232},{48,240},{56,2... | collective-permute-start | bytes 417800 | tf_op jit(solution)/shard_map/ppermute | solution.py:43
  12.8 1.9 %collective-permute-start.10 = (bf16[272,256]{1,0:T(8,128)(2,1)}, bf16[272,256]{1,0:T(8,128)(2,1)S(1)}, u32[]{:S(2)}, u32[]{:S(2)}) collective-permute-start(bf16[272,256]{1,0:T(8,128)(2,1)} %get-tuple-element.41.kv_ref), channel_id=1, source_target_pairs={{0,224},{8,232},{16,240},{24,248},{32,0},{40,8},{48,16},{56,24},{6... | collective-permute-start | bytes 417800 | tf_op jit(solution)/shard_map/ppermute | solution.py:43
  14.7 1.9 %collective-permute-done.4.refs_4_.refs_5_ = bf16[272,256]{1,0:T(8,128)(2,1)S(1)} collective-permute-done((bf16[272,256]{1,0:T(8,128)(2,1)}, bf16[272,256]{1,0:T(8,128)(2,1)S(1)}, u32[]{:S(2)}, u32[]{:S(2)}) %collective-permute-start.4) | collective-permute-done | bytes 139296 | tf_op jit(solution)/shard_map/ppermute | solution.py:43
  16.6 3.8 %collective-permute-start.9 = (bf16[272,256]{1,0:T(8,128)(2,1)}, bf16[272,256]{1,0:T(8,128)(2,1)S(1)}, u32[]{:S(2)}, u32[]{:S(2)}) collective-permute-start(bf16[272,256]{1,0:T(8,128)(2,1)} %get-tuple-element.41.kv_ref), channel_id=1, source_target_pairs={{0,32},{8,40},{16,48},{24,56},{32,64},{40,72},{48,80},{56,88},{64,... | collective-permute-start | bytes 417800 | tf_op jit(solution)/shard_map/ppermute | solution.py:43
  20.4 1.1 %copy-done.3 = bf16[288,1024]{1,0:T(8,128)(2,1)S(1)} copy-done((bf16[288,1024]{1,0:T(8,128)(2,1)S(1)}, bf16[288,1024]{1,0:T(8,128)(2,1)}, u32[]{:S(2)}) %copy-start.3) | copy-done | bytes 589848
  21.5 0.9 copy-done.4
  22.4 0.1 collective-permute-start.5
  22.5 0.4 collective-permute-done.10.refs_3_.refs_4_
  22.9 3.4 %collective-permute-start.8 = (bf16[272,256]{1,0:T(8,128)(2,1)S(1)}, bf16[272,256]{1,0:T(8,128)(2,1)S(1)}, u32[]{:S(2)}, u32[]{:S(2)}) collective-permute-start(bf16[272,256]{1,0:T(8,128)(2,1)S(1)} %collective-permute-done.4.refs_4_.refs_5_), channel_id=1, source_target_pairs={{0,64},{8,72},{16,80},{24,88},{32,96},{40,104},{48,112},{56,120},{... | collective-permute-start | bytes 417800 | tf_op jit(solution)/shard_map/ppermute | solution.py:43
  26.3 0.2 collective-permute-start.7
  26.5 3.1 %shard_map.102 = (f32[512,256]{1,0:T(8,128)S(1)}, f32[256,256]{1,0:T(8,128)S(1)}, f32[256,256]{1,0:T(8,128)S(1)}, f32[256,256]{1,0:T(8,128)S(1)}, f32[256,256]{1,0:T(8,128)S(1)}, /*index=5*/f32[256,256]{1,0:T(8,128)S(1)}) custom-call(bf16[288,1024]{1,0:T(8,128)(2,1)S(1)} %get-tuple-element.42.refs_0_, ...), custom_call_target="tpu_custom_call" | custom-call | flops 1700000000 | bytes 4000000 | tf_op jit(solution)/shard_map/pallas_call | solution.py:292
  29.7 0.1 collective-permute-start.2
  29.8 2.7 %collective-permute-start.3 = (bf16[144,1024]{1,0:T(8,128)(2,1)S(1)}, bf16[144,1024]{1,0:T(8,128)(2,1)S(1)}, u32[]{:S(2)}, u32[]{:S(2)}) collective-permute-start(bf16[144,1024]{1,0:T(8,128)(2,1)S(1)} %slice.41), channel_id=1, source_target_pairs={{0,24},{8,0},{16,8},{24,16},{32,56},{40,32},{48,40},{56,48},{64,88... | collective-permute-start | bytes 884744 | tf_op jit(solution)/shard_map/ppermute | solution.py:50
  32.6 5.2 %shard_map.103 = (f32[512,256]{1,0:T(8,128)S(1)}, f32[512,256]{1,0:T(8,128)S(1)}, f32[256,256]{1,0:T(8,128)S(1)}, f32[256,256]{1,0:T(8,128)S(1)}, f32[256,256]{1...) custom-call(bf16[288,1024]{1,0:T(8,128)(2,1)S(1)} %collective-permute-done.refs_0_.refs_1_, ...), custom_call_target="tpu_custom_call" | custom-call | flops 3400000000 | bytes 4000000 | tf_op jit(solution)/shard_map/pallas_call | solution.py:292
  37.8 8.5 %shard_map.104 = (f32[512,256]{1,0:T(8,128)S(1)}, bf16[512,256]{1,0:T(8,128)(2,1)S(1)}, bf16[512,256]{1,0:T(8,128)(2,1)S(1)}, f32[512,256]{1,0:T(8,128)S(1)}, bf...) custom-call(bf16[288,1024]{1,0:T(8,128)(2,1)S(1)} %get-tuple-element.42.refs_0_, ...), custom_call_target="tpu_custom_call" | custom-call | flops 4080000000 | bytes 4000000 | tf_op jit(solution)/shard_map/pallas_call | solution.py:292
  46.4 0.0 copy-start.5
  46.4 0.0 copy-start.2
  46.4 3.9 %shard_map.105 = (bf16[512,256]{1,0:T(8,128)(2,1)S(1)}, f32[256,256]{1,0:T(8,128)S(1)}, f32[256,256]{1,0:T(8,128)S(1)}, f32[256,256]{1,0:T(8,128)S(1)}, f32[256,256]{1,0:T(8,128)S(1)}, /*index=5*/f32[256,256]{1,0:T(8,128)S(1)}) custom-call(bf16[144,1024]{1,0:T(8,128)(2,1)S(1)} %collective-permute-done.2.refs_3_.refs_0_, ...), custom_call_target="tpu_custom_call" | custom-call | flops 1700000000 | bytes 4000000 | tf_op jit(solution)/shard_map/pallas_call | solution.py:292
  50.3 0.0 copy-start.1
  50.3 0.1 collective-permute-start.13
  50.4 1.0 collective-permute-start.11
  51.4 1.2 %collective-permute-start.14 = (bf16[384,256]{1,0:T(8,128)(2,1)S(1)}, bf16[384,256]{1,0:T(8,128)(2,1)S(1)}, u32[]{:S(2)}, u32[]{:S(2)}) collective-permute-start(bf16[384,256]{1,0:T(8,128)(2,1)S(1)} %get-tuple-element.67), channel_id=1, source_target_pairs={{0,192},{8,200},{16,208},{24,216},{32,224},{40,232},{48,240},{56,2... | collective-permute-start | bytes 589832 | tf_op jit(solution)/shard_map/ppermute | solution.py:43
  52.6 1.2 %collective-permute-start.15 = (bf16[384,256]{1,0:T(8,128)(2,1)S(1)}, bf16[384,256]{1,0:T(8,128)(2,1)S(1)}, u32[]{:S(2)}, u32[]{:S(2)}) collective-permute-start(bf16[384,256]{1,0:T(8,128)(2,1)S(1)} %get-tuple-element.68), channel_id=1, source_target_pairs={{0,64},{8,72},{16,80},{24,88},{32,96},{40,104},{48,112},{56,120},{... | collective-permute-start | bytes 589832 | tf_op jit(solution)/shard_map/ppermute | solution.py:43
  53.8 0.6 collective-permute-start.12
  54.4 2.5 %collective-permute-done.14.from_up = bf16[384,256]{1,0:T(8,128)(2,1)S(1)} collective-permute-done((bf16[384,256]{1,0:T(8,128)(2,1)S(1)}, bf16[384,256]{1,0:T(8,128)(2,1)S(1)}, u32[]{:S(2)}, u32[]{:S(2)}) %collective-permute-start.14) | collective-permute-done | bytes 196640 | tf_op jit(solution)/shard_map/ppermute | solution.py:43
  56.8 2.7 %collective-permute-done.15.from_down = bf16[384,256]{1,0:T(8,128)(2,1)S(1)} collective-permute-done((bf16[384,256]{1,0:T(8,128)(2,1)S(1)}, bf16[384,256]{1,0:T(8,128)(2,1)S(1)}, u32[]{:S(2)}, u32[]{:S(2)}) %collective-permute-start.15) | collective-permute-done | bytes 196640 | tf_op jit(solution)/shard_map/ppermute | solution.py:43
  59.5 0.1 shard_map.106
  59.6 0.1 collective-permute-start.16
  59.7 2.4 %collective-permute-start.17 = (bf16[256,256]{1,0:T(8,128)(2,1)S(1)}, bf16[256,256]{1,0:T(8,128)(2,1)S(1)}, u32[]{:S(2)}, u32[]{:S(2)}) collective-permute-start(bf16[256,256]{1,0:T(8,128)(2,1)S(1)} %get-tuple-element.70), channel_id=1, source_target_pairs={{0,64},{8,72},{16,80},{24,88},{32,96},{40,104},{48,112},{56,120},{... | collective-permute-start | bytes 393224 | tf_op jit(solution)/shard_map/ppermute | solution.py:43
  62.0 9.0 %collective-permute-start.18 = (bf16[256,256]{1,0:T(8,128)(2,1)S(1)}, bf16[256,256]{1,0:T(8,128)(2,1)S(1)}, u32[]{:S(2)}, u32[]{:S(2)}) collective-permute-start(bf16[256,256]{1,0:T(8,128)(2,1)S(1)} %get-tuple-element.71), channel_id=1, source_target_pairs={{0,224},{8,232},{16,240},{24,248},{32,0},{40,8},{48,16},{56,24},{6... | collective-permute-start | bytes 393224 | tf_op jit(solution)/shard_map/ppermute | solution.py:43
  71.1 0.3 multiply_sine_fusion
  71.4 4.1 %collective-permute-done.18.refs_7_ = bf16[256,256]{1,0:T(8,128)(2,1)S(1)} collective-permute-done((bf16[256,256]{1,0:T(8,128)(2,1)S(1)}, bf16[256,256]{1,0:T(8,128)(2,1)S(1)}, u32[]{:S(2)}, u32[]{:S(2)}) %collective-permute-start.18) | collective-permute-done | bytes 131104 | tf_op jit(solution)/shard_map/ppermute | solution.py:43
  75.5 2.7 %collective-permute-done.19.refs_8_ = bf16[256,256]{1,0:T(8,128)(2,1)S(1)} collective-permute-done((bf16[256,256]{1,0:T(8,128)(2,1)S(1)}, bf16[256,256]{1,0:T(8,128)(2,1)S(1)}, u32[]{:S(2)}, u32[]{:S(2)}) %collective-permute-start.19) | collective-permute-done | bytes 131104 | tf_op jit(solution)/shard_map/ppermute | solution.py:43
  78.3 1.4 %shard_map.107 = (bf16[768,256]{1,0:T(8,128)(2,1)S(1)}, bf16[4,512,256]{2,1,0:T(8,128)(2,1)S(1)}) custom-call(f32[512,256]{1,0:T(8,128)S(1)} %get-tuple-element.52.refs_0_, bf16[512,256]{1,0:T(8,128)(2,1)S(1)} %collective-permute-done.11.refs_1_, bf16[512,256]{1,0:T(8,128)(2,1)S(1)} %collective-permute-done.12.refs_2_, ...), custom_call_target="tpu_custom_call" | custom-call | tf_op jit(solution)/shard_map/pallas_call | solution.py:454
  79.7 3.0 %collective-permute-start.20 = (bf16[4,512,256]{2,1,0:T(8,128)(2,1)S(1)}, bf16[4,512,256]{2,1,0:T(8,128)(2,1)S(1)}, u32[]{:S(2)}, u32[]{:S(2)}) collective-permute-start(bf16[4,512,256]{2,1,0:T(8,128)(2,1)S(1)} %get-tuple-element.74), channel_id=1, source_target_pairs={{0,1},{1,0},{2,3},{3,2},{4,5},{5,4},{6,7},{7,6},{8,9},{9,8},{10,11... | collective-permute-start | bytes 3145736 | tf_op jit(solution)/shard_map/ppermute | solution.py:62
  82.7 1.2 %shard_map.108 = f32[4,512,256]{2,1,0:T(8,128)S(1)} custom-call(bf16[768,256]{1,0:T(8,128)(2,1)S(1)} %get-tuple-element.73.x_ref, bf16[4096,512]{1,0:T(8,128)(2,1)S(1)} %copy-done, bf16[4096,128]{1,0:T(8,128)(2,1)S(1)} %copy-done.1, bf16[4096,128]{1,0:T(8,128)(2,1)S(1)} %copy-done.2), custom_call_target="tpu_custom_call" | custom-call | flops 800000000 | bytes 4000000 | tf_op jit(solution)/shard_map/pallas_call | solution.py:462
  84.0 1.0 %collective-permute-done.20 = bf16[4,512,256]{2,1,0:T(8,128)(2,1)S(1)} collective-permute-done((bf16[4,512,256]{2,1,0:T(8,128)(2,1)S(1)}, bf16[4,512,256]{2,1,0:T(8,128)(2,1)S(1)}, u32[]{:S(2)}, u32[]{:S(2)}) %collective-permute-start.20) | collective-permute-done | bytes 1048608 | tf_op jit(solution)/shard_map/ppermute | solution.py:62
  85.0 0.2 fusion.6
  85.2 2.8 %collective-permute-start.21 = (bf16[512,256]{1,0:T(8,128)(2,1)S(1)}, bf16[512,256]{1,0:T(8,128)(2,1)S(1)}, u32[]{:S(2)}, u32[]{:S(2)}) collective-permute-start(bf16[512,256]{1,0:T(8,128)(2,1)S(1)} %get-tuple-element.77), channel_id=1, source_target_pairs={{0,4},{1,5},{2,6},{3,7},{4,0},{5,1},{6,2},{7,3},{8,12},{9,13},{10,... | collective-permute-start | bytes 786440 | tf_op jit(solution)/shard_map/ppermute | solution.py:57
  88.1 0.3 collective-permute-start.22
  88.4 2.4 %collective-permute-start.23 = (bf16[512,256]{1,0:T(8,128)(2,1)S(1)}, bf16[512,256]{1,0:T(8,128)(2,1)S(1)}, u32[]{:S(2)}, u32[]{:S(2)}) collective-permute-start(bf16[512,256]{1,0:T(8,128)(2,1)S(1)} %get-tuple-element.75), channel_id=1, source_target_pairs={{0,6},{1,7},{2,0},{3,1},{4,2},{5,3},{6,4},{7,5},{8,14},{9,15},{10,... | collective-permute-start | bytes 786440 | tf_op jit(solution)/shard_map/ppermute | solution.py:57
  90.8 3.6 %collective-permute-done.21.a_ref = bf16[512,256]{1,0:T(8,128)(2,1)S(1)} collective-permute-done((bf16[512,256]{1,0:T(8,128)(2,1)S(1)}, bf16[512,256]{1,0:T(8,128)(2,1)S(1)}, u32[]{:S(2)}, u32[]{:S(2)}) %collective-permute-start.21) | collective-permute-done | bytes 262176 | tf_op jit(solution)/shard_map/ppermute | solution.py:57
  94.4 6.3 %collective-permute-done.22.b_ref = bf16[512,256]{1,0:T(8,128)(2,1)S(1)} collective-permute-done((bf16[512,256]{1,0:T(8,128)(2,1)S(1)}, bf16[512,256]{1,0:T(8,128)(2,1)S(1)}, u32[]{:S(2)}, u32[]{:S(2)}) %collective-permute-start.22) | collective-permute-done | bytes 262176 | tf_op jit(solution)/shard_map/ppermute | solution.py:57
  100.7 0.9 shard_map.109
  (28 shorter events, 0.2 us)
Async XLA Ops:
  3.0 26.6 %collective-permute-start = (bf16[288,1024]{1,0:T(8,128)(2,1)}, bf16[288,1024]{1,0:T(8,128)(2,1)S(1)}, u32[]{:S(2)}, u32[]{:S(2)}) collective-permute-start(bf16[288,1024]{1,0:T(8,128)(2,1)} %get-tuple-element.40.pack_ref), channel_id=1, source_target_pairs={{0,8},{8,16},{16,24},{24,0},{32,40},{40,48},{48,56},{56,32},{64,72... | collective-permute-start | bytes 1769480 | tf_op jit(solution)/shard_map/ppermute | solution.py:50
  5.2 24.6 %collective-permute-start.1 = (bf16[288,1024]{1,0:T(8,128)(2,1)}, bf16[288,1024]{1,0:T(8,128)(2,1)S(1)}, u32[]{:S(2)}, u32[]{:S(2)}) collective-permute-start(bf16[288,1024]{1,0:T(8,128)(2,1)} %get-tuple-element.40.pack_ref), channel_id=1, source_target_pairs={{0,24},{8,0},{16,8},{24,16},{32,56},{40,32},{48,40},{56,48},{64,88... | collective-permute-start | bytes 1769480 | tf_op jit(solution)/shard_map/ppermute | solution.py:50
  6.8 9.8 %collective-permute-start.4 = (bf16[272,256]{1,0:T(8,128)(2,1)}, bf16[272,256]{1,0:T(8,128)(2,1)S(1)}, u32[]{:S(2)}, u32[]{:S(2)}) collective-permute-start(bf16[272,256]{1,0:T(8,128)(2,1)} %get-tuple-element.41.kv_ref), channel_id=1, source_target_pairs={{0,64},{8,72},{16,80},{24,88},{32,96},{40,104},{48,112},{56,120},{... | collective-permute-start | bytes 417800 | tf_op jit(solution)/shard_map/ppermute | solution.py:43
  9.8 12.7 %collective-permute-start.6 = (bf16[272,256]{1,0:T(8,128)(2,1)}, bf16[272,256]{1,0:T(8,128)(2,1)S(1)}, u32[]{:S(2)}, u32[]{:S(2)}) collective-permute-start(bf16[272,256]{1,0:T(8,128)(2,1)} %get-tuple-element.41.kv_ref), channel_id=1, source_target_pairs={{0,192},{8,200},{16,208},{24,216},{32,224},{40,232},{48,240},{56,2... | collective-permute-start | bytes 417800 | tf_op jit(solution)/shard_map/ppermute | solution.py:43
  12.8 10.1 %collective-permute-start.10 = (bf16[272,256]{1,0:T(8,128)(2,1)}, bf16[272,256]{1,0:T(8,128)(2,1)S(1)}, u32[]{:S(2)}, u32[]{:S(2)}) collective-permute-start(bf16[272,256]{1,0:T(8,128)(2,1)} %get-tuple-element.41.kv_ref), channel_id=1, source_target_pairs={{0,224},{8,232},{16,240},{24,248},{32,0},{40,8},{48,16},{56,24},{6... | collective-permute-start | bytes 417800 | tf_op jit(solution)/shard_map/ppermute | solution.py:43
  16.6 9.7 %collective-permute-start.9 = (bf16[272,256]{1,0:T(8,128)(2,1)}, bf16[272,256]{1,0:T(8,128)(2,1)S(1)}, u32[]{:S(2)}, u32[]{:S(2)}) collective-permute-start(bf16[272,256]{1,0:T(8,128)(2,1)} %get-tuple-element.41.kv_ref), channel_id=1, source_target_pairs={{0,32},{8,40},{16,48},{24,56},{32,64},{40,72},{48,80},{56,88},{64,... | collective-permute-start | bytes 417800 | tf_op jit(solution)/shard_map/ppermute | solution.py:43
  20.4 1.1 %copy-start.3 = (bf16[288,1024]{1,0:T(8,128)(2,1)S(1)}, bf16[288,1024]{1,0:T(8,128)(2,1)}, u32[]{:S(2)}) copy-start(bf16[288,1024]{1,0:T(8,128)(2,1)} %get-tuple-element.40.pack_ref) | copy-start | bytes 1769476
  21.5 0.9 copy-start.4
  22.4 15.3 %collective-permute-start.5 = (bf16[272,256]{1,0:T(8,128)(2,1)S(1)}, bf16[272,256]{1,0:T(8,128)(2,1)S(1)}, u32[]{:S(2)}, u32[]{:S(2)}) collective-permute-start(bf16[272,256]{1,0:T(8,128)(2,1)S(1)} %collective-permute-done.4.refs_4_.refs_5_), channel_id=1, source_target_pairs={{0,32},{8,40},{16,48},{24,56},{32,64},{40,72},{48,80},{56,88},{64,... | collective-permute-start | bytes 417800 | tf_op jit(solution)/shard_map/ppermute | solution.py:43
  22.9 14.8 %collective-permute-start.8 = (bf16[272,256]{1,0:T(8,128)(2,1)S(1)}, bf16[272,256]{1,0:T(8,128)(2,1)S(1)}, u32[]{:S(2)}, u32[]{:S(2)}) collective-permute-start(bf16[272,256]{1,0:T(8,128)(2,1)S(1)} %collective-permute-done.4.refs_4_.refs_5_), channel_id=1, source_target_pairs={{0,64},{8,72},{16,80},{24,88},{32,96},{40,104},{48,112},{56,120},{... | collective-permute-start | bytes 417800 | tf_op jit(solution)/shard_map/ppermute | solution.py:43
  26.3 11.5 %collective-permute-start.7 = (bf16[272,256]{1,0:T(8,128)(2,1)S(1)}, bf16[272,256]{1,0:T(8,128)(2,1)S(1)}, u32[]{:S(2)}, u32[]{:S(2)}) collective-permute-start(bf16[272,256]{1,0:T(8,128)(2,1)S(1)} %collective-permute-done.6.refs_5_.refs_6_), channel_id=1, source_target_pairs={{0,224},{8,232},{16,240},{24,248},{32,0},{40,8},{48,16},{56,24},{6... | collective-permute-start | bytes 417800 | tf_op jit(solution)/shard_map/ppermute | solution.py:43
  29.7 8.1 %collective-permute-start.2 = (bf16[144,1024]{1,0:T(8,128)(2,1)S(1)}, bf16[144,1024]{1,0:T(8,128)(2,1)S(1)}, u32[]{:S(2)}, u32[]{:S(2)}) collective-permute-start(bf16[144,1024]{1,0:T(8,128)(2,1)S(1)} %slice.40), channel_id=1, source_target_pairs={{0,8},{8,16},{16,24},{24,0},{32,40},{40,48},{48,56},{56,32},{64,72... | collective-permute-start | bytes 884744 | tf_op jit(solution)/shard_map/ppermute | solution.py:50
  29.8 8.0 %collective-permute-start.3 = (bf16[144,1024]{1,0:T(8,128)(2,1)S(1)}, bf16[144,1024]{1,0:T(8,128)(2,1)S(1)}, u32[]{:S(2)}, u32[]{:S(2)}) collective-permute-start(bf16[144,1024]{1,0:T(8,128)(2,1)S(1)} %slice.41), channel_id=1, source_target_pairs={{0,24},{8,0},{16,8},{24,16},{32,56},{40,32},{48,40},{56,48},{64,88... | collective-permute-start | bytes 884744 | tf_op jit(solution)/shard_map/ppermute | solution.py:50
  46.4 8.0 %copy-start.5 = (s32[256]{0:T(256)S(1)}, s32[256]{0:T(256)}, u32[]{:S(2)}) copy-start(s32[256]{0:T(256)} %pos_hbm.1) | copy-start | bytes 3076
  46.4 31.9 %copy-start = (bf16[4096,512]{1,0:T(8,128)(2,1)S(1)}, bf16[4096,512]{1,0:T(8,128)(2,1)}, u32[]{:S(2)}) copy-start(bf16[4096,512]{1,0:T(8,128)(2,1)} %wq_ref.1) | copy-start | bytes 12582916
  46.4 31.9 %copy-start.2 = (bf16[4096,128]{1,0:T(8,128)(2,1)S(1)}, bf16[4096,128]{1,0:T(8,128)(2,1)}, u32[]{:S(2)}) copy-start(bf16[4096,128]{1,0:T(8,128)(2,1)} %wv_ref.1) | copy-start | bytes 3145732
  50.3 27.9 %copy-start.1 = (bf16[4096,128]{1,0:T(8,128)(2,1)S(1)}, bf16[4096,128]{1,0:T(8,128)(2,1)}, u32[]{:S(2)}) copy-start(bf16[4096,128]{1,0:T(8,128)(2,1)} %wk_ref.1) | copy-start | bytes 3145732
  50.3 11.7 %collective-permute-start.13 = (bf16[512,256]{1,0:T(8,128)(2,1)S(1)}, bf16[512,256]{1,0:T(8,128)(2,1)S(1)}, u32[]{:S(2)}, u32[]{:S(2)}) collective-permute-start(bf16[512,256]{1,0:T(8,128)(2,1)S(1)} %get-tuple-element.61), channel_id=1, source_target_pairs={{0,16},{8,24},{16,0},{24,8},{32,48},{40,56},{48,32},{56,40},{64,80... | collective-permute-start | bytes 786440 | tf_op jit(solution)/shard_map/ppermute | solution.py:50
  50.4 20.6 %collective-permute-start.11 = (bf16[512,256]{1,0:T(8,128)(2,1)S(1)}, bf16[512,256]{1,0:T(8,128)(2,1)S(1)}, u32[]{:S(2)}, u32[]{:S(2)}) collective-permute-start(bf16[512,256]{1,0:T(8,128)(2,1)S(1)} %get-tuple-element.53), channel_id=1, source_target_pairs={{0,24},{8,0},{16,8},{24,16},{32,56},{40,32},{48,40},{56,48},{64,88... | collective-permute-start | bytes 786440 | tf_op jit(solution)/shard_map/ppermute | solution.py:50
  51.4 5.4 %collective-permute-start.14 = (bf16[384,256]{1,0:T(8,128)(2,1)S(1)}, bf16[384,256]{1,0:T(8,128)(2,1)S(1)}, u32[]{:S(2)}, u32[]{:S(2)}) collective-permute-start(bf16[384,256]{1,0:T(8,128)(2,1)S(1)} %get-tuple-element.67), channel_id=1, source_target_pairs={{0,192},{8,200},{16,208},{24,216},{32,224},{40,232},{48,240},{56,2... | collective-permute-start | bytes 589832 | tf_op jit(solution)/shard_map/ppermute | solution.py:43
  52.6 6.9 %collective-permute-start.15 = (bf16[384,256]{1,0:T(8,128)(2,1)S(1)}, bf16[384,256]{1,0:T(8,128)(2,1)S(1)}, u32[]{:S(2)}, u32[]{:S(2)}) collective-permute-start(bf16[384,256]{1,0:T(8,128)(2,1)S(1)} %get-tuple-element.68), channel_id=1, source_target_pairs={{0,64},{8,72},{16,80},{24,88},{32,96},{40,104},{48,112},{56,120},{... | collective-permute-start | bytes 589832 | tf_op jit(solution)/shard_map/ppermute | solution.py:43
  53.8 17.6 %collective-permute-start.12 = (bf16[512,256]{1,0:T(8,128)(2,1)S(1)}, bf16[512,256]{1,0:T(8,128)(2,1)S(1)}, u32[]{:S(2)}, u32[]{:S(2)}) collective-permute-start(bf16[512,256]{1,0:T(8,128)(2,1)S(1)} %get-tuple-element.54), channel_id=1, source_target_pairs={{0,8},{8,16},{16,24},{24,0},{32,40},{40,48},{48,56},{56,32},{64,72... | collective-permute-start | bytes 786440 | tf_op jit(solution)/shard_map/ppermute | solution.py:50
  59.6 11.8 %collective-permute-start.16 = (bf16[256,256]{1,0:T(8,128)(2,1)S(1)}, bf16[256,256]{1,0:T(8,128)(2,1)S(1)}, u32[]{:S(2)}, u32[]{:S(2)}) collective-permute-start(bf16[256,256]{1,0:T(8,128)(2,1)S(1)} %get-tuple-element.69), channel_id=1, source_target_pairs={{0,192},{8,200},{16,208},{24,216},{32,224},{40,232},{48,240},{56,2... | collective-permute-start | bytes 393224 | tf_op jit(solution)/shard_map/ppermute | solution.py:43
  59.7 11.7 %collective-permute-start.17 = (bf16[256,256]{1,0:T(8,128)(2,1)S(1)}, bf16[256,256]{1,0:T(8,128)(2,1)S(1)}, u32[]{:S(2)}, u32[]{:S(2)}) collective-permute-start(bf16[256,256]{1,0:T(8,128)(2,1)S(1)} %get-tuple-element.70), channel_id=1, source_target_pairs={{0,64},{8,72},{16,80},{24,88},{32,96},{40,104},{48,112},{56,120},{... | collective-permute-start | bytes 393224 | tf_op jit(solution)/shard_map/ppermute | solution.py:43
  62.0 13.5 %collective-permute-start.18 = (bf16[256,256]{1,0:T(8,128)(2,1)S(1)}, bf16[256,256]{1,0:T(8,128)(2,1)S(1)}, u32[]{:S(2)}, u32[]{:S(2)}) collective-permute-start(bf16[256,256]{1,0:T(8,128)(2,1)S(1)} %get-tuple-element.71), channel_id=1, source_target_pairs={{0,224},{8,232},{16,240},{24,248},{32,0},{40,8},{48,16},{56,24},{6... | collective-permute-start | bytes 393224 | tf_op jit(solution)/shard_map/ppermute | solution.py:43
  71.1 7.2 %collective-permute-start.19 = (bf16[256,256]{1,0:T(8,128)(2,1)S(1)}, bf16[256,256]{1,0:T(8,128)(2,1)S(1)}, u32[]{:S(2)}, u32[]{:S(2)}) collective-permute-start(bf16[256,256]{1,0:T(8,128)(2,1)S(1)} %get-tuple-element.72), channel_id=1, source_target_pairs={{0,32},{8,40},{16,48},{24,56},{32,64},{40,72},{48,80},{56,88},{64,... | collective-permute-start | bytes 393224 | tf_op jit(solution)/shard_map/ppermute | solution.py:43
  79.7 5.3 %collective-permute-start.20 = (bf16[4,512,256]{2,1,0:T(8,128)(2,1)S(1)}, bf16[4,512,256]{2,1,0:T(8,128)(2,1)S(1)}, u32[]{:S(2)}, u32[]{:S(2)}) collective-permute-start(bf16[4,512,256]{2,1,0:T(8,128)(2,1)S(1)} %get-tuple-element.74), channel_id=1, source_target_pairs={{0,1},{1,0},{2,3},{3,2},{4,5},{5,4},{6,7},{7,6},{8,9},{9,8},{10,11... | collective-permute-start | bytes 3145736 | tf_op jit(solution)/shard_map/ppermute | solution.py:62
  85.2 9.1 %collective-permute-start.21 = (bf16[512,256]{1,0:T(8,128)(2,1)S(1)}, bf16[512,256]{1,0:T(8,128)(2,1)S(1)}, u32[]{:S(2)}, u32[]{:S(2)}) collective-permute-start(bf16[512,256]{1,0:T(8,128)(2,1)S(1)} %get-tuple-element.77), channel_id=1, source_target_pairs={{0,4},{1,5},{2,6},{3,7},{4,0},{5,1},{6,2},{7,3},{8,12},{9,13},{10,... | collective-permute-start | bytes 786440 | tf_op jit(solution)/shard_map/ppermute | solution.py:57
  88.1 12.6 %collective-permute-start.22 = (bf16[512,256]{1,0:T(8,128)(2,1)S(1)}, bf16[512,256]{1,0:T(8,128)(2,1)S(1)}, u32[]{:S(2)}, u32[]{:S(2)}) collective-permute-start(bf16[512,256]{1,0:T(8,128)(2,1)S(1)} %get-tuple-element.76), channel_id=1, source_target_pairs={{0,2},{1,3},{2,4},{3,5},{4,6},{5,7},{6,0},{7,1},{8,10},{9,11},{10,... | collective-permute-start | bytes 786440 | tf_op jit(solution)/shard_map/ppermute | solution.py:57
  88.4 12.3 %collective-permute-start.23 = (bf16[512,256]{1,0:T(8,128)(2,1)S(1)}, bf16[512,256]{1,0:T(8,128)(2,1)S(1)}, u32[]{:S(2)}, u32[]{:S(2)}) collective-permute-start(bf16[512,256]{1,0:T(8,128)(2,1)S(1)} %get-tuple-element.75), channel_id=1, source_target_pairs={{0,6},{1,7},{2,0},{3,1},{4,2},{5,3},{6,4},{7,5},{8,14},{9,15},{10,... | collective-permute-start | bytes 786440 | tf_op jit(solution)/shard_map/ppermute | solution.py:57

commit v2 on v1

--- a/solution.py
+++ b/solution.py
@@ -411,8 +411,7 @@
     up3 = move_z(up2, 1)
     down3 = move_z(down2, -1)
     up4 = move_z(up2, 2)
-    far0 = move_y(left[0:PIECE], 1)
-    far1 = move_y(right[PIECE : 2 * PIECE], -1)
+    far = move_y(pack, 2)
 
     pack, kv = pl.pallas_call(
         stage_kernel,
@@ -422,12 +421,11 @@
         compiler_params=pltpu.CompilerParams(vmem_limit_bytes=8 * MIB),
     )(pack, kv)
     near = [kv, up1, down1, up2, down2]
-    own = attend([pack], near, [None], [None] * 5, [F32], [F32] * 5)
-    side = attend([left, right], near, [None] * 2, list(own[1:]), [F32] * 2, [F32] * 5)
+    first = attend([pack, left, right], near, [None] * 3, [None] * 5, [F32] * 3, [F32] * 5)
     outer = attend(
-        [pack, left, right, far0, far1],
+        [pack, left, right, far],
         [up3, down3, up4],
-        [own[0], side[0], side[1], None],
+        list(first[0:3]) + [None],
         [None] * 3,
         [F32, BF, BF, F32],
         [BF] * 2,
@@ -435,7 +433,7 @@
     )
     back_up = move_z(outer[4], -2)
     back_down = move_z(outer[5], 2)
-    last = attend([far0, far1], near, [outer[3]], list(side[2:]), [BF], [F32] * 5)
+    last = attend([far], near, [outer[3]], list(first[3:8]), [BF], [F32] * 5)
     dqs = [outer[0], move_y(outer[1], -1), move_y(outer[2], 1), move_y(last[0], 2)]
     merged = pl.pallas_call(
         merge_kernel,

time: 102 us -> 108 us (1.059)
  waiting for transfers between devices: 25.3 us -> 30.3 us
  starting transfers between devices: 46 us -> 47.2 us
    ppermute x1, starting transfers between devices: 3.04 us -> 10.9 us  [swap_core(): return lax.ppermute(value, 'tp', pairs)]
    ppermute x13, starting transfers between devices: 29.2 us -> 23.6 us  [move_z(): return lax.ppermute(value, 'seq', pairs)]
    ppermute x13, waiting for transfers between devices: 14.3 us -> 19.3 us  [move_z(): return lax.ppermute(value, 'seq', pairs)]
    ppermute x7 -> x6, starting transfers between devices: 8.17 us -> 7.26 us  [move_y(): return lax.ppermute(value, 'seq', pairs)]
    pallas_call x4 -> x3, Pallas kernels: 20.8 us -> 20.4 us  [attend(): pl.pallas_call(functools.partial(attn_kernel, sizes, len(kvs), has_dq, ha...]
  transfers between devices with their start and end apart: 24 -> 23, of which waited for: 9 -> 9; matrix products, arithmetic and copies ran while one was open for 0% -> 0% of each run, Pallas kernels for 10% -> 9%
where the time goes in v2:
time: 108 us; the launch traced here: 107 us
  starting transfers between devices  47.2 us (44%)
  waiting for transfers between devices  30.3 us (28%)
  Pallas kernels  27.1 us (25%)
  local copies, waits for them, and re-layouts  2.03 us (2%)
    ppermute x13, starting transfers between devices, move_z(): return lax.ppermute(value, 'seq', pairs)  23.6 us
    pallas_call x3, Pallas kernels, attend(): pl.pallas_call(functools.partial(attn_kernel, sizes, len(kvs), has_dq, ha...  20.4 us
    ppermute x13, waiting for transfers between devices, move_z(): return lax.ppermute(value, 'seq', pairs)  19.3 us
    ppermute x1, starting transfers between devices, swap_core(): return lax.ppermute(value, 'tp', pairs)  10.9 us
    ppermute x3, waiting for transfers between devices, move_x(): return lax.ppermute(value, 'tp', pairs)  9.92 us
    ppermute x6, starting transfers between devices, move_y(): return lax.ppermute(value, 'seq', pairs)  7.26 us
    ppermute x3, starting transfers between devices, move_x(): return lax.ppermute(value, 'tp', pairs)  5.51 us
    pallas_call x1, Pallas kernels, layer(): pl.pallas_call(prep_kernel, out_shape=(whole((2 * PIECE, 1024), BF), whol...  3.03 us
  transfers between devices with their start and end apart: 23, of which 9 were waited for; matrix products, arithmetic and copies ran while one was open for 0% of the time, Pallas kernels for 9%

profile of v2, /device:TPU:1, one launch (start us, length us, event | category | flops | bytes accessed | tf_op | source)
XLA Modules:
  0.0 107.4 jit_solution(6675265821259800419)
XLA Ops:
  0.0 3.0 %shard_map.100 = (bf16[288,1024]{1,0:T(8,128)(2,1)}, bf16[272,256]{1,0:T(8,128)(2,1)}) custom-call(s32[256]{0:T(256)} %pos_hbm.1, bf16[256,512]{1,0:T(8,128)(2,1)} %q_hbm.1, bf16[256,512]{1,0:T(8,128)(2,1)} %do_hbm.1, bf16[256,512]{1,0:T(8,128)(2,1)} %o_hbm.1, f32[4,256]{1,0:T(4,128)} %lse_hbm.1, bf16[256,128]{1,0:T(8,128)(2,1)} %k_hbm.1, bf16[256,128]{1,0:T(8,128)(2,1)} %v_hbm.1), custom_call_target="tpu_custom_call" | custom-call | tf_op jit(solution)/shard_map/pallas_call | solution.py:391
  3.0 2.2 %collective-permute-start = (bf16[288,1024]{1,0:T(8,128)(2,1)}, bf16[288,1024]{1,0:T(8,128)(2,1)S(1)}, u32[]{:S(2)}, u32[]{:S(2)}) collective-permute-start(bf16[288,1024]{1,0:T(8,128)(2,1)} %get-tuple-element.35.pack_ref), channel_id=1, source_target_pairs={{0,8},{8,16},{16,24},{24,0},{32,40},{40,48},{48,56},{56,32},{64,72... | collective-permute-start | bytes 1769480 | tf_op jit(solution)/shard_map/ppermute | solution.py:50
  5.2 1.5 %collective-permute-start.1 = (bf16[288,1024]{1,0:T(8,128)(2,1)}, bf16[288,1024]{1,0:T(8,128)(2,1)S(1)}, u32[]{:S(2)}, u32[]{:S(2)}) collective-permute-start(bf16[288,1024]{1,0:T(8,128)(2,1)} %get-tuple-element.35.pack_ref), channel_id=1, source_target_pairs={{0,24},{8,0},{16,8},{24,16},{32,56},{40,32},{48,40},{56,48},{64,88... | collective-permute-start | bytes 1769480 | tf_op jit(solution)/shard_map/ppermute | solution.py:50
  6.8 3.0 %collective-permute-start.3 = (bf16[272,256]{1,0:T(8,128)(2,1)}, bf16[272,256]{1,0:T(8,128)(2,1)S(1)}, u32[]{:S(2)}, u32[]{:S(2)}) collective-permute-start(bf16[272,256]{1,0:T(8,128)(2,1)} %get-tuple-element.36.kv_ref), channel_id=1, source_target_pairs={{0,64},{8,72},{16,80},{24,88},{32,96},{40,104},{48,112},{56,120},{... | collective-permute-start | bytes 417800 | tf_op jit(solution)/shard_map/ppermute | solution.py:43
  9.8 3.0 %collective-permute-start.5 = (bf16[272,256]{1,0:T(8,128)(2,1)}, bf16[272,256]{1,0:T(8,128)(2,1)S(1)}, u32[]{:S(2)}, u32[]{:S(2)}) collective-permute-start(bf16[272,256]{1,0:T(8,128)(2,1)} %get-tuple-element.36.kv_ref), channel_id=1, source_target_pairs={{0,192},{8,200},{16,208},{24,216},{32,224},{40,232},{48,240},{56,2... | collective-permute-start | bytes 417800 | tf_op jit(solution)/shard_map/ppermute | solution.py:43
  12.8 0.7 collective-permute-start.8
  13.5 3.1 %collective-permute-done.3.refs_6_.refs_4_ = bf16[272,256]{1,0:T(8,128)(2,1)S(1)} collective-permute-done((bf16[272,256]{1,0:T(8,128)(2,1)}, bf16[272,256]{1,0:T(8,128)(2,1)S(1)}, u32[]{:S(2)}, u32[]{:S(2)}) %collective-permute-start.3) | collective-permute-done | bytes 139296 | tf_op jit(solution)/shard_map/ppermute | solution.py:43
  16.6 4.3 %collective-permute-start.9 = (bf16[272,256]{1,0:T(8,128)(2,1)}, bf16[272,256]{1,0:T(8,128)(2,1)S(1)}, u32[]{:S(2)}, u32[]{:S(2)}) collective-permute-start(bf16[272,256]{1,0:T(8,128)(2,1)} %get-tuple-element.36.kv_ref), channel_id=1, source_target_pairs={{0,224},{8,232},{16,240},{24,248},{32,0},{40,8},{48,16},{56,24},{6... | collective-permute-start | bytes 417800 | tf_op jit(solution)/shard_map/ppermute | solution.py:43
  20.9 0.0 collective-permute-done.5.refs_7_.refs_5_
  20.9 1.5 %collective-permute-start.2 = (bf16[288,1024]{1,0:T(8,128)(2,1)}, bf16[288,1024]{1,0:T(8,128)(2,1)S(1)}, u32[]{:S(2)}, u32[]{:S(2)}) collective-permute-start(bf16[288,1024]{1,0:T(8,128)(2,1)} %get-tuple-element.35.pack_ref), channel_id=1, source_target_pairs={{0,16},{8,24},{16,0},{24,8},{32,48},{40,56},{48,32},{56,40},{64,80... | collective-permute-start | bytes 1769480 | tf_op jit(solution)/shard_map/ppermute | solution.py:50
  22.4 1.1 %copy-done.3 = bf16[288,1024]{1,0:T(8,128)(2,1)S(1)} copy-done((bf16[288,1024]{1,0:T(8,128)(2,1)S(1)}, bf16[288,1024]{1,0:T(8,128)(2,1)}, u32[]{:S(2)}) %copy-start.3) | copy-done | bytes 589848
  23.5 0.9 copy-done.4
  24.5 0.0 collective-permute-done.8.refs_4_.refs_2_
  24.5 0.1 collective-permute-start.4
  24.6 3.0 %collective-permute-start.7 = (bf16[272,256]{1,0:T(8,128)(2,1)S(1)}, bf16[272,256]{1,0:T(8,128)(2,1)S(1)}, u32[]{:S(2)}, u32[]{:S(2)}) collective-permute-start(bf16[272,256]{1,0:T(8,128)(2,1)S(1)} %collective-permute-done.3.refs_6_.refs_4_), channel_id=1, source_target_pairs={{0,64},{8,72},{16,80},{24,88},{32,96},{40,104},{48,112},{56,120},{... | collective-permute-start | bytes 417800 | tf_op jit(solution)/shard_map/ppermute | solution.py:43
  27.5 2.6 %collective-permute-start.6 = (bf16[272,256]{1,0:T(8,128)(2,1)S(1)}, bf16[272,256]{1,0:T(8,128)(2,1)S(1)}, u32[]{:S(2)}, u32[]{:S(2)}) collective-permute-start(bf16[272,256]{1,0:T(8,128)(2,1)S(1)} %collective-permute-done.5.refs_7_.refs_5_), channel_id=1, source_target_pairs={{0,224},{8,232},{16,240},{24,248},{32,0},{40,8},{48,16},{56,24},{6... | collective-permute-start | bytes 417800 | tf_op jit(solution)/shard_map/ppermute | solution.py:43
  30.1 7.8 %shard_map.102 = (f32[512,256]{1,0:T(8,128)S(1)}, f32[512,256]{1,0:T(8,128)S(1)}, f32[512,256]{1,0:T(8,128)S(1)}, f32[256,256]{1,0:T(8,128)S(1)}, f32[256,256]{1...) custom-call(bf16[288,1024]{1,0:T(8,128)(2,1)S(1)} %get-tuple-element.37.refs_0_, ...), custom_call_target="tpu_custom_call" | custom-call | flops 5100000256 | bytes 4000000 | tf_op jit(solution)/shard_map/pallas_call | solution.py:292
  37.9 8.5 %shard_map.103 = (f32[512,256]{1,0:T(8,128)S(1)}, bf16[512,256]{1,0:T(8,128)(2,1)S(1)}, bf16[512,256]{1,0:T(8,128)(2,1)S(1)}, f32[512,256]{1,0:T(8,128)S(1)}, bf...) custom-call(bf16[288,1024]{1,0:T(8,128)(2,1)S(1)} %get-tuple-element.37.refs_0_, ...), custom_call_target="tpu_custom_call" | custom-call | flops 4080000000 | bytes 4000000 | tf_op jit(solution)/shard_map/pallas_call | solution.py:292
  46.5 0.0 copy-start.5
  46.5 0.0 copy-start
  46.5 0.0 copy-start.2
  46.5 4.1 %shard_map.104 = (bf16[512,256]{1,0:T(8,128)(2,1)S(1)}, f32[256,256]{1,0:T(8,128)S(1)}, f32[256,256]{1,0:T(8,128)S(1)}, f32[256,256]{1,0:T(8,128)S(1)}, f32[256,256]{1,0:T(8,128)S(1)}, /*index=5*/f32[256,256]{1,0:T(8,128)S(1)}) custom-call(bf16[288,1024]{1,0:T(8,128)(2,1)S(1)} %collective-permute-done.2.refs_3_.refs_0_, ...), custom_call_target="tpu_custom_call" | custom-call | flops 1700000000 | bytes 4000000 | tf_op jit(solution)/shard_map/pallas_call | solution.py:292
  50.6 0.0 copy-start.1
  50.6 0.1 collective-permute-start.12
  50.7 2.0 %collective-permute-start.10 = (bf16[512,256]{1,0:T(8,128)(2,1)S(1)}, bf16[512,256]{1,0:T(8,128)(2,1)S(1)}, u32[]{:S(2)}, u32[]{:S(2)}) collective-permute-start(bf16[512,256]{1,0:T(8,128)(2,1)S(1)} %get-tuple-element.43), channel_id=1, source_target_pairs={{0,24},{8,0},{16,8},{24,16},{32,56},{40,32},{48,40},{56,48},{64,88... | collective-permute-start | bytes 786440 | tf_op jit(solution)/shard_map/ppermute | solution.py:50
  52.7 1.2 %collective-permute-start.13 = (bf16[384,256]{1,0:T(8,128)(2,1)S(1)}, bf16[384,256]{1,0:T(8,128)(2,1)S(1)}, u32[]{:S(2)}, u32[]{:S(2)}) collective-permute-start(bf16[384,256]{1,0:T(8,128)(2,1)S(1)} %get-tuple-element.57), channel_id=1, source_target_pairs={{0,192},{8,200},{16,208},{24,216},{32,224},{40,232},{48,240},{56,2... | collective-permute-start | bytes 589832 | tf_op jit(solution)/shard_map/ppermute | solution.py:43
  53.9 1.2 %collective-permute-start.14 = (bf16[384,256]{1,0:T(8,128)(2,1)S(1)}, bf16[384,256]{1,0:T(8,128)(2,1)S(1)}, u32[]{:S(2)}, u32[]{:S(2)}) collective-permute-start(bf16[384,256]{1,0:T(8,128)(2,1)S(1)} %get-tuple-element.58), channel_id=1, source_target_pairs={{0,64},{8,72},{16,80},{24,88},{32,96},{40,104},{48,112},{56,120},{... | collective-permute-start | bytes 589832 | tf_op jit(solution)/shard_map/ppermute | solution.py:43
  55.1 4.9 %collective-permute-done.13.from_up = bf16[384,256]{1,0:T(8,128)(2,1)S(1)} collective-permute-done((bf16[384,256]{1,0:T(8,128)(2,1)S(1)}, bf16[384,256]{1,0:T(8,128)(2,1)S(1)}, u32[]{:S(2)}, u32[]{:S(2)}) %collective-permute-start.13) | collective-permute-done | bytes 196640 | tf_op jit(solution)/shard_map/ppermute | solution.py:43
  60.0 2.9 %collective-permute-done.14.from_down = bf16[384,256]{1,0:T(8,128)(2,1)S(1)} collective-permute-done((bf16[384,256]{1,0:T(8,128)(2,1)S(1)}, bf16[384,256]{1,0:T(8,128)(2,1)S(1)}, u32[]{:S(2)}, u32[]{:S(2)}) %collective-permute-start.14) | collective-permute-done | bytes 196640 | tf_op jit(solution)/shard_map/ppermute | solution.py:43
  62.9 0.1 shard_map.105
  63.0 0.1 collective-permute-start.15
  63.1 2.4 %collective-permute-start.16 = (bf16[256,256]{1,0:T(8,128)(2,1)S(1)}, bf16[256,256]{1,0:T(8,128)(2,1)S(1)}, u32[]{:S(2)}, u32[]{:S(2)}) collective-permute-start(bf16[256,256]{1,0:T(8,128)(2,1)S(1)} %get-tuple-element.60), channel_id=1, source_target_pairs={{0,64},{8,72},{16,80},{24,88},{32,96},{40,104},{48,112},{56,120},{... | collective-permute-start | bytes 393224 | tf_op jit(solution)/shard_map/ppermute | solution.py:43
  65.5 2.0 %collective-permute-start.17 = (bf16[256,256]{1,0:T(8,128)(2,1)S(1)}, bf16[256,256]{1,0:T(8,128)(2,1)S(1)}, u32[]{:S(2)}, u32[]{:S(2)}) collective-permute-start(bf16[256,256]{1,0:T(8,128)(2,1)S(1)} %get-tuple-element.61), channel_id=1, source_target_pairs={{0,224},{8,232},{16,240},{24,248},{32,0},{40,8},{48,16},{56,24},{6... | collective-permute-start | bytes 393224 | tf_op jit(solution)/shard_map/ppermute | solution.py:43
  67.5 0.3 multiply_sine_fusion
  67.9 0.3 collective-permute-done.15.refs_5_
  68.2 5.9 %collective-permute-done.16.refs_6_ = bf16[256,256]{1,0:T(8,128)(2,1)S(1)} collective-permute-done((bf16[256,256]{1,0:T(8,128)(2,1)S(1)}, bf16[256,256]{1,0:T(8,128)(2,1)S(1)}, u32[]{:S(2)}, u32[]{:S(2)}) %collective-permute-start.16) | collective-permute-done | bytes 131104 | tf_op jit(solution)/shard_map/ppermute | solution.py:43
  74.1 2.2 %collective-permute-done.18.refs_8_ = bf16[256,256]{1,0:T(8,128)(2,1)S(1)} collective-permute-done((bf16[256,256]{1,0:T(8,128)(2,1)S(1)}, bf16[256,256]{1,0:T(8,128)(2,1)S(1)}, u32[]{:S(2)}, u32[]{:S(2)}) %collective-permute-start.18) | collective-permute-done | bytes 131104 | tf_op jit(solution)/shard_map/ppermute | solution.py:43
  76.2 1.4 %shard_map.106 = (bf16[768,256]{1,0:T(8,128)(2,1)S(1)}, bf16[4,512,256]{2,1,0:T(8,128)(2,1)S(1)}) custom-call(f32[512,256]{1,0:T(8,128)S(1)} %get-tuple-element.42.refs_0_, bf16[512,256]{1,0:T(8,128)(2,1)S(1)} %collective-permute-done.10.refs_1_, bf16[512,256]{1,0:T(8,128)(2,1)S(1)} %collective-permute-done.11.refs_2_, ...), custom_call_target="tpu_custom_call" | custom-call | tf_op jit(solution)/shard_map/pallas_call | solution.py:452
  77.7 10.9 %collective-permute-start.19 = (bf16[4,512,256]{2,1,0:T(8,128)(2,1)S(1)}, bf16[4,512,256]{2,1,0:T(8,128)(2,1)S(1)}, u32[]{:S(2)}, u32[]{:S(2)}) collective-permute-start(bf16[4,512,256]{2,1,0:T(8,128)(2,1)S(1)} %get-tuple-element.64), channel_id=1, source_target_pairs={{0,1},{1,0},{2,3},{3,2},{4,5},{5,4},{6,7},{7,6},{8,9},{9,8},{10,11... | collective-permute-start | bytes 3145736 | tf_op jit(solution)/shard_map/ppermute | solution.py:62
  88.5 1.2 %shard_map.107 = f32[4,512,256]{2,1,0:T(8,128)S(1)} custom-call(bf16[768,256]{1,0:T(8,128)(2,1)S(1)} %get-tuple-element.63.x_ref, bf16[4096,512]{1,0:T(8,128)(2,1)S(1)} %copy-done, bf16[4096,128]{1,0:T(8,128)(2,1)S(1)} %copy-done.1, bf16[4096,128]{1,0:T(8,128)(2,1)S(1)} %copy-done.2), custom_call_target="tpu_custom_call" | custom-call | flops 800000000 | bytes 4000000 | tf_op jit(solution)/shard_map/pallas_call | solution.py:460
  89.8 1.1 collective-permute-done.19
  90.8 0.2 fusion.6
  91.0 2.8 %collective-permute-start.20 = (bf16[512,256]{1,0:T(8,128)(2,1)S(1)}, bf16[512,256]{1,0:T(8,128)(2,1)S(1)}, u32[]{:S(2)}, u32[]{:S(2)}) collective-permute-start(bf16[512,256]{1,0:T(8,128)(2,1)S(1)} %get-tuple-element.67), channel_id=1, source_target_pairs={{0,4},{1,5},{2,6},{3,7},{4,0},{5,1},{6,2},{7,3},{8,12},{9,13},{10,... | collective-permute-start | bytes 786440 | tf_op jit(solution)/shard_map/ppermute | solution.py:57
  93.9 0.3 collective-permute-start.21
  94.2 2.4 %collective-permute-start.22 = (bf16[512,256]{1,0:T(8,128)(2,1)S(1)}, bf16[512,256]{1,0:T(8,128)(2,1)S(1)}, u32[]{:S(2)}, u32[]{:S(2)}) collective-permute-start(bf16[512,256]{1,0:T(8,128)(2,1)S(1)} %get-tuple-element.65), channel_id=1, source_target_pairs={{0,6},{1,7},{2,0},{3,1},{4,2},{5,3},{6,4},{7,5},{8,14},{9,15},{10,... | collective-permute-start | bytes 786440 | tf_op jit(solution)/shard_map/ppermute | solution.py:57
  96.6 3.6 %collective-permute-done.20.a_ref = bf16[512,256]{1,0:T(8,128)(2,1)S(1)} collective-permute-done((bf16[512,256]{1,0:T(8,128)(2,1)S(1)}, bf16[512,256]{1,0:T(8,128)(2,1)S(1)}, u32[]{:S(2)}, u32[]{:S(2)}) %collective-permute-start.20) | collective-permute-done | bytes 262176 | tf_op jit(solution)/shard_map/ppermute | solution.py:57
  100.2 6.3 %collective-permute-done.21.b_ref = bf16[512,256]{1,0:T(8,128)(2,1)S(1)} collective-permute-done((bf16[512,256]{1,0:T(8,128)(2,1)S(1)}, bf16[512,256]{1,0:T(8,128)(2,1)S(1)}, u32[]{:S(2)}, u32[]{:S(2)}) %collective-permute-start.21) | collective-permute-done | bytes 262176 | tf_op jit(solution)/shard_map/ppermute | solution.py:57
  106.5 0.9 shard_map.108
  (23 shorter events, 0.1 us)
Async XLA Ops:
  3.0 24.5 %collective-permute-start = (bf16[288,1024]{1,0:T(8,128)(2,1)}, bf16[288,1024]{1,0:T(8,128)(2,1)S(1)}, u32[]{:S(2)}, u32[]{:S(2)}) collective-permute-start(bf16[288,1024]{1,0:T(8,128)(2,1)} %get-tuple-element.35.pack_ref), channel_id=1, source_target_pairs={{0,8},{8,16},{16,24},{24,0},{32,40},{40,48},{48,56},{56,32},{64,72... | collective-permute-start | bytes 1769480 | tf_op jit(solution)/shard_map/ppermute | solution.py:50
  5.2 24.9 %collective-permute-start.1 = (bf16[288,1024]{1,0:T(8,128)(2,1)}, bf16[288,1024]{1,0:T(8,128)(2,1)S(1)}, u32[]{:S(2)}, u32[]{:S(2)}) collective-permute-start(bf16[288,1024]{1,0:T(8,128)(2,1)} %get-tuple-element.35.pack_ref), channel_id=1, source_target_pairs={{0,24},{8,0},{16,8},{24,16},{32,56},{40,32},{48,40},{56,48},{64,88... | collective-permute-start | bytes 1769480 | tf_op jit(solution)/shard_map/ppermute | solution.py:50
  6.8 9.8 %collective-permute-start.3 = (bf16[272,256]{1,0:T(8,128)(2,1)}, bf16[272,256]{1,0:T(8,128)(2,1)S(1)}, u32[]{:S(2)}, u32[]{:S(2)}) collective-permute-start(bf16[272,256]{1,0:T(8,128)(2,1)} %get-tuple-element.36.kv_ref), channel_id=1, source_target_pairs={{0,64},{8,72},{16,80},{24,88},{32,96},{40,104},{48,112},{56,120},{... | collective-permute-start | bytes 417800 | tf_op jit(solution)/shard_map/ppermute | solution.py:43
  9.8 11.2 %collective-permute-start.5 = (bf16[272,256]{1,0:T(8,128)(2,1)}, bf16[272,256]{1,0:T(8,128)(2,1)S(1)}, u32[]{:S(2)}, u32[]{:S(2)}) collective-permute-start(bf16[272,256]{1,0:T(8,128)(2,1)} %get-tuple-element.36.kv_ref), channel_id=1, source_target_pairs={{0,192},{8,200},{16,208},{24,216},{32,224},{40,232},{48,240},{56,2... | collective-permute-start | bytes 417800 | tf_op jit(solution)/shard_map/ppermute | solution.py:43
  12.8 11.7 %collective-permute-start.8 = (bf16[272,256]{1,0:T(8,128)(2,1)}, bf16[272,256]{1,0:T(8,128)(2,1)S(1)}, u32[]{:S(2)}, u32[]{:S(2)}) collective-permute-start(bf16[272,256]{1,0:T(8,128)(2,1)} %get-tuple-element.36.kv_ref), channel_id=1, source_target_pairs={{0,32},{8,40},{16,48},{24,56},{32,64},{40,72},{48,80},{56,88},{64,... | collective-permute-start | bytes 417800 | tf_op jit(solution)/shard_map/ppermute | solution.py:43
  16.6 8.0 %collective-permute-start.9 = (bf16[272,256]{1,0:T(8,128)(2,1)}, bf16[272,256]{1,0:T(8,128)(2,1)S(1)}, u32[]{:S(2)}, u32[]{:S(2)}) collective-permute-start(bf16[272,256]{1,0:T(8,128)(2,1)} %get-tuple-element.36.kv_ref), channel_id=1, source_target_pairs={{0,224},{8,232},{16,240},{24,248},{32,0},{40,8},{48,16},{56,24},{6... | collective-permute-start | bytes 417800 | tf_op jit(solution)/shard_map/ppermute | solution.py:43
  20.9 17.0 %collective-permute-start.2 = (bf16[288,1024]{1,0:T(8,128)(2,1)}, bf16[288,1024]{1,0:T(8,128)(2,1)S(1)}, u32[]{:S(2)}, u32[]{:S(2)}) collective-permute-start(bf16[288,1024]{1,0:T(8,128)(2,1)} %get-tuple-element.35.pack_ref), channel_id=1, source_target_pairs={{0,16},{8,24},{16,0},{24,8},{32,48},{40,56},{48,32},{56,40},{64,80... | collective-permute-start | bytes 1769480 | tf_op jit(solution)/shard_map/ppermute | solution.py:50
  22.4 1.1 %copy-start.3 = (bf16[288,1024]{1,0:T(8,128)(2,1)S(1)}, bf16[288,1024]{1,0:T(8,128)(2,1)}, u32[]{:S(2)}) copy-start(bf16[288,1024]{1,0:T(8,128)(2,1)} %get-tuple-element.35.pack_ref) | copy-start | bytes 1769476
  23.5 0.9 copy-start.4
  24.5 13.4 %collective-permute-start.4 = (bf16[272,256]{1,0:T(8,128)(2,1)S(1)}, bf16[272,256]{1,0:T(8,128)(2,1)S(1)}, u32[]{:S(2)}, u32[]{:S(2)}) collective-permute-start(bf16[272,256]{1,0:T(8,128)(2,1)S(1)} %collective-permute-done.3.refs_6_.refs_4_), channel_id=1, source_target_pairs={{0,32},{8,40},{16,48},{24,56},{32,64},{40,72},{48,80},{56,88},{64,... | collective-permute-start | bytes 417800 | tf_op jit(solution)/shard_map/ppermute | solution.py:43
  24.6 13.3 %collective-permute-start.7 = (bf16[272,256]{1,0:T(8,128)(2,1)S(1)}, bf16[272,256]{1,0:T(8,128)(2,1)S(1)}, u32[]{:S(2)}, u32[]{:S(2)}) collective-permute-start(bf16[272,256]{1,0:T(8,128)(2,1)S(1)} %collective-permute-done.3.refs_6_.refs_4_), channel_id=1, source_target_pairs={{0,64},{8,72},{16,80},{24,88},{32,96},{40,104},{48,112},{56,120},{... | collective-permute-start | bytes 417800 | tf_op jit(solution)/shard_map/ppermute | solution.py:43
  27.5 10.4 %collective-permute-start.6 = (bf16[272,256]{1,0:T(8,128)(2,1)S(1)}, bf16[272,256]{1,0:T(8,128)(2,1)S(1)}, u32[]{:S(2)}, u32[]{:S(2)}) collective-permute-start(bf16[272,256]{1,0:T(8,128)(2,1)S(1)} %collective-permute-done.5.refs_7_.refs_5_), channel_id=1, source_target_pairs={{0,224},{8,232},{16,240},{24,248},{32,0},{40,8},{48,16},{56,24},{6... | collective-permute-start | bytes 417800 | tf_op jit(solution)/shard_map/ppermute | solution.py:43
  46.5 8.6 %copy-start.5 = (s32[256]{0:T(256)S(1)}, s32[256]{0:T(256)}, u32[]{:S(2)}) copy-start(s32[256]{0:T(256)} %pos_hbm.1) | copy-start | bytes 3076
  46.5 29.7 %copy-start = (bf16[4096,512]{1,0:T(8,128)(2,1)S(1)}, bf16[4096,512]{1,0:T(8,128)(2,1)}, u32[]{:S(2)}) copy-start(bf16[4096,512]{1,0:T(8,128)(2,1)} %wq_ref.1) | copy-start | bytes 12582916
  46.5 29.7 %copy-start.2 = (bf16[4096,128]{1,0:T(8,128)(2,1)S(1)}, bf16[4096,128]{1,0:T(8,128)(2,1)}, u32[]{:S(2)}) copy-start(bf16[4096,128]{1,0:T(8,128)(2,1)} %wv_ref.1) | copy-start | bytes 3145732
  50.6 25.6 %copy-start.1 = (bf16[4096,128]{1,0:T(8,128)(2,1)S(1)}, bf16[4096,128]{1,0:T(8,128)(2,1)}, u32[]{:S(2)}) copy-start(bf16[4096,128]{1,0:T(8,128)(2,1)} %wk_ref.1) | copy-start | bytes 3145732
  50.6 14.9 %collective-permute-start.12 = (bf16[512,256]{1,0:T(8,128)(2,1)S(1)}, bf16[512,256]{1,0:T(8,128)(2,1)S(1)}, u32[]{:S(2)}, u32[]{:S(2)}) collective-permute-start(bf16[512,256]{1,0:T(8,128)(2,1)S(1)} %get-tuple-element.51), channel_id=1, source_target_pairs={{0,16},{8,24},{16,0},{24,8},{32,48},{40,56},{48,32},{56,40},{64,80... | collective-permute-start | bytes 786440 | tf_op jit(solution)/shard_map/ppermute | solution.py:50
  50.7 16.8 %collective-permute-start.10 = (bf16[512,256]{1,0:T(8,128)(2,1)S(1)}, bf16[512,256]{1,0:T(8,128)(2,1)S(1)}, u32[]{:S(2)}, u32[]{:S(2)}) collective-permute-start(bf16[512,256]{1,0:T(8,128)(2,1)S(1)} %get-tuple-element.43), channel_id=1, source_target_pairs={{0,24},{8,0},{16,8},{24,16},{32,56},{40,32},{48,40},{56,48},{64,88... | collective-permute-start | bytes 786440 | tf_op jit(solution)/shard_map/ppermute | solution.py:50
  52.7 7.3 %collective-permute-start.13 = (bf16[384,256]{1,0:T(8,128)(2,1)S(1)}, bf16[384,256]{1,0:T(8,128)(2,1)S(1)}, u32[]{:S(2)}, u32[]{:S(2)}) collective-permute-start(bf16[384,256]{1,0:T(8,128)(2,1)S(1)} %get-tuple-element.57), channel_id=1, source_target_pairs={{0,192},{8,200},{16,208},{24,216},{32,224},{40,232},{48,240},{56,2... | collective-permute-start | bytes 589832 | tf_op jit(solution)/shard_map/ppermute | solution.py:43
  53.9 9.1 %collective-permute-start.14 = (bf16[384,256]{1,0:T(8,128)(2,1)S(1)}, bf16[384,256]{1,0:T(8,128)(2,1)S(1)}, u32[]{:S(2)}, u32[]{:S(2)}) collective-permute-start(bf16[384,256]{1,0:T(8,128)(2,1)S(1)} %get-tuple-element.58), channel_id=1, source_target_pairs={{0,64},{8,72},{16,80},{24,88},{32,96},{40,104},{48,112},{56,120},{... | collective-permute-start | bytes 589832 | tf_op jit(solution)/shard_map/ppermute | solution.py:43
  55.1 12.8 %collective-permute-start.11 = (bf16[512,256]{1,0:T(8,128)(2,1)S(1)}, bf16[512,256]{1,0:T(8,128)(2,1)S(1)}, u32[]{:S(2)}, u32[]{:S(2)}) collective-permute-start(bf16[512,256]{1,0:T(8,128)(2,1)S(1)} %get-tuple-element.44), channel_id=1, source_target_pairs={{0,8},{8,16},{16,24},{24,0},{32,40},{40,48},{48,56},{56,32},{64,72... | collective-permute-start | bytes 786440 | tf_op jit(solution)/shard_map/ppermute | solution.py:50
  63.0 5.1 %collective-permute-start.15 = (bf16[256,256]{1,0:T(8,128)(2,1)S(1)}, bf16[256,256]{1,0:T(8,128)(2,1)S(1)}, u32[]{:S(2)}, u32[]{:S(2)}) collective-permute-start(bf16[256,256]{1,0:T(8,128)(2,1)S(1)} %get-tuple-element.59), channel_id=1, source_target_pairs={{0,192},{8,200},{16,208},{24,216},{32,224},{40,232},{48,240},{56,2... | collective-permute-start | bytes 393224 | tf_op jit(solution)/shard_map/ppermute | solution.py:43
  63.1 10.9 %collective-permute-start.16 = (bf16[256,256]{1,0:T(8,128)(2,1)S(1)}, bf16[256,256]{1,0:T(8,128)(2,1)S(1)}, u32[]{:S(2)}, u32[]{:S(2)}) collective-permute-start(bf16[256,256]{1,0:T(8,128)(2,1)S(1)} %get-tuple-element.60), channel_id=1, source_target_pairs={{0,64},{8,72},{16,80},{24,88},{32,96},{40,104},{48,112},{56,120},{... | collective-permute-start | bytes 393224 | tf_op jit(solution)/shard_map/ppermute | solution.py:43
  65.5 8.6 %collective-permute-start.17 = (bf16[256,256]{1,0:T(8,128)(2,1)S(1)}, bf16[256,256]{1,0:T(8,128)(2,1)S(1)}, u32[]{:S(2)}, u32[]{:S(2)}) collective-permute-start(bf16[256,256]{1,0:T(8,128)(2,1)S(1)} %get-tuple-element.61), channel_id=1, source_target_pairs={{0,224},{8,232},{16,240},{24,248},{32,0},{40,8},{48,16},{56,24},{6... | collective-permute-start | bytes 393224 | tf_op jit(solution)/shard_map/ppermute | solution.py:43
  67.5 8.7 %collective-permute-start.18 = (bf16[256,256]{1,0:T(8,128)(2,1)S(1)}, bf16[256,256]{1,0:T(8,128)(2,1)S(1)}, u32[]{:S(2)}, u32[]{:S(2)}) collective-permute-start(bf16[256,256]{1,0:T(8,128)(2,1)S(1)} %get-tuple-element.62), channel_id=1, source_target_pairs={{0,32},{8,40},{16,48},{24,56},{32,64},{40,72},{48,80},{56,88},{64,... | collective-permute-start | bytes 393224 | tf_op jit(solution)/shard_map/ppermute | solution.py:43
  77.7 13.2 %collective-permute-start.19 = (bf16[4,512,256]{2,1,0:T(8,128)(2,1)S(1)}, bf16[4,512,256]{2,1,0:T(8,128)(2,1)S(1)}, u32[]{:S(2)}, u32[]{:S(2)}) collective-permute-start(bf16[4,512,256]{2,1,0:T(8,128)(2,1)S(1)} %get-tuple-element.64), channel_id=1, source_target_pairs={{0,1},{1,0},{2,3},{3,2},{4,5},{5,4},{6,7},{7,6},{8,9},{9,8},{10,11... | collective-permute-start | bytes 3145736 | tf_op jit(solution)/shard_map/ppermute | solution.py:62
  91.0 9.1 %collective-permute-start.20 = (bf16[512,256]{1,0:T(8,128)(2,1)S(1)}, bf16[512,256]{1,0:T(8,128)(2,1)S(1)}, u32[]{:S(2)}, u32[]{:S(2)}) collective-permute-start(bf16[512,256]{1,0:T(8,128)(2,1)S(1)} %get-tuple-element.67), channel_id=1, source_target_pairs={{0,4},{1,5},{2,6},{3,7},{4,0},{5,1},{6,2},{7,3},{8,12},{9,13},{10,... | collective-permute-start | bytes 786440 | tf_op jit(solution)/shard_map/ppermute | solution.py:57
  93.9 12.6 %collective-permute-start.21 = (bf16[512,256]{1,0:T(8,128)(2,1)S(1)}, bf16[512,256]{1,0:T(8,128)(2,1)S(1)}, u32[]{:S(2)}, u32[]{:S(2)}) collective-permute-start(bf16[512,256]{1,0:T(8,128)(2,1)S(1)} %get-tuple-element.66), channel_id=1, source_target_pairs={{0,2},{1,3},{2,4},{3,5},{4,6},{5,7},{6,0},{7,1},{8,10},{9,11},{10,... | collective-permute-start | bytes 786440 | tf_op jit(solution)/shard_map/ppermute | solution.py:57
  94.2 12.3 %collective-permute-start.22 = (bf16[512,256]{1,0:T(8,128)(2,1)S(1)}, bf16[512,256]{1,0:T(8,128)(2,1)S(1)}, u32[]{:S(2)}, u32[]{:S(2)}) collective-permute-start(bf16[512,256]{1,0:T(8,128)(2,1)S(1)} %get-tuple-element.65), channel_id=1, source_target_pairs={{0,6},{1,7},{2,0},{3,1},{4,2},{5,3},{6,4},{7,5},{8,14},{9,15},{10,... | collective-permute-start | bytes 786440 | tf_op jit(solution)/shard_map/ppermute | solution.py:57

commit v3 on v2

--- a/solution.py
+++ b/solution.py
@@ -70,7 +70,10 @@
     return high, mid, low
 
 
-def prep_kernel(pos_hbm, q_hbm, do_hbm, o_hbm, lse_hbm, k_hbm, v_hbm, pack_ref, kv_ref, *scratch):
+def prep_kernel(
+    pos_hbm, q_hbm, do_hbm, o_hbm, lse_hbm, k_hbm, v_hbm, pack_ref, kv_ref, mark_ref, *scratch
+):
+    mark_ref[...] = jnp.zeros_like(mark_ref)
     pos_ref, o_ref, lse_ref, sems = scratch
     copies = [
         pltpu.make_async_copy(pos_hbm, pos_ref, sems.at[0]),
@@ -114,9 +117,8 @@
         pack_ref[base + CHUNK : base + PIECE, :] = block.astype(BF)
 
 
-def stage_kernel(pack_ref, kv_ref, pack_out, kv_out):
-    pack_out[...] = pack_ref[...]
-    kv_out[...] = kv_ref[...]
+def pause_kernel(mark_ref, out_ref):
+    del mark_ref, out_ref
 
 
 def attn_kernel(q_sizes, nkv, has_dq, has_dkv, layout, *refs):
@@ -340,7 +342,7 @@
 def send_kernel(*refs):
     dqs = refs[0:4]
     dkvs = refs[4:9]
-    cos_ref, sin_ref, wq_ref, wk_ref, wv_ref, x_out, out_ref = refs[9:]
+    cos_ref, sin_ref, wq_ref, wk_ref, wv_ref, _, x_out, out_ref = refs[9:]
     cosine = cos_ref[...]
     sine = sin_ref[...]
     for head in range(REPEAT):
@@ -382,17 +384,22 @@
 
 
 VM = pl.BlockSpec(memory_space=pltpu.VMEM)
+ANY = pl.BlockSpec(memory_space=pl.ANY)
 HB = pl.BlockSpec(memory_space=pltpu.HBM)
 
 
 def layer(
     query_act, key_act, value_act, attn_out, out_grad, log_sum, positions, w_query, w_key, w_value
 ):
-    pack, kv = pl.pallas_call(
+    pack, kv, mark = pl.pallas_call(
         prep_kernel,
-        out_shape=(whole((2 * PIECE, 1024), BF), whole((ROWS + 16, 256), BF)),
+        out_shape=(
+            whole((2 * PIECE, 1024), BF),
+            whole((ROWS + 16, 256), BF),
+            whole((8, 128), F32),
+        ),
         in_specs=[HB] * 7,
-        out_specs=(VM, VM),
+        out_specs=(VM, VM, VM),
         scratch_shapes=[
             pltpu.SMEM((ROWS,), jnp.int32),
             pltpu.VMEM((ROWS, 512), BF),
@@ -401,6 +408,14 @@
         ],
         compiler_params=pltpu.CompilerParams(vmem_limit_bytes=PREP_LIMIT),
     )(positions, query_act, out_grad, attn_out, log_sum, key_act, value_act)
+
+    mark = pl.pallas_call(
+        pause_kernel,
+        out_shape=whole((8, 128), F32),
+        in_specs=[ANY],
+        out_specs=ANY,
+        cost_estimate=pl.CostEstimate(flops=8_000_000_000, bytes_accessed=8192, transcendentals=0),
+    )(mark)
 
     left = move_y(pack, 1)
     right = move_y(pack, -1)
@@ -411,19 +426,13 @@
     up3 = move_z(up2, 1)
     down3 = move_z(down2, -1)
     up4 = move_z(up2, 2)
-    far = move_y(pack, 2)
-
-    pack, kv = pl.pallas_call(
-        stage_kernel,
-        out_shape=(whole(pack.shape, BF), whole(kv.shape, BF)),
-        in_specs=[VM] * 2,
-        out_specs=(VM, VM),
-        compiler_params=pltpu.CompilerParams(vmem_limit_bytes=8 * MIB),
-    )(pack, kv)
+    far0 = move_y(left[0:PIECE], 1)
+    far1 = move_y(right[PIECE : 2 * PIECE], -1)
+
     near = [kv, up1, down1, up2, down2]
     first = attend([pack, left, right], near, [None] * 3, [None] * 5, [F32] * 3, [F32] * 5)
     outer = attend(
-        [pack, left, right, far],
+        [pack, left, right, far0, far1],
         [up3, down3, up4],
         list(first[0:3]) + [None],
         [None] * 3,
@@ -433,7 +442,7 @@
     )
     back_up = move_z(outer[4], -2)
     back_down = move_z(outer[5], 2)
-    last = attend([far], near, [outer[3]], list(first[3:8]), [BF], [F32] * 5)
+    last = attend([far0, far1], near, [outer[3]], list(first[3:8]), [BF], [F32] * 5)
     dqs = [outer[0], move_y(outer[1], -1), move_y(outer[2], 1), move_y(last[0], 2)]
     merged = pl.pallas_call(
         merge_kernel,
@@ -452,10 +461,10 @@
     grads, to_send = pl.pallas_call(
         send_kernel,
         out_shape=(whole((768, ROWS), BF), whole((NX, 512, ROWS), BF)),
-        in_specs=[VM] * 14,
+        in_specs=[VM] * 14 + [ANY],
         out_specs=(VM, VM),
         compiler_params=pltpu.CompilerParams(vmem_limit_bytes=20 * MIB),
-    )(*dqs, *dkvs, cosine, sine, w_query, w_key, w_value)
+    )(*dqs, *dkvs, cosine, sine, w_query, w_key, w_value, mark)
     got = swap_core(to_send)
     kept = pl.pallas_call(
         keep_kernel,

time: 108 us -> 104 us (0.963)
  waiting for transfers between devices: 30.3 us -> 21.2 us
  local copies, waits for them, and re-layouts: 2.03 us -> 4.9 us
  Pallas kernels: 27.1 us -> 29.4 us
    ppermute x13, waiting for transfers between devices: 19.3 us -> 7.1 us  [move_z(): return lax.ppermute(value, 'seq', pairs)]
    ppermute x13, starting transfers between devices: 23.6 us -> 28.5 us  [move_z(): return lax.ppermute(value, 'seq', pairs)]
    ppermute x1, starting transfers between devices: 10.9 us -> 5.95 us  [swap_core(): return lax.ppermute(value, 'tp', pairs)]
    ppermute x6 -> x7, waiting for transfers between devices: 0.02 us -> 3.13 us  [move_y(): return lax.ppermute(value, 'seq', pairs)]
    unnamed x12 -> x20, local copies, waits for them, and re-layouts: 2.03 us -> 4.86 us
    pallas_call x3, Pallas kernels: 20.4 us -> 21.7 us  [attend(): pl.pallas_call(functools.partial(attn_kernel, sizes, len(kvs), has_dq, ha...]
    ppermute x6 -> x7, starting transfers between devices: 7.26 us -> 7.9 us  [move_y(): return lax.ppermute(value, 'seq', pairs)]
  transfers between devices with their start and end apart: 23 -> 24, of which waited for: 9 -> 9; matrix products, arithmetic and copies ran while one was open for 0% -> 0% of each run, Pallas kernels for 9% -> 14%
where the time goes in v3:
time: 104 us
  starting transfers between devices  47.9 us (46%)
  Pallas kernels  29.4 us (28%)
  waiting for transfers between devices  21.2 us (20%)
  local copies, waits for them, and re-layouts  4.9 us (5%)
    ppermute x13, starting transfers between devices, move_z(): return lax.ppermute(value, 'seq', pairs)  28.5 us
    pallas_call x3, Pallas kernels, attend(): pl.pallas_call(functools.partial(attn_kernel, sizes, len(kvs), has_dq, ha...  21.7 us
    ppermute x3, waiting for transfers between devices, move_x(): return lax.ppermute(value, 'tp', pairs)  9.93 us
    ppermute x7, starting transfers between devices, move_y(): return lax.ppermute(value, 'seq', pairs)  7.9 us
    ppermute x13, waiting for transfers between devices, move_z(): return lax.ppermute(value, 'seq', pairs)  7.1 us
    ppermute x1, starting transfers between devices, swap_core(): return lax.ppermute(value, 'tp', pairs)  5.95 us
    ppermute x3, starting transfers between devices, move_x(): return lax.ppermute(value, 'tp', pairs)  5.51 us
    unnamed x20, local copies, waits for them, and re-layouts  4.86 us
  transfers between devices with their start and end apart: 24, of which 9 were waited for; matrix products, arithmetic and copies ran while one was open for 0% of the time, Pallas kernels for 14%

profile of v3, /device:TPU:1, one launch (start us, length us, event | category | flops | bytes accessed | tf_op | source)
XLA Modules:
  0.0 104.1 jit_solution(7163306753771317786)
XLA Ops:
  0.0 3.1 %shard_map.100 = (bf16[288,1024]{1,0:T(8,128)(2,1)}, bf16[272,256]{1,0:T(8,128)(2,1)}, f32[8,128]{1,0:T(8,128)}) custom-call(s32[256]{0:T(256)} %pos_hbm.1, bf16[256,512]{1,0:T(8,128)(2,1)} %q_hbm.1, bf16[256,512]{1,0:T(8,128)(2,1)} %do_hbm.1, bf16[256,512]{1,0:T(8,128)(2,1)} %o_hbm.1, f32[4,256]{1,0:T(4,128)} %lse_hbm.1, bf16[256,128]{1,0:T(8,128)(2,1)} %k_hbm.1, ...), custom_call_target="tpu_custom_call" | custom-call | tf_op jit(solution)/shard_map/pallas_call | solution.py:394
  3.1 2.2 %collective-permute-start = (bf16[288,1024]{1,0:T(8,128)(2,1)}, bf16[288,1024]{1,0:T(8,128)(2,1)S(1)}, u32[]{:S(2)}, u32[]{:S(2)}) collective-permute-start(bf16[288,1024]{1,0:T(8,128)(2,1)} %get-tuple-element.34.refs_0_), channel_id=1, source_target_pairs={{0,8},{8,16},{16,24},{24,0},{32,40},{40,48},{48,56},{56,32},{64,72... | collective-permute-start | bytes 1769480 | tf_op jit(solution)/shard_map/ppermute | solution.py:50
  5.3 1.5 %collective-permute-start.1 = (bf16[288,1024]{1,0:T(8,128)(2,1)}, bf16[288,1024]{1,0:T(8,128)(2,1)S(1)}, u32[]{:S(2)}, u32[]{:S(2)}) collective-permute-start(bf16[288,1024]{1,0:T(8,128)(2,1)} %get-tuple-element.34.refs_0_), channel_id=1, source_target_pairs={{0,24},{8,0},{16,8},{24,16},{32,56},{40,32},{48,40},{56,48},{64,88... | collective-permute-start | bytes 1769480 | tf_op jit(solution)/shard_map/ppermute | solution.py:50
  6.8 3.0 %collective-permute-start.4 = (bf16[272,256]{1,0:T(8,128)(2,1)}, bf16[272,256]{1,0:T(8,128)(2,1)S(1)}, u32[]{:S(2)}, u32[]{:S(2)}) collective-permute-start(bf16[272,256]{1,0:T(8,128)(2,1)} %get-tuple-element.35.refs_3_.refs_2_), channel_id=1, source_target_pairs={{0,64},{8,72},{16,80},{24,88},{32,96},{40,104},{48,112},{56,120},{... | collective-permute-start | bytes 417800 | tf_op jit(solution)/shard_map/ppermute | solution.py:43
  9.8 3.0 %collective-permute-start.6 = (bf16[272,256]{1,0:T(8,128)(2,1)}, bf16[272,256]{1,0:T(8,128)(2,1)S(1)}, u32[]{:S(2)}, u32[]{:S(2)}) collective-permute-start(bf16[272,256]{1,0:T(8,128)(2,1)} %get-tuple-element.35.refs_3_.refs_2_), channel_id=1, source_target_pairs={{0,192},{8,200},{16,208},{24,216},{32,224},{40,232},{48,240},{56,2... | collective-permute-start | bytes 417800 | tf_op jit(solution)/shard_map/ppermute | solution.py:43
  12.8 1.9 %collective-permute-start.10 = (bf16[272,256]{1,0:T(8,128)(2,1)}, bf16[272,256]{1,0:T(8,128)(2,1)S(1)}, u32[]{:S(2)}, u32[]{:S(2)}) collective-permute-start(bf16[272,256]{1,0:T(8,128)(2,1)} %get-tuple-element.35.refs_3_.refs_2_), channel_id=1, source_target_pairs={{0,224},{8,232},{16,240},{24,248},{32,0},{40,8},{48,16},{56,24},{6... | collective-permute-start | bytes 417800 | tf_op jit(solution)/shard_map/ppermute | solution.py:43
  14.7 1.9 %collective-permute-done.4.refs_6_.refs_5_ = bf16[272,256]{1,0:T(8,128)(2,1)S(1)} collective-permute-done((bf16[272,256]{1,0:T(8,128)(2,1)}, bf16[272,256]{1,0:T(8,128)(2,1)S(1)}, u32[]{:S(2)}, u32[]{:S(2)}) %collective-permute-start.4) | collective-permute-done | bytes 139296 | tf_op jit(solution)/shard_map/ppermute | solution.py:43
  16.6 3.8 %collective-permute-start.9 = (bf16[272,256]{1,0:T(8,128)(2,1)}, bf16[272,256]{1,0:T(8,128)(2,1)S(1)}, u32[]{:S(2)}, u32[]{:S(2)}) collective-permute-start(bf16[272,256]{1,0:T(8,128)(2,1)} %get-tuple-element.35.refs_3_.refs_2_), channel_id=1, source_target_pairs={{0,32},{8,40},{16,48},{24,56},{32,64},{40,72},{48,80},{56,88},{64,... | collective-permute-start | bytes 417800 | tf_op jit(solution)/shard_map/ppermute | solution.py:43
  20.4 0.9 collective-permute-start.5
  21.4 0.0 collective-permute-done.6.refs_7_.refs_6_
  21.4 3.1 %collective-permute-start.8 = (bf16[272,256]{1,0:T(8,128)(2,1)S(1)}, bf16[272,256]{1,0:T(8,128)(2,1)S(1)}, u32[]{:S(2)}, u32[]{:S(2)}) collective-permute-start(bf16[272,256]{1,0:T(8,128)(2,1)S(1)} %collective-permute-done.4.refs_6_.refs_5_), channel_id=1, source_target_pairs={{0,64},{8,72},{16,80},{24,88},{32,96},{40,104},{48,112},{56,120},{... | collective-permute-start | bytes 417800 | tf_op jit(solution)/shard_map/ppermute | solution.py:43
  24.5 1.0 %collective-permute-start.7 = (bf16[272,256]{1,0:T(8,128)(2,1)S(1)}, bf16[272,256]{1,0:T(8,128)(2,1)S(1)}, u32[]{:S(2)}, u32[]{:S(2)}) collective-permute-start(bf16[272,256]{1,0:T(8,128)(2,1)S(1)} %collective-permute-done.6.refs_7_.refs_6_), channel_id=1, source_target_pairs={{0,224},{8,232},{16,240},{24,248},{32,0},{40,8},{48,16},{56,24},{6... | collective-permute-start | bytes 417800 | tf_op jit(solution)/shard_map/ppermute | solution.py:43
  25.5 0.8 collective-permute-start.2
  26.4 1.9 %collective-permute-start.3 = (bf16[144,1024]{1,0:T(8,128)(2,1)S(1)}, bf16[144,1024]{1,0:T(8,128)(2,1)S(1)}, u32[]{:S(2)}, u32[]{:S(2)}) collective-permute-start(bf16[144,1024]{1,0:T(8,128)(2,1)S(1)} %slice.41), channel_id=1, source_target_pairs={{0,24},{8,0},{16,8},{24,16},{32,56},{40,32},{48,40},{56,48},{64,88... | collective-permute-start | bytes 884744 | tf_op jit(solution)/shard_map/ppermute | solution.py:50
  28.3 1.1 %copy-done.5 = bf16[288,1024]{1,0:T(8,128)(2,1)S(1)} copy-done((bf16[288,1024]{1,0:T(8,128)(2,1)S(1)}, bf16[288,1024]{1,0:T(8,128)(2,1)}, u32[]{:S(2)}) %copy-start.5) | copy-done | bytes 589848
  29.4 0.9 copy-done.7
  30.3 7.8 %shard_map.101 = (f32[512,256]{1,0:T(8,128)S(1)}, f32[512,256]{1,0:T(8,128)S(1)}, f32[512,256]{1,0:T(8,128)S(1)}, f32[256,256]{1,0:T(8,128)S(1)}, f32[256,256]{1...) custom-call(bf16[288,1024]{1,0:T(8,128)(2,1)S(1)} %copy-done.5, ...), custom_call_target="tpu_custom_call" | custom-call | flops 5100000256 | bytes 4000000 | tf_op jit(solution)/shard_map/pallas_call | solution.py:294
  38.1 9.4 %shard_map.102 = (f32[512,256]{1,0:T(8,128)S(1)}, bf16[512,256]{1,0:T(8,128)(2,1)}, bf16[512,256]{1,0:T(8,128)(2,1)S(1)}, f32[512,256]{1,0:T(8,128)S(1)}, bf16[3...) custom-call(bf16[288,1024]{1,0:T(8,128)(2,1)S(1)} %copy-done.5, bf16[288,1024]{1,0:T(8,128)(2,1)S(1)} %collective-permute-done.refs_1_, ...), custom_call_target="tpu_custom_call" | custom-call | flops 4080000000 | bytes 4000000 | tf_op jit(solution)/shard_map/pallas_call | solution.py:294
  47.5 3.9 %collective-permute-start.14 = (bf16[384,256]{1,0:T(8,128)(2,1)}, bf16[384,256]{1,0:T(8,128)(2,1)}, u32[]{:S(2)}, u32[]{:S(2)}) collective-permute-start(bf16[384,256]{1,0:T(8,128)(2,1)} %get-tuple-element.54), channel_id=1, source_target_pairs={{0,192},{8,200},{16,208},{24,216},{32,224},{40,232},{48,240},{56,2... | collective-permute-start | bytes 589832 | tf_op jit(solution)/shard_map/ppermute | solution.py:43
  51.5 4.5 %shard_map.103 = (bf16[512,256]{1,0:T(8,128)(2,1)}, f32[256,256]{1,0:T(8,128)S(1)}, f32[256,256]{1,0:T(8,128)S(1)}, f32[256,256]{1,0:T(8,128)S(1)}, f32[256,256]{1,0:T(8,128)S(1)}, /*index=5*/f32[256,256]{1,0:T(8,128)S(1)}) custom-call(bf16[144,1024]{1,0:T(8,128)(2,1)S(1)} %collective-permute-done.2.refs_3_.refs_0_, ...), custom_call_target="tpu_custom_call" | custom-call | flops 1700000000 | bytes 4000000 | tf_op jit(solution)/shard_map/pallas_call | solution.py:294
  56.0 0.0 copy-start.9
  56.0 0.0 copy-start.3
  56.0 0.0 copy-start.2
  56.0 1.4 %collective-permute-start.12 = (bf16[512,256]{1,0:T(8,128)(2,1)}, bf16[512,256]{1,0:T(8,128)(2,1)S(1)}, u32[]{:S(2)}, u32[]{:S(2)}) collective-permute-start(bf16[512,256]{1,0:T(8,128)(2,1)} %copy-done.6), channel_id=1, source_target_pairs={{0,8},{8,16},{16,24},{24,0},{32,40},{40,48},{48,56},{56,32},{64,72... | collective-permute-start | bytes 786440 | tf_op jit(solution)/shard_map/ppermute | solution.py:50
  57.5 1.0 collective-permute-done.15.from_down
  58.4 1.1 %shard_map.104 = (bf16[256,256]{1,0:T(8,128)(2,1)S(1)}, bf16[256,256]{1,0:T(8,128)(2,1)S(1)}, bf16[256,256]{1,0:T(8,128)(2,1)S(1)}, bf16[256,256]{1,0:T(8,128)(2,1)S(1)}) custom-call(f32[256,256]{1,0:T(8,128)S(1)} %get-tuple-element.50.up1, f32[256,256]{1,0:T(8,128)S(1)} %get-tuple-element.51.down1, f32[256,256]{1,0:T(8,128)S(1)} %get-tuple-element.52.up2, ...), custom_call_target="tpu_custom_call" | custom-call | tf_op jit(solution)/shard_map/pallas_call | solution.py:447
  59.5 1.5 %collective-permute-start.16 = (bf16[256,256]{1,0:T(8,128)(2,1)S(1)}, bf16[256,256]{1,0:T(8,128)(2,1)S(1)}, u32[]{:S(2)}, u32[]{:S(2)}) collective-permute-start(bf16[256,256]{1,0:T(8,128)(2,1)S(1)} %get-tuple-element.56), channel_id=1, source_target_pairs={{0,192},{8,200},{16,208},{24,216},{32,224},{40,232},{48,240},{56,2... | collective-permute-start | bytes 393224 | tf_op jit(solution)/shard_map/ppermute | solution.py:43
  61.1 0.9 collective-permute-start.17
  62.0 1.4 %collective-permute-done.13.refs_3_ = bf16[512,256]{1,0:T(8,128)(2,1)S(1)} collective-permute-done((bf16[512,256]{1,0:T(8,128)(2,1)}, bf16[512,256]{1,0:T(8,128)(2,1)S(1)}, u32[]{:S(2)}, u32[]{:S(2)}) %collective-permute-start.13) | collective-permute-done | bytes 262176 | tf_op jit(solution)/shard_map/ppermute | solution.py:50
  63.4 4.9 %collective-permute-start.18 = (bf16[256,256]{1,0:T(8,128)(2,1)S(1)}, bf16[256,256]{1,0:T(8,128)(2,1)S(1)}, u32[]{:S(2)}, u32[]{:S(2)}) collective-permute-start(bf16[256,256]{1,0:T(8,128)(2,1)S(1)} %get-tuple-element.58), channel_id=1, source_target_pairs={{0,224},{8,232},{16,240},{24,248},{32,0},{40,8},{48,16},{56,24},{6... | collective-permute-start | bytes 393224 | tf_op jit(solution)/shard_map/ppermute | solution.py:43
  68.3 0.5 collective-permute-start.19
  68.8 0.3 multiply_sine_fusion
  69.1 1.7 %collective-permute-done.12.refs_2_ = bf16[512,256]{1,0:T(8,128)(2,1)S(1)} collective-permute-done((bf16[512,256]{1,0:T(8,128)(2,1)}, bf16[512,256]{1,0:T(8,128)(2,1)S(1)}, u32[]{:S(2)}, u32[]{:S(2)}) %collective-permute-start.12) | collective-permute-done | bytes 262176 | tf_op jit(solution)/shard_map/ppermute | solution.py:50
  70.8 1.9 %collective-permute-done.18.refs_7_ = bf16[256,256]{1,0:T(8,128)(2,1)S(1)} collective-permute-done((bf16[256,256]{1,0:T(8,128)(2,1)S(1)}, bf16[256,256]{1,0:T(8,128)(2,1)S(1)}, u32[]{:S(2)}, u32[]{:S(2)}) %collective-permute-start.18) | collective-permute-done | bytes 131104 | tf_op jit(solution)/shard_map/ppermute | solution.py:43
  72.7 2.3 %collective-permute-done.19.refs_8_ = bf16[256,256]{1,0:T(8,128)(2,1)S(1)} collective-permute-done((bf16[256,256]{1,0:T(8,128)(2,1)S(1)}, bf16[256,256]{1,0:T(8,128)(2,1)S(1)}, u32[]{:S(2)}, u32[]{:S(2)}) %collective-permute-start.19) | collective-permute-done | bytes 131104 | tf_op jit(solution)/shard_map/ppermute | solution.py:43
  75.1 2.2 %copy-done = bf16[4096,512]{1,0:T(8,128)(2,1)S(1)} copy-done((bf16[4096,512]{1,0:T(8,128)(2,1)S(1)}, bf16[4096,512]{1,0:T(8,128)(2,1)}, u32[]{:S(2)}) %copy-start) | copy-done | bytes 4194328
  77.3 0.7 copy-done.4
  77.9 1.4 %shard_map.106 = (bf16[768,256]{1,0:T(8,128)(2,1)S(1)}, bf16[4,512,256]{2,1,0:T(8,128)(2,1)S(1)}) custom-call(f32[512,256]{1,0:T(8,128)S(1)} %get-tuple-element.39.refs_0_, bf16[512,256]{1,0:T(8,128)(2,1)S(1)} %collective-permute-done.11.refs_1_, bf16[512,256]{1,0:T(8,128)(2,1)S(1)} %collective-permute-done.12.refs_2_, ...), custom_call_target="tpu_custom_call" | custom-call | tf_op jit(solution)/shard_map/pallas_call | solution.py:461
  79.3 6.0 %collective-permute-start.20 = (bf16[4,512,256]{2,1,0:T(8,128)(2,1)S(1)}, bf16[4,512,256]{2,1,0:T(8,128)(2,1)S(1)}, u32[]{:S(2)}, u32[]{:S(2)}) collective-permute-start(bf16[4,512,256]{2,1,0:T(8,128)(2,1)S(1)} %get-tuple-element.62), channel_id=1, source_target_pairs={{0,1},{1,0},{2,3},{3,2},{4,5},{5,4},{6,7},{7,6},{8,9},{9,8},{10,11... | collective-permute-start | bytes 3145736 | tf_op jit(solution)/shard_map/ppermute | solution.py:62
  85.3 1.2 %shard_map.107 = f32[4,512,256]{2,1,0:T(8,128)S(1)} custom-call(bf16[768,256]{1,0:T(8,128)(2,1)S(1)} %get-tuple-element.61.x_ref, bf16[4096,512]{1,0:T(8,128)(2,1)S(1)} %copy-done.1, bf16[4096,128]{1,0:T(8,128)(2,1)S(1)} %copy-done.2, bf16[4096,128]{1,0:T(8,128)(2,1)S(1)} %copy-done.3), custom_call_target="tpu_custom_call" | custom-call | flops 800000000 | bytes 4000000 | tf_op jit(solution)/shard_map/pallas_call | solution.py:469
  86.5 1.0 %collective-permute-done.20 = bf16[4,512,256]{2,1,0:T(8,128)(2,1)S(1)} collective-permute-done((bf16[4,512,256]{2,1,0:T(8,128)(2,1)S(1)}, bf16[4,512,256]{2,1,0:T(8,128)(2,1)S(1)}, u32[]{:S(2)}, u32[]{:S(2)}) %collective-permute-start.20) | collective-permute-done | bytes 1048608 | tf_op jit(solution)/shard_map/ppermute | solution.py:62
  87.6 0.2 fusion.6
  87.8 2.8 %collective-permute-start.21 = (bf16[512,256]{1,0:T(8,128)(2,1)S(1)}, bf16[512,256]{1,0:T(8,128)(2,1)S(1)}, u32[]{:S(2)}, u32[]{:S(2)}) collective-permute-start(bf16[512,256]{1,0:T(8,128)(2,1)S(1)} %get-tuple-element.65), channel_id=1, source_target_pairs={{0,4},{1,5},{2,6},{3,7},{4,0},{5,1},{6,2},{7,3},{8,12},{9,13},{10,... | collective-permute-start | bytes 786440 | tf_op jit(solution)/shard_map/ppermute | solution.py:57
  90.6 0.3 collective-permute-start.22
  90.9 2.4 %collective-permute-start.23 = (bf16[512,256]{1,0:T(8,128)(2,1)S(1)}, bf16[512,256]{1,0:T(8,128)(2,1)S(1)}, u32[]{:S(2)}, u32[]{:S(2)}) collective-permute-start(bf16[512,256]{1,0:T(8,128)(2,1)S(1)} %get-tuple-element.63), channel_id=1, source_target_pairs={{0,6},{1,7},{2,0},{3,1},{4,2},{5,3},{6,4},{7,5},{8,14},{9,15},{10,... | collective-permute-start | bytes 786440 | tf_op jit(solution)/shard_map/ppermute | solution.py:57
  93.3 3.6 %collective-permute-done.21.a_ref = bf16[512,256]{1,0:T(8,128)(2,1)S(1)} collective-permute-done((bf16[512,256]{1,0:T(8,128)(2,1)S(1)}, bf16[512,256]{1,0:T(8,128)(2,1)S(1)}, u32[]{:S(2)}, u32[]{:S(2)}) %collective-permute-start.21) | collective-permute-done | bytes 262176 | tf_op jit(solution)/shard_map/ppermute | solution.py:57
  96.9 6.3 %collective-permute-done.22.b_ref = bf16[512,256]{1,0:T(8,128)(2,1)S(1)} collective-permute-done((bf16[512,256]{1,0:T(8,128)(2,1)S(1)}, bf16[512,256]{1,0:T(8,128)(2,1)S(1)}, u32[]{:S(2)}, u32[]{:S(2)}) %collective-permute-start.22) | collective-permute-done | bytes 262176 | tf_op jit(solution)/shard_map/ppermute | solution.py:57
  103.2 0.9 shard_map.108
  (35 shorter events, 0.1 us)
Async XLA Ops:
  3.1 17.4 %collective-permute-start = (bf16[288,1024]{1,0:T(8,128)(2,1)}, bf16[288,1024]{1,0:T(8,128)(2,1)S(1)}, u32[]{:S(2)}, u32[]{:S(2)}) collective-permute-start(bf16[288,1024]{1,0:T(8,128)(2,1)} %get-tuple-element.34.refs_0_), channel_id=1, source_target_pairs={{0,8},{8,16},{16,24},{24,0},{32,40},{40,48},{48,56},{56,32},{64,72... | collective-permute-start | bytes 1769480 | tf_op jit(solution)/shard_map/ppermute | solution.py:50
  5.3 19.2 %collective-permute-start.1 = (bf16[288,1024]{1,0:T(8,128)(2,1)}, bf16[288,1024]{1,0:T(8,128)(2,1)S(1)}, u32[]{:S(2)}, u32[]{:S(2)}) collective-permute-start(bf16[288,1024]{1,0:T(8,128)(2,1)} %get-tuple-element.34.refs_0_), channel_id=1, source_target_pairs={{0,24},{8,0},{16,8},{24,16},{32,56},{40,32},{48,40},{56,48},{64,88... | collective-permute-start | bytes 1769480 | tf_op jit(solution)/shard_map/ppermute | solution.py:50
  6.8 9.8 %collective-permute-start.4 = (bf16[272,256]{1,0:T(8,128)(2,1)}, bf16[272,256]{1,0:T(8,128)(2,1)S(1)}, u32[]{:S(2)}, u32[]{:S(2)}) collective-permute-start(bf16[272,256]{1,0:T(8,128)(2,1)} %get-tuple-element.35.refs_3_.refs_2_), channel_id=1, source_target_pairs={{0,64},{8,72},{16,80},{24,88},{32,96},{40,104},{48,112},{56,120},{... | collective-permute-start | bytes 417800 | tf_op jit(solution)/shard_map/ppermute | solution.py:43
  9.8 11.6 %collective-permute-start.6 = (bf16[272,256]{1,0:T(8,128)(2,1)}, bf16[272,256]{1,0:T(8,128)(2,1)S(1)}, u32[]{:S(2)}, u32[]{:S(2)}) collective-permute-start(bf16[272,256]{1,0:T(8,128)(2,1)} %get-tuple-element.35.refs_3_.refs_2_), channel_id=1, source_target_pairs={{0,192},{8,200},{16,208},{24,216},{32,224},{40,232},{48,240},{56,2... | collective-permute-start | bytes 417800 | tf_op jit(solution)/shard_map/ppermute | solution.py:43
  12.8 12.7 %collective-permute-start.10 = (bf16[272,256]{1,0:T(8,128)(2,1)}, bf16[272,256]{1,0:T(8,128)(2,1)S(1)}, u32[]{:S(2)}, u32[]{:S(2)}) collective-permute-start(bf16[272,256]{1,0:T(8,128)(2,1)} %get-tuple-element.35.refs_3_.refs_2_), channel_id=1, source_target_pairs={{0,224},{8,232},{16,240},{24,248},{32,0},{40,8},{48,16},{56,24},{6... | collective-permute-start | bytes 417800 | tf_op jit(solution)/shard_map/ppermute | solution.py:43
  16.6 9.8 %collective-permute-start.9 = (bf16[272,256]{1,0:T(8,128)(2,1)}, bf16[272,256]{1,0:T(8,128)(2,1)S(1)}, u32[]{:S(2)}, u32[]{:S(2)}) collective-permute-start(bf16[272,256]{1,0:T(8,128)(2,1)} %get-tuple-element.35.refs_3_.refs_2_), channel_id=1, source_target_pairs={{0,32},{8,40},{16,48},{24,56},{32,64},{40,72},{48,80},{56,88},{64,... | collective-permute-start | bytes 417800 | tf_op jit(solution)/shard_map/ppermute | solution.py:43
  20.4 17.6 %collective-permute-start.5 = (bf16[272,256]{1,0:T(8,128)(2,1)S(1)}, bf16[272,256]{1,0:T(8,128)(2,1)S(1)}, u32[]{:S(2)}, u32[]{:S(2)}) collective-permute-start(bf16[272,256]{1,0:T(8,128)(2,1)S(1)} %collective-permute-done.4.refs_6_.refs_5_), channel_id=1, source_target_pairs={{0,32},{8,40},{16,48},{24,56},{32,64},{40,72},{48,80},{56,88},{64,... | collective-permute-start | bytes 417800 | tf_op jit(solution)/shard_map/ppermute | solution.py:43
  21.4 16.7 %collective-permute-start.8 = (bf16[272,256]{1,0:T(8,128)(2,1)S(1)}, bf16[272,256]{1,0:T(8,128)(2,1)S(1)}, u32[]{:S(2)}, u32[]{:S(2)}) collective-permute-start(bf16[272,256]{1,0:T(8,128)(2,1)S(1)} %collective-permute-done.4.refs_6_.refs_5_), channel_id=1, source_target_pairs={{0,64},{8,72},{16,80},{24,88},{32,96},{40,104},{48,112},{56,120},{... | collective-permute-start | bytes 417800 | tf_op jit(solution)/shard_map/ppermute | solution.py:43
  24.5 13.6 %collective-permute-start.7 = (bf16[272,256]{1,0:T(8,128)(2,1)S(1)}, bf16[272,256]{1,0:T(8,128)(2,1)S(1)}, u32[]{:S(2)}, u32[]{:S(2)}) collective-permute-start(bf16[272,256]{1,0:T(8,128)(2,1)S(1)} %collective-permute-done.6.refs_7_.refs_6_), channel_id=1, source_target_pairs={{0,224},{8,232},{16,240},{24,248},{32,0},{40,8},{48,16},{56,24},{6... | collective-permute-start | bytes 417800 | tf_op jit(solution)/shard_map/ppermute | solution.py:43
  25.5 12.5 %collective-permute-start.2 = (bf16[144,1024]{1,0:T(8,128)(2,1)S(1)}, bf16[144,1024]{1,0:T(8,128)(2,1)S(1)}, u32[]{:S(2)}, u32[]{:S(2)}) collective-permute-start(bf16[144,1024]{1,0:T(8,128)(2,1)S(1)} %slice.40), channel_id=1, source_target_pairs={{0,8},{8,16},{16,24},{24,0},{32,40},{40,48},{48,56},{56,32},{64,72... | collective-permute-start | bytes 884744 | tf_op jit(solution)/shard_map/ppermute | solution.py:50
  26.4 11.7 %collective-permute-start.3 = (bf16[144,1024]{1,0:T(8,128)(2,1)S(1)}, bf16[144,1024]{1,0:T(8,128)(2,1)S(1)}, u32[]{:S(2)}, u32[]{:S(2)}) collective-permute-start(bf16[144,1024]{1,0:T(8,128)(2,1)S(1)} %slice.41), channel_id=1, source_target_pairs={{0,24},{8,0},{16,8},{24,16},{32,56},{40,32},{48,40},{56,48},{64,88... | collective-permute-start | bytes 884744 | tf_op jit(solution)/shard_map/ppermute | solution.py:50
  28.3 1.1 %copy-start.5 = (bf16[288,1024]{1,0:T(8,128)(2,1)S(1)}, bf16[288,1024]{1,0:T(8,128)(2,1)}, u32[]{:S(2)}) copy-start(bf16[288,1024]{1,0:T(8,128)(2,1)} %get-tuple-element.34.refs_0_) | copy-start | bytes 1769476
  29.4 0.9 copy-start.7
  38.1 13.3 %copy-start.8 = (bf16[272,256]{1,0:T(8,128)(2,1)S(1)}, bf16[272,256]{1,0:T(8,128)(2,1)}, u32[]{:S(2)}) copy-start(bf16[272,256]{1,0:T(8,128)(2,1)} %get-tuple-element.35.refs_3_.refs_2_) | copy-start | bytes 417796
  47.5 8.4 %copy-start.6 = (bf16[512,256]{1,0:T(8,128)(2,1)}, bf16[512,256]{1,0:T(8,128)(2,1)S(1)}, u32[]{:S(2)}) copy-start(bf16[512,256]{1,0:T(8,128)(2,1)S(1)} %get-tuple-element.41) | copy-start | bytes 786436
  47.5 9.9 %collective-permute-start.14 = (bf16[384,256]{1,0:T(8,128)(2,1)}, bf16[384,256]{1,0:T(8,128)(2,1)}, u32[]{:S(2)}, u32[]{:S(2)}) collective-permute-start(bf16[384,256]{1,0:T(8,128)(2,1)} %get-tuple-element.54), channel_id=1, source_target_pairs={{0,192},{8,200},{16,208},{24,216},{32,224},{40,232},{48,240},{56,2... | collective-permute-start | bytes 589832 | tf_op jit(solution)/shard_map/ppermute | solution.py:43
  51.4 7.0 %collective-permute-start.15 = (bf16[384,256]{1,0:T(8,128)(2,1)}, bf16[384,256]{1,0:T(8,128)(2,1)}, u32[]{:S(2)}, u32[]{:S(2)}) collective-permute-start(bf16[384,256]{1,0:T(8,128)(2,1)} %get-tuple-element.55), channel_id=1, source_target_pairs={{0,64},{8,72},{16,80},{24,88},{32,96},{40,104},{48,112},{56,120},{... | collective-permute-start | bytes 589832 | tf_op jit(solution)/shard_map/ppermute | solution.py:43
  56.0 7.4 %collective-permute-start.13 = (bf16[512,256]{1,0:T(8,128)(2,1)}, bf16[512,256]{1,0:T(8,128)(2,1)S(1)}, u32[]{:S(2)}, u32[]{:S(2)}) collective-permute-start(bf16[512,256]{1,0:T(8,128)(2,1)} %get-tuple-element.48), channel_id=1, source_target_pairs={{0,16},{8,24},{16,0},{24,8},{32,48},{40,56},{48,32},{56,40},{64,80... | collective-permute-start | bytes 786440 | tf_op jit(solution)/shard_map/ppermute | solution.py:50
  56.0 12.3 %collective-permute-start.11 = (bf16[512,256]{1,0:T(8,128)(2,1)}, bf16[512,256]{1,0:T(8,128)(2,1)S(1)}, u32[]{:S(2)}, u32[]{:S(2)}) collective-permute-start(bf16[512,256]{1,0:T(8,128)(2,1)} %get-tuple-element.40), channel_id=1, source_target_pairs={{0,24},{8,0},{16,8},{24,16},{32,56},{40,32},{48,40},{56,48},{64,88... | collective-permute-start | bytes 786440 | tf_op jit(solution)/shard_map/ppermute | solution.py:50
  56.0 1.5 %copy-start.9 = (s32[256]{0:T(256)S(1)}, s32[256]{0:T(256)}, u32[]{:S(2)}) copy-start(s32[256]{0:T(256)} %pos_hbm.1) | copy-start | bytes 3076
  56.0 19.1 %copy-start.3 = (bf16[4096,128]{1,0:T(8,128)(2,1)S(1)}, bf16[4096,128]{1,0:T(8,128)(2,1)}, u32[]{:S(2)}) copy-start(bf16[4096,128]{1,0:T(8,128)(2,1)} %wv_ref.1) | copy-start | bytes 3145732
  56.0 19.1 %copy-start.2 = (bf16[4096,128]{1,0:T(8,128)(2,1)S(1)}, bf16[4096,128]{1,0:T(8,128)(2,1)}, u32[]{:S(2)}) copy-start(bf16[4096,128]{1,0:T(8,128)(2,1)} %wk_ref.1) | copy-start | bytes 3145732
  56.0 14.8 %collective-permute-start.12 = (bf16[512,256]{1,0:T(8,128)(2,1)}, bf16[512,256]{1,0:T(8,128)(2,1)S(1)}, u32[]{:S(2)}, u32[]{:S(2)}) collective-permute-start(bf16[512,256]{1,0:T(8,128)(2,1)} %copy-done.6), channel_id=1, source_target_pairs={{0,8},{8,16},{16,24},{24,0},{32,40},{40,48},{48,56},{56,32},{64,72... | collective-permute-start | bytes 786440 | tf_op jit(solution)/shard_map/ppermute | solution.py:50
  59.5 11.3 %collective-permute-start.16 = (bf16[256,256]{1,0:T(8,128)(2,1)S(1)}, bf16[256,256]{1,0:T(8,128)(2,1)S(1)}, u32[]{:S(2)}, u32[]{:S(2)}) collective-permute-start(bf16[256,256]{1,0:T(8,128)(2,1)S(1)} %get-tuple-element.56), channel_id=1, source_target_pairs={{0,192},{8,200},{16,208},{24,216},{32,224},{40,232},{48,240},{56,2... | collective-permute-start | bytes 393224 | tf_op jit(solution)/shard_map/ppermute | solution.py:43
  61.1 9.8 %collective-permute-start.17 = (bf16[256,256]{1,0:T(8,128)(2,1)S(1)}, bf16[256,256]{1,0:T(8,128)(2,1)S(1)}, u32[]{:S(2)}, u32[]{:S(2)}) collective-permute-start(bf16[256,256]{1,0:T(8,128)(2,1)S(1)} %get-tuple-element.57), channel_id=1, source_target_pairs={{0,64},{8,72},{16,80},{24,88},{32,96},{40,104},{48,112},{56,120},{... | collective-permute-start | bytes 393224 | tf_op jit(solution)/shard_map/ppermute | solution.py:43
  63.4 9.4 %collective-permute-start.18 = (bf16[256,256]{1,0:T(8,128)(2,1)S(1)}, bf16[256,256]{1,0:T(8,128)(2,1)S(1)}, u32[]{:S(2)}, u32[]{:S(2)}) collective-permute-start(bf16[256,256]{1,0:T(8,128)(2,1)S(1)} %get-tuple-element.58), channel_id=1, source_target_pairs={{0,224},{8,232},{16,240},{24,248},{32,0},{40,8},{48,16},{56,24},{6... | collective-permute-start | bytes 393224 | tf_op jit(solution)/shard_map/ppermute | solution.py:43
  68.3 6.8 %collective-permute-start.19 = (bf16[256,256]{1,0:T(8,128)(2,1)S(1)}, bf16[256,256]{1,0:T(8,128)(2,1)S(1)}, u32[]{:S(2)}, u32[]{:S(2)}) collective-permute-start(bf16[256,256]{1,0:T(8,128)(2,1)S(1)} %get-tuple-element.59), channel_id=1, source_target_pairs={{0,32},{8,40},{16,48},{24,56},{32,64},{40,72},{48,80},{56,88},{64,... | collective-permute-start | bytes 393224 | tf_op jit(solution)/shard_map/ppermute | solution.py:43
  75.1 2.2 %copy-start = (bf16[4096,512]{1,0:T(8,128)(2,1)S(1)}, bf16[4096,512]{1,0:T(8,128)(2,1)}, u32[]{:S(2)}) copy-start(bf16[4096,512]{1,0:T(8,128)(2,1)} %wq_ref.1) | copy-start | bytes 12582916
  77.3 0.7 copy-start.4
  77.9 7.3 %copy-start.1 = (bf16[4096,512]{1,0:T(8,128)(2,1)S(1)}, bf16[4096,512]{1,0:T(8,128)(2,1)}, u32[]{:S(2)}) copy-start(bf16[4096,512]{1,0:T(8,128)(2,1)} %wq_ref.1) | copy-start | bytes 12582916
  79.3 8.2 %collective-permute-start.20 = (bf16[4,512,256]{2,1,0:T(8,128)(2,1)S(1)}, bf16[4,512,256]{2,1,0:T(8,128)(2,1)S(1)}, u32[]{:S(2)}, u32[]{:S(2)}) collective-permute-start(bf16[4,512,256]{2,1,0:T(8,128)(2,1)S(1)} %get-tuple-element.62), channel_id=1, source_target_pairs={{0,1},{1,0},{2,3},{3,2},{4,5},{5,4},{6,7},{7,6},{8,9},{9,8},{10,11... | collective-permute-start | bytes 3145736 | tf_op jit(solution)/shard_map/ppermute | solution.py:62
  87.8 9.1 %collective-permute-start.21 = (bf16[512,256]{1,0:T(8,128)(2,1)S(1)}, bf16[512,256]{1,0:T(8,128)(2,1)S(1)}, u32[]{:S(2)}, u32[]{:S(2)}) collective-permute-start(bf16[512,256]{1,0:T(8,128)(2,1)S(1)} %get-tuple-element.65), channel_id=1, source_target_pairs={{0,4},{1,5},{2,6},{3,7},{4,0},{5,1},{6,2},{7,3},{8,12},{9,13},{10,... | collective-permute-start | bytes 786440 | tf_op jit(solution)/shard_map/ppermute | solution.py:57
  90.6 12.6 %collective-permute-start.22 = (bf16[512,256]{1,0:T(8,128)(2,1)S(1)}, bf16[512,256]{1,0:T(8,128)(2,1)S(1)}, u32[]{:S(2)}, u32[]{:S(2)}) collective-permute-start(bf16[512,256]{1,0:T(8,128)(2,1)S(1)} %get-tuple-element.64), channel_id=1, source_target_pairs={{0,2},{1,3},{2,4},{3,5},{4,6},{5,7},{6,0},{7,1},{8,10},{9,11},{10,... | collective-permute-start | bytes 786440 | tf_op jit(solution)/shard_map/ppermute | solution.py:57
  90.9 12.3 %collective-permute-start.23 = (bf16[512,256]{1,0:T(8,128)(2,1)S(1)}, bf16[512,256]{1,0:T(8,128)(2,1)S(1)}, u32[]{:S(2)}, u32[]{:S(2)}) collective-permute-start(bf16[512,256]{1,0:T(8,128)(2,1)S(1)} %get-tuple-element.63), channel_id=1, source_target_pairs={{0,6},{1,7},{2,0},{3,1},{4,2},{5,3},{6,4},{7,5},{8,14},{9,15},{10,... | collective-permute-start | bytes 786440 | tf_op jit(solution)/shard_map/ppermute | solution.py:57

commit v4 on v3

--- a/solution.py
+++ b/solution.py
@@ -326,23 +326,16 @@
     )
 
 
-def project(x, weights, i, other):
+def block_rows(i):
     tp = lax.axis_index("tp")
     core = tp % NC
-    block = NC * lax.rem(tp // NC + i, NX) + (1 - core if other else core)
-    rows = pl.ds(pl.multiple_of(block * 512, 512), 512)
-    w_query, w_key, w_value = (ref[rows, :] for ref in weights)
-    return (
-        dot(w_query, x[0:512, :], NN)
-        + dot(w_key, x[512:640, :], NN)
-        + dot(w_value, x[640:768, :], NN)
-    )
-
-
-def send_kernel(*refs):
+    block = NC * lax.rem(tp // NC + i % NX, NX) + (1 - core if i < NX else core)
+    return pl.ds(pl.multiple_of(block * 512, 512), 512)
+
+
+def query_kernel(*refs):
     dqs = refs[0:4]
-    dkvs = refs[4:9]
-    cos_ref, sin_ref, wq_ref, wk_ref, wv_ref, _, x_out, out_ref = refs[9:]
+    cos_ref, sin_ref, wq_ref, out_ref, x_ref = refs[4:]
     cosine = cos_ref[...]
     sine = sin_ref[...]
     for head in range(REPEAT):
@@ -350,19 +343,35 @@
         total = dqs[0][rows, :]
         for ref in dqs[1:]:
             total = total + ref[rows, :].astype(F32)
-        x_out[rows, :] = rotate(total, cosine, sine).astype(BF)
+        x_ref[rows, :] = rotate(total, cosine, sine).astype(BF)
+    for i in range(2 * NX):
+        out_ref[i] = dot(wq_ref[block_rows(i), :], x_ref[...], NN)
+
+
+def add_terms(part_ref, x_ref, wk_ref, wv_ref, i):
+    rows = block_rows(i)
+    return (
+        part_ref[i]
+        + dot(wk_ref[rows, :], x_ref[0:128, :], NN)
+        + dot(wv_ref[rows, :], x_ref[128:256, :], NN)
+    )
+
+
+def send_kernel(*refs):
+    dkvs = refs[0:5]
+    cos_ref, sin_ref, part_ref, wk_ref, wv_ref, _, x_out, out_ref = refs[5:]
     total = dkvs[0][...]
     for ref in dkvs[1:]:
         total = total + ref[...].astype(F32)
-    x_out[512:640, :] = rotate(total[:, 0:128].T, cosine, sine).astype(BF)
-    x_out[640:768, :] = total[:, 128:256].T.astype(BF)
+    x_out[0:128, :] = rotate(total[:, 0:128].T, cos_ref[...], sin_ref[...]).astype(BF)
+    x_out[128:256, :] = total[:, 128:256].T.astype(BF)
     for i in range(NX):
-        out_ref[i] = project(x_out, (wq_ref, wk_ref, wv_ref), i, True).astype(BF)
-
-
-def keep_kernel(x_ref, wq_ref, wk_ref, wv_ref, out_ref):
+        out_ref[i] = add_terms(part_ref, x_out, wk_ref, wv_ref, i).astype(BF)
+
+
+def keep_kernel(x_ref, part_ref, wk_ref, wv_ref, out_ref):
     for i in range(NX):
-        out_ref[i] = project(x_ref, (wq_ref, wk_ref, wv_ref), i, False)
+        out_ref[i] = add_terms(part_ref, x_ref, wk_ref, wv_ref, NX + i)
 
 
 def merge_kernel(up1, down1, up2, down2, from_up, from_down, *outs):
@@ -458,13 +467,24 @@
     cosine = jnp.cos(angles)
     sine = jnp.sin(angles)
 
+    part = pl.pallas_call(
+        query_kernel,
+        out_shape=whole((2 * NX, 512, ROWS), F32),
+        in_specs=[VM] * 7,
+        out_specs=VM,
+        scratch_shapes=[pltpu.VMEM((512, ROWS), BF)],
+        compiler_params=pltpu.CompilerParams(vmem_limit_bytes=20 * MIB),
+        cost_estimate=pl.CostEstimate(
+            flops=1_100_000_000, bytes_accessed=8_000_000, transcendentals=0
+        ),
+    )(*dqs, cosine, sine, w_query)
     grads, to_send = pl.pallas_call(
         send_kernel,
-        out_shape=(whole((768, ROWS), BF), whole((NX, 512, ROWS), BF)),
-        in_specs=[VM] * 14 + [ANY],
+        out_shape=(whole((256, ROWS), BF), whole((NX, 512, ROWS), BF)),
+        in_specs=[VM] * 10 + [ANY],
         out_specs=(VM, VM),
         compiler_params=pltpu.CompilerParams(vmem_limit_bytes=20 * MIB),
-    )(*dqs, *dkvs, cosine, sine, w_query, w_key, w_value, mark)
+    )(*dkvs, cosine, sine, part, w_key, w_value, mark)
     got = swap_core(to_send)
     kept = pl.pallas_call(
         keep_kernel,
@@ -475,7 +495,7 @@
         cost_estimate=pl.CostEstimate(
             flops=800_000_000, bytes_accessed=4_000_000, transcendentals=0
         ),
-    )(grads, w_query, w_key, w_value)
+    )(grads, part, w_key, w_value)
     parts = [kept[i] + got[i].astype(F32) for i in range(4)]
     came = [move_x(parts[i].astype(BF), i) for i in (2, 1, 3)]
     return pl.pallas_call(

time: 104 us -> 102 us (0.981)
  the two profiles are of different devices: /device:TPU:1 before, /device:TPU:8 now
where the time goes in v4:
time: 102 us; the launch traced here: 100 us
  starting transfers between devices  39.2 us (38%)
  waiting for transfers between devices  28.9 us (28%)
  Pallas kernels  27.1 us (27%)
  local copies, waits for them, and re-layouts  4.21 us (4%)
    ppermute x13, starting transfers between devices, move_z(): return lax.ppermute(value, 'seq', pairs)  23.6 us
    pallas_call x3, Pallas kernels, attend(): pl.pallas_call(functools.partial(attn_kernel, sizes, len(kvs), has_dq, ha...  20.3 us
    ppermute x13, waiting for transfers between devices, move_z(): return lax.ppermute(value, 'seq', pairs)  17.6 us
    ppermute x3, waiting for transfers between devices, move_x(): return lax.ppermute(value, 'tp', pairs)  9.32 us
    ppermute x7, starting transfers between devices, move_y(): return lax.ppermute(value, 'seq', pairs)  9.19 us
    ppermute x3, starting transfers between devices, move_x(): return lax.ppermute(value, 'tp', pairs)  6.36 us
    unnamed x16, local copies, waits for them, and re-layouts  4.17 us
    pallas_call x1, Pallas kernels, layer(): pl.pallas_call(prep_kernel, out_shape=(whole((2 * PIECE, 1024), BF), whol...  3.04 us
  transfers between devices with their start and end apart: 24, of which 8 were waited for; matrix products, arithmetic and copies ran while one was open for 0% of the time, Pallas kernels for 11%

profile of v4, /device:TPU:8, one launch (start us, length us, event | category | flops | bytes accessed | tf_op | source)
XLA Modules:
  0.0 100.2 jit_solution(6304857622272528846)
XLA Ops:
  0.0 3.0 %shard_map.100 = (bf16[288,1024]{1,0:T(8,128)(2,1)}, bf16[272,256]{1,0:T(8,128)(2,1)}, f32[8,128]{1,0:T(8,128)}) custom-call(s32[256]{0:T(256)} %pos_hbm.1, bf16[256,512]{1,0:T(8,128)(2,1)} %q_hbm.1, bf16[256,512]{1,0:T(8,128)(2,1)} %do_hbm.1, bf16[256,512]{1,0:T(8,128)(2,1)} %o_hbm.1, f32[4,256]{1,0:T(4,128)} %lse_hbm.1, bf16[256,128]{1,0:T(8,128)(2,1)} %k_hbm.1, ...), custom_call_target="tpu_custom_call" | custom-call | tf_op jit(solution)/shard_map/pallas_call | solution.py:403
  3.0 1.7 %collective-permute-start = (bf16[288,1024]{1,0:T(8,128)(2,1)}, bf16[288,1024]{1,0:T(8,128)(2,1)S(1)}, u32[]{:S(2)}, u32[]{:S(2)}) collective-permute-start(bf16[288,1024]{1,0:T(8,128)(2,1)} %get-tuple-element.34.refs_0_), channel_id=1, source_target_pairs={{0,8},{8,16},{16,24},{24,0},{32,40},{40,48},{48,56},{56,32},{64,72... | collective-permute-start | bytes 1769480 | tf_op jit(solution)/shard_map/ppermute | solution.py:50
  4.7 0.7 collective-permute-start.2
  5.4 3.0 %collective-permute-start.6 = (bf16[272,256]{1,0:T(8,128)(2,1)}, bf16[272,256]{1,0:T(8,128)(2,1)S(1)}, u32[]{:S(2)}, u32[]{:S(2)}) collective-permute-start(bf16[272,256]{1,0:T(8,128)(2,1)} %get-tuple-element.35.refs_3_.refs_2_), channel_id=1, source_target_pairs={{0,64},{8,72},{16,80},{24,88},{32,96},{40,104},{48,112},{56,120},{... | collective-permute-start | bytes 417800 | tf_op jit(solution)/shard_map/ppermute | solution.py:43
  8.4 3.0 %collective-permute-start.7 = (bf16[272,256]{1,0:T(8,128)(2,1)}, bf16[272,256]{1,0:T(8,128)(2,1)S(1)}, u32[]{:S(2)}, u32[]{:S(2)}) collective-permute-start(bf16[272,256]{1,0:T(8,128)(2,1)} %get-tuple-element.35.refs_3_.refs_2_), channel_id=1, source_target_pairs={{0,192},{8,200},{16,208},{24,216},{32,224},{40,232},{48,240},{56,2... | collective-permute-start | bytes 417800 | tf_op jit(solution)/shard_map/ppermute | solution.py:43
  11.5 1.0 %collective-permute-start.4 = (bf16[272,256]{1,0:T(8,128)(2,1)}, bf16[272,256]{1,0:T(8,128)(2,1)S(1)}, u32[]{:S(2)}, u32[]{:S(2)}) collective-permute-start(bf16[272,256]{1,0:T(8,128)(2,1)} %get-tuple-element.35.refs_3_.refs_2_), channel_id=1, source_target_pairs={{0,32},{8,40},{16,48},{24,56},{32,64},{40,72},{48,80},{56,88},{64,... | collective-permute-start | bytes 417800 | tf_op jit(solution)/shard_map/ppermute | solution.py:43
  12.5 4.5 %collective-permute-done.6.refs_6_.refs_5_ = bf16[272,256]{1,0:T(8,128)(2,1)S(1)} collective-permute-done((bf16[272,256]{1,0:T(8,128)(2,1)}, bf16[272,256]{1,0:T(8,128)(2,1)S(1)}, u32[]{:S(2)}, u32[]{:S(2)}) %collective-permute-start.6) | collective-permute-done | bytes 139296 | tf_op jit(solution)/shard_map/ppermute | solution.py:43
  17.0 3.0 %collective-permute-start.5 = (bf16[272,256]{1,0:T(8,128)(2,1)}, bf16[272,256]{1,0:T(8,128)(2,1)S(1)}, u32[]{:S(2)}, u32[]{:S(2)}) collective-permute-start(bf16[272,256]{1,0:T(8,128)(2,1)} %get-tuple-element.35.refs_3_.refs_2_), channel_id=1, source_target_pairs={{0,224},{8,232},{16,240},{24,248},{32,0},{40,8},{48,16},{56,24},{6... | collective-permute-start | bytes 417800 | tf_op jit(solution)/shard_map/ppermute | solution.py:43
  20.0 0.0 collective-permute-done.refs_1_
  20.0 1.7 %collective-permute-start.10 = (bf16[272,256]{1,0:T(8,128)(2,1)S(1)}, bf16[272,256]{1,0:T(8,128)(2,1)S(1)}, u32[]{:S(2)}, u32[]{:S(2)}) collective-permute-start(bf16[272,256]{1,0:T(8,128)(2,1)S(1)} %collective-permute-done.6.refs_6_.refs_5_), channel_id=1, source_target_pairs={{0,64},{8,72},{16,80},{24,88},{32,96},{40,104},{48,112},{56,120},{... | collective-permute-start | bytes 417800 | tf_op jit(solution)/shard_map/ppermute | solution.py:43
  21.7 2.0 %collective-permute-start.8 = (bf16[272,256]{1,0:T(8,128)(2,1)S(1)}, bf16[272,256]{1,0:T(8,128)(2,1)S(1)}, u32[]{:S(2)}, u32[]{:S(2)}) collective-permute-start(bf16[272,256]{1,0:T(8,128)(2,1)S(1)} %collective-permute-done.6.refs_6_.refs_5_), channel_id=1, source_target_pairs={{0,32},{8,40},{16,48},{24,56},{32,64},{40,72},{48,80},{56,88},{64,... | collective-permute-start | bytes 417800 | tf_op jit(solution)/shard_map/ppermute | solution.py:43
  23.7 1.8 %collective-permute-start.9 = (bf16[272,256]{1,0:T(8,128)(2,1)S(1)}, bf16[272,256]{1,0:T(8,128)(2,1)S(1)}, u32[]{:S(2)}, u32[]{:S(2)}) collective-permute-start(bf16[272,256]{1,0:T(8,128)(2,1)S(1)} %collective-permute-done.7.refs_7_.refs_6_), channel_id=1, source_target_pairs={{0,224},{8,232},{16,240},{24,248},{32,0},{40,8},{48,16},{56,24},{6... | collective-permute-start | bytes 417800 | tf_op jit(solution)/shard_map/ppermute | solution.py:43
  25.6 1.4 %collective-permute-start.1 = (bf16[144,1024]{1,0:T(8,128)(2,1)S(1)}, bf16[144,1024]{1,0:T(8,128)(2,1)S(1)}, u32[]{:S(2)}, u32[]{:S(2)}) collective-permute-start(bf16[144,1024]{1,0:T(8,128)(2,1)S(1)} %slice.40), channel_id=1, source_target_pairs={{0,8},{8,16},{16,24},{24,0},{32,40},{40,48},{48,56},{56,32},{64,72... | collective-permute-start | bytes 884744 | tf_op jit(solution)/shard_map/ppermute | solution.py:50
  27.0 0.7 collective-permute-start.3
  27.7 1.1 %copy-done.4 = bf16[288,1024]{1,0:T(8,128)(2,1)S(1)} copy-done((bf16[288,1024]{1,0:T(8,128)(2,1)S(1)}, bf16[288,1024]{1,0:T(8,128)(2,1)}, u32[]{:S(2)}) %copy-start.4) | copy-done | bytes 589848
  28.8 0.9 copy-done.5
  29.7 9.4 %shard_map.101 = (f32[512,256]{1,0:T(8,128)S(1)}, f32[512,256]{1,0:T(8,128)S(1)}, f32[512,256]{1,0:T(8,128)S(1)}, f32[256,256]{1,0:T(8,128)S(1)}, f32[256,256]{1...) custom-call(bf16[288,1024]{1,0:T(8,128)(2,1)S(1)} %copy-done.4, ...), custom_call_target="tpu_custom_call" | custom-call | flops 5100000256 | bytes 4000000 | tf_op jit(solution)/shard_map/pallas_call | solution.py:294
  39.1 7.8 %shard_map.102 = (f32[512,256]{1,0:T(8,128)S(1)}, bf16[512,256]{1,0:T(8,128)(2,1)S(1)}, bf16[512,256]{1,0:T(8,128)(2,1)S(1)}, f32[512,256]{1,0:T(8,128)S(1)}, bf...) custom-call(bf16[288,1024]{1,0:T(8,128)(2,1)S(1)} %copy-done.4, bf16[288,1024]{1,0:T(8,128)(2,1)S(1)} %collective-permute-done.refs_1_, ...), custom_call_target="tpu_custom_call" | custom-call | flops 4080000000 | bytes 4000000 | tf_op jit(solution)/shard_map/pallas_call | solution.py:294
  46.9 3.1 %shard_map.103 = (bf16[512,256]{1,0:T(8,128)(2,1)S(1)}, f32[256,256]{1,0:T(8,128)S(1)}, f32[256,256]{1,0:T(8,128)S(1)}, f32[256,256]{1,0:T(8,128)S(1)}, f32[256,256]{1,0:T(8,128)S(1)}, /*index=5*/f32[256,256]{1,0:T(8,128)S(1)}) custom-call(bf16[144,1024]{1,0:T(8,128)(2,1)S(1)} %collective-permute-done.1.refs_3_.refs_0_, ...), custom_call_target="tpu_custom_call" | custom-call | flops 1700000000 | bytes 4000000 | tf_op jit(solution)/shard_map/pallas_call | solution.py:294
  50.0 1.6 %collective-permute-start.19 = (bf16[512,256]{1,0:T(8,128)(2,1)S(1)}, bf16[512,256]{1,0:T(8,128)(2,1)S(1)}, u32[]{:S(2)}, u32[]{:S(2)}) collective-permute-start(bf16[512,256]{1,0:T(8,128)(2,1)S(1)} %get-tuple-element.59), channel_id=1, source_target_pairs={{0,16},{8,24},{16,0},{24,8},{32,48},{40,56},{48,32},{56,40},{64,80... | collective-permute-start | bytes 786440 | tf_op jit(solution)/shard_map/ppermute | solution.py:50
  51.6 1.8 %collective-permute-start.17 = (bf16[512,256]{1,0:T(8,128)(2,1)S(1)}, bf16[512,256]{1,0:T(8,128)(2,1)S(1)}, u32[]{:S(2)}, u32[]{:S(2)}) collective-permute-start(bf16[512,256]{1,0:T(8,128)(2,1)S(1)} %get-tuple-element.57), channel_id=1, source_target_pairs={{0,24},{8,0},{16,8},{24,16},{32,56},{40,32},{48,40},{56,48},{64,88... | collective-permute-start | bytes 786440 | tf_op jit(solution)/shard_map/ppermute | solution.py:50
  53.4 2.4 %collective-permute-start.11 = (bf16[384,256]{1,0:T(8,128)(2,1)}, bf16[384,256]{1,0:T(8,128)(2,1)S(1)}, u32[]{:S(2)}, u32[]{:S(2)}) collective-permute-start(bf16[384,256]{1,0:T(8,128)(2,1)} %get-tuple-element.50), channel_id=1, source_target_pairs={{0,192},{8,200},{16,208},{24,216},{32,224},{40,232},{48,240},{56,2... | collective-permute-start | bytes 589832 | tf_op jit(solution)/shard_map/ppermute | solution.py:43
  55.8 0.5 collective-permute-start.12
  56.3 1.4 %collective-permute-start.18 = (bf16[512,256]{1,0:T(8,128)(2,1)S(1)}, bf16[512,256]{1,0:T(8,128)(2,1)S(1)}, u32[]{:S(2)}, u32[]{:S(2)}) collective-permute-start(bf16[512,256]{1,0:T(8,128)(2,1)S(1)} %get-tuple-element.58), channel_id=1, source_target_pairs={{0,8},{8,16},{16,24},{24,0},{32,40},{40,48},{48,56},{56,32},{64,72... | collective-permute-start | bytes 786440 | tf_op jit(solution)/shard_map/ppermute | solution.py:50
  57.7 4.7 %collective-permute-done.11.from_up = bf16[384,256]{1,0:T(8,128)(2,1)S(1)} collective-permute-done((bf16[384,256]{1,0:T(8,128)(2,1)}, bf16[384,256]{1,0:T(8,128)(2,1)S(1)}, u32[]{:S(2)}, u32[]{:S(2)}) %collective-permute-start.11) | collective-permute-done | bytes 196640 | tf_op jit(solution)/shard_map/ppermute | solution.py:43
  62.4 6.1 %collective-permute-done.12.from_down = bf16[384,256]{1,0:T(8,128)(2,1)S(1)} collective-permute-done((bf16[384,256]{1,0:T(8,128)(2,1)}, bf16[384,256]{1,0:T(8,128)(2,1)S(1)}, u32[]{:S(2)}, u32[]{:S(2)}) %collective-permute-start.12) | collective-permute-done | bytes 196640 | tf_op jit(solution)/shard_map/ppermute | solution.py:43
  68.5 0.1 shard_map.104
  68.6 0.1 collective-permute-start.13
  68.7 2.9 %collective-permute-start.14 = (bf16[256,256]{1,0:T(8,128)(2,1)S(1)}, bf16[256,256]{1,0:T(8,128)(2,1)S(1)}, u32[]{:S(2)}, u32[]{:S(2)}) collective-permute-start(bf16[256,256]{1,0:T(8,128)(2,1)S(1)} %get-tuple-element.53), channel_id=1, source_target_pairs={{0,64},{8,72},{16,80},{24,88},{32,96},{40,104},{48,112},{56,120},{... | collective-permute-start | bytes 393224 | tf_op jit(solution)/shard_map/ppermute | solution.py:43
  71.6 2.0 %collective-permute-start.15 = (bf16[256,256]{1,0:T(8,128)(2,1)S(1)}, bf16[256,256]{1,0:T(8,128)(2,1)S(1)}, u32[]{:S(2)}, u32[]{:S(2)}) collective-permute-start(bf16[256,256]{1,0:T(8,128)(2,1)S(1)} %get-tuple-element.54), channel_id=1, source_target_pairs={{0,224},{8,232},{16,240},{24,248},{32,0},{40,8},{48,16},{56,24},{6... | collective-permute-start | bytes 393224 | tf_op jit(solution)/shard_map/ppermute | solution.py:43
  73.6 0.0 collective-permute-start.16
  73.6 0.3 multiply_sine_fusion
  73.9 0.0 copy-start
  74.0 2.2 %copy-done = bf16[4096,512]{1,0:T(8,128)(2,1)S(1)} copy-done((bf16[4096,512]{1,0:T(8,128)(2,1)S(1)}, bf16[4096,512]{1,0:T(8,128)(2,1)}, u32[]{:S(2)}) %copy-start) | copy-done | bytes 4194328
  76.1 1.3 %shard_map.105.refs_7_.part_ref = f32[8,512,256]{2,1,0:T(8,128)S(1)} custom-call(f32[512,256]{1,0:T(8,128)S(1)} %get-tuple-element.56.refs_0_, bf16[512,256]{1,0:T(8,128)(2,1)S(1)} %collective-permute-done.17.refs_1_, bf16[512,256]{1,0:T(8,128)(2,1)S(1)} %collective-permute-done.18.refs_2_, bf16[512,256]{1,0:T(8,128)(2,1)S(1)} %collective-permute-done.19.refs_3_, ...), custom_call_target="tpu_custom_call" | custom-call | flops 1100000000 | bytes 8000000 | tf_op jit(solution)/shard_map/pallas_call | solution.py:470
  77.5 2.3 %collective-permute-done.16.refs_4_ = bf16[256,256]{1,0:T(8,128)(2,1)S(1)} collective-permute-done((bf16[256,256]{1,0:T(8,128)(2,1)S(1)}, bf16[256,256]{1,0:T(8,128)(2,1)S(1)}, u32[]{:S(2)}, u32[]{:S(2)}) %collective-permute-start.16) | collective-permute-done | bytes 131104 | tf_op jit(solution)/shard_map/ppermute | solution.py:43
  79.8 0.8 shard_map.107
  80.6 0.1 collective-permute-start.20
  80.7 0.7 shard_map.108
  81.4 1.9 %collective-permute-done.20 = bf16[4,512,256]{2,1,0:T(8,128)(2,1)S(1)} collective-permute-done((bf16[4,512,256]{2,1,0:T(8,128)(2,1)S(1)}, bf16[4,512,256]{2,1,0:T(8,128)(2,1)S(1)}, u32[]{:S(2)}, u32[]{:S(2)}) %collective-permute-start.20) | collective-permute-done | bytes 1048608 | tf_op jit(solution)/shard_map/ppermute | solution.py:62
  83.4 0.2 fusion.6
  83.6 3.1 %collective-permute-start.21 = (bf16[512,256]{1,0:T(8,128)(2,1)S(1)}, bf16[512,256]{1,0:T(8,128)(2,1)S(1)}, u32[]{:S(2)}, u32[]{:S(2)}) collective-permute-start(bf16[512,256]{1,0:T(8,128)(2,1)S(1)} %get-tuple-element.65), channel_id=1, source_target_pairs={{0,4},{1,5},{2,6},{3,7},{4,0},{5,1},{6,2},{7,3},{8,12},{9,13},{10,... | collective-permute-start | bytes 786440 | tf_op jit(solution)/shard_map/ppermute | solution.py:57
  86.7 0.6 collective-permute-start.22
  87.3 2.7 %collective-permute-start.23 = (bf16[512,256]{1,0:T(8,128)(2,1)S(1)}, bf16[512,256]{1,0:T(8,128)(2,1)S(1)}, u32[]{:S(2)}, u32[]{:S(2)}) collective-permute-start(bf16[512,256]{1,0:T(8,128)(2,1)S(1)} %get-tuple-element.63), channel_id=1, source_target_pairs={{0,6},{1,7},{2,0},{3,1},{4,2},{5,3},{6,4},{7,5},{8,14},{9,15},{10,... | collective-permute-start | bytes 786440 | tf_op jit(solution)/shard_map/ppermute | solution.py:57
  89.9 4.4 %collective-permute-done.21.a_ref = bf16[512,256]{1,0:T(8,128)(2,1)S(1)} collective-permute-done((bf16[512,256]{1,0:T(8,128)(2,1)S(1)}, bf16[512,256]{1,0:T(8,128)(2,1)S(1)}, u32[]{:S(2)}, u32[]{:S(2)}) %collective-permute-start.21) | collective-permute-done | bytes 262176 | tf_op jit(solution)/shard_map/ppermute | solution.py:57
  94.4 4.7 %collective-permute-done.22.b_ref = bf16[512,256]{1,0:T(8,128)(2,1)S(1)} collective-permute-done((bf16[512,256]{1,0:T(8,128)(2,1)S(1)}, bf16[512,256]{1,0:T(8,128)(2,1)S(1)}, u32[]{:S(2)}, u32[]{:S(2)}) %collective-permute-start.22) | collective-permute-done | bytes 262176 | tf_op jit(solution)/shard_map/ppermute | solution.py:57
  99.1 0.1 collective-permute-done.23.c_ref
  99.3 0.9 shard_map.109
  (32 shorter events, 0.1 us)
Async XLA Ops:
  3.0 16.9 %collective-permute-start = (bf16[288,1024]{1,0:T(8,128)(2,1)}, bf16[288,1024]{1,0:T(8,128)(2,1)S(1)}, u32[]{:S(2)}, u32[]{:S(2)}) collective-permute-start(bf16[288,1024]{1,0:T(8,128)(2,1)} %get-tuple-element.34.refs_0_), channel_id=1, source_target_pairs={{0,8},{8,16},{16,24},{24,0},{32,40},{40,48},{48,56},{56,32},{64,72... | collective-permute-start | bytes 1769480 | tf_op jit(solution)/shard_map/ppermute | solution.py:50
  4.7 19.0 %collective-permute-start.2 = (bf16[288,1024]{1,0:T(8,128)(2,1)}, bf16[288,1024]{1,0:T(8,128)(2,1)S(1)}, u32[]{:S(2)}, u32[]{:S(2)}) collective-permute-start(bf16[288,1024]{1,0:T(8,128)(2,1)} %get-tuple-element.34.refs_0_), channel_id=1, source_target_pairs={{0,24},{8,0},{16,8},{24,16},{32,56},{40,32},{48,40},{56,48},{64,88... | collective-permute-start | bytes 1769480 | tf_op jit(solution)/shard_map/ppermute | solution.py:50
  5.4 11.6 %collective-permute-start.6 = (bf16[272,256]{1,0:T(8,128)(2,1)}, bf16[272,256]{1,0:T(8,128)(2,1)S(1)}, u32[]{:S(2)}, u32[]{:S(2)}) collective-permute-start(bf16[272,256]{1,0:T(8,128)(2,1)} %get-tuple-element.35.refs_3_.refs_2_), channel_id=1, source_target_pairs={{0,64},{8,72},{16,80},{24,88},{32,96},{40,104},{48,112},{56,120},{... | collective-permute-start | bytes 417800 | tf_op jit(solution)/shard_map/ppermute | solution.py:43
  8.4 13.3 %collective-permute-start.7 = (bf16[272,256]{1,0:T(8,128)(2,1)}, bf16[272,256]{1,0:T(8,128)(2,1)S(1)}, u32[]{:S(2)}, u32[]{:S(2)}) collective-permute-start(bf16[272,256]{1,0:T(8,128)(2,1)} %get-tuple-element.35.refs_3_.refs_2_), channel_id=1, source_target_pairs={{0,192},{8,200},{16,208},{24,216},{32,224},{40,232},{48,240},{56,2... | collective-permute-start | bytes 417800 | tf_op jit(solution)/shard_map/ppermute | solution.py:43
  11.5 14.1 %collective-permute-start.4 = (bf16[272,256]{1,0:T(8,128)(2,1)}, bf16[272,256]{1,0:T(8,128)(2,1)S(1)}, u32[]{:S(2)}, u32[]{:S(2)}) collective-permute-start(bf16[272,256]{1,0:T(8,128)(2,1)} %get-tuple-element.35.refs_3_.refs_2_), channel_id=1, source_target_pairs={{0,32},{8,40},{16,48},{24,56},{32,64},{40,72},{48,80},{56,88},{64,... | collective-permute-start | bytes 417800 | tf_op jit(solution)/shard_map/ppermute | solution.py:43
  17.0 9.9 %collective-permute-start.5 = (bf16[272,256]{1,0:T(8,128)(2,1)}, bf16[272,256]{1,0:T(8,128)(2,1)S(1)}, u32[]{:S(2)}, u32[]{:S(2)}) collective-permute-start(bf16[272,256]{1,0:T(8,128)(2,1)} %get-tuple-element.35.refs_3_.refs_2_), channel_id=1, source_target_pairs={{0,224},{8,232},{16,240},{24,248},{32,0},{40,8},{48,16},{56,24},{6... | collective-permute-start | bytes 417800 | tf_op jit(solution)/shard_map/ppermute | solution.py:43
  20.0 19.1 %collective-permute-start.10 = (bf16[272,256]{1,0:T(8,128)(2,1)S(1)}, bf16[272,256]{1,0:T(8,128)(2,1)S(1)}, u32[]{:S(2)}, u32[]{:S(2)}) collective-permute-start(bf16[272,256]{1,0:T(8,128)(2,1)S(1)} %collective-permute-done.6.refs_6_.refs_5_), channel_id=1, source_target_pairs={{0,64},{8,72},{16,80},{24,88},{32,96},{40,104},{48,112},{56,120},{... | collective-permute-start | bytes 417800 | tf_op jit(solution)/shard_map/ppermute | solution.py:43
  21.7 17.4 %collective-permute-start.8 = (bf16[272,256]{1,0:T(8,128)(2,1)S(1)}, bf16[272,256]{1,0:T(8,128)(2,1)S(1)}, u32[]{:S(2)}, u32[]{:S(2)}) collective-permute-start(bf16[272,256]{1,0:T(8,128)(2,1)S(1)} %collective-permute-done.6.refs_6_.refs_5_), channel_id=1, source_target_pairs={{0,32},{8,40},{16,48},{24,56},{32,64},{40,72},{48,80},{56,88},{64,... | collective-permute-start | bytes 417800 | tf_op jit(solution)/shard_map/ppermute | solution.py:43
  23.7 15.4 %collective-permute-start.9 = (bf16[272,256]{1,0:T(8,128)(2,1)S(1)}, bf16[272,256]{1,0:T(8,128)(2,1)S(1)}, u32[]{:S(2)}, u32[]{:S(2)}) collective-permute-start(bf16[272,256]{1,0:T(8,128)(2,1)S(1)} %collective-permute-done.7.refs_7_.refs_6_), channel_id=1, source_target_pairs={{0,224},{8,232},{16,240},{24,248},{32,0},{40,8},{48,16},{56,24},{6... | collective-permute-start | bytes 417800 | tf_op jit(solution)/shard_map/ppermute | solution.py:43
  25.6 13.5 %collective-permute-start.1 = (bf16[144,1024]{1,0:T(8,128)(2,1)S(1)}, bf16[144,1024]{1,0:T(8,128)(2,1)S(1)}, u32[]{:S(2)}, u32[]{:S(2)}) collective-permute-start(bf16[144,1024]{1,0:T(8,128)(2,1)S(1)} %slice.40), channel_id=1, source_target_pairs={{0,8},{8,16},{16,24},{24,0},{32,40},{40,48},{48,56},{56,32},{64,72... | collective-permute-start | bytes 884744 | tf_op jit(solution)/shard_map/ppermute | solution.py:50
  27.0 12.2 %collective-permute-start.3 = (bf16[144,1024]{1,0:T(8,128)(2,1)S(1)}, bf16[144,1024]{1,0:T(8,128)(2,1)S(1)}, u32[]{:S(2)}, u32[]{:S(2)}) collective-permute-start(bf16[144,1024]{1,0:T(8,128)(2,1)S(1)} %slice.41), channel_id=1, source_target_pairs={{0,24},{8,0},{16,8},{24,16},{32,56},{40,32},{48,40},{56,48},{64,88... | collective-permute-start | bytes 884744 | tf_op jit(solution)/shard_map/ppermute | solution.py:50
  27.7 1.1 %copy-start.4 = (bf16[288,1024]{1,0:T(8,128)(2,1)S(1)}, bf16[288,1024]{1,0:T(8,128)(2,1)}, u32[]{:S(2)}) copy-start(bf16[288,1024]{1,0:T(8,128)(2,1)} %get-tuple-element.34.refs_0_) | copy-start | bytes 1769476
  28.8 0.9 copy-start.5
  39.1 7.8 %copy-start.6 = (bf16[272,256]{1,0:T(8,128)(2,1)S(1)}, bf16[272,256]{1,0:T(8,128)(2,1)}, u32[]{:S(2)}) copy-start(bf16[272,256]{1,0:T(8,128)(2,1)} %get-tuple-element.35.refs_3_.refs_2_) | copy-start | bytes 417796
  50.0 21.6 %collective-permute-start.19 = (bf16[512,256]{1,0:T(8,128)(2,1)S(1)}, bf16[512,256]{1,0:T(8,128)(2,1)S(1)}, u32[]{:S(2)}, u32[]{:S(2)}) collective-permute-start(bf16[512,256]{1,0:T(8,128)(2,1)S(1)} %get-tuple-element.59), channel_id=1, source_target_pairs={{0,16},{8,24},{16,0},{24,8},{32,48},{40,56},{48,32},{56,40},{64,80... | collective-permute-start | bytes 786440 | tf_op jit(solution)/shard_map/ppermute | solution.py:50
  51.6 22.0 %collective-permute-start.17 = (bf16[512,256]{1,0:T(8,128)(2,1)S(1)}, bf16[512,256]{1,0:T(8,128)(2,1)S(1)}, u32[]{:S(2)}, u32[]{:S(2)}) collective-permute-start(bf16[512,256]{1,0:T(8,128)(2,1)S(1)} %get-tuple-element.57), channel_id=1, source_target_pairs={{0,24},{8,0},{16,8},{24,16},{32,56},{40,32},{48,40},{56,48},{64,88... | collective-permute-start | bytes 786440 | tf_op jit(solution)/shard_map/ppermute | solution.py:50
  53.4 9.0 %collective-permute-start.11 = (bf16[384,256]{1,0:T(8,128)(2,1)}, bf16[384,256]{1,0:T(8,128)(2,1)S(1)}, u32[]{:S(2)}, u32[]{:S(2)}) collective-permute-start(bf16[384,256]{1,0:T(8,128)(2,1)} %get-tuple-element.50), channel_id=1, source_target_pairs={{0,192},{8,200},{16,208},{24,216},{32,224},{40,232},{48,240},{56,2... | collective-permute-start | bytes 589832 | tf_op jit(solution)/shard_map/ppermute | solution.py:43
  55.8 12.7 %collective-permute-start.12 = (bf16[384,256]{1,0:T(8,128)(2,1)}, bf16[384,256]{1,0:T(8,128)(2,1)S(1)}, u32[]{:S(2)}, u32[]{:S(2)}) collective-permute-start(bf16[384,256]{1,0:T(8,128)(2,1)} %get-tuple-element.51), channel_id=1, source_target_pairs={{0,64},{8,72},{16,80},{24,88},{32,96},{40,104},{48,112},{56,120},{... | collective-permute-start | bytes 589832 | tf_op jit(solution)/shard_map/ppermute | solution.py:43
  56.3 1.4 %copy-start.7 = (s32[256]{0:T(256)S(1)}, s32[256]{0:T(256)}, u32[]{:S(2)}) copy-start(s32[256]{0:T(256)} %pos_hbm.1) | copy-start | bytes 3076
  56.3 17.6 %collective-permute-start.18 = (bf16[512,256]{1,0:T(8,128)(2,1)S(1)}, bf16[512,256]{1,0:T(8,128)(2,1)S(1)}, u32[]{:S(2)}, u32[]{:S(2)}) collective-permute-start(bf16[512,256]{1,0:T(8,128)(2,1)S(1)} %get-tuple-element.58), channel_id=1, source_target_pairs={{0,8},{8,16},{16,24},{24,0},{32,40},{40,48},{48,56},{56,32},{64,72... | collective-permute-start | bytes 786440 | tf_op jit(solution)/shard_map/ppermute | solution.py:50
  68.6 8.9 %collective-permute-start.13 = (bf16[256,256]{1,0:T(8,128)(2,1)S(1)}, bf16[256,256]{1,0:T(8,128)(2,1)S(1)}, u32[]{:S(2)}, u32[]{:S(2)}) collective-permute-start(bf16[256,256]{1,0:T(8,128)(2,1)S(1)} %get-tuple-element.52), channel_id=1, source_target_pairs={{0,192},{8,200},{16,208},{24,216},{32,224},{40,232},{48,240},{56,2... | collective-permute-start | bytes 393224 | tf_op jit(solution)/shard_map/ppermute | solution.py:43
  68.7 8.8 %collective-permute-start.14 = (bf16[256,256]{1,0:T(8,128)(2,1)S(1)}, bf16[256,256]{1,0:T(8,128)(2,1)S(1)}, u32[]{:S(2)}, u32[]{:S(2)}) collective-permute-start(bf16[256,256]{1,0:T(8,128)(2,1)S(1)} %get-tuple-element.53), channel_id=1, source_target_pairs={{0,64},{8,72},{16,80},{24,88},{32,96},{40,104},{48,112},{56,120},{... | collective-permute-start | bytes 393224 | tf_op jit(solution)/shard_map/ppermute | solution.py:43
  71.6 5.9 %collective-permute-start.15 = (bf16[256,256]{1,0:T(8,128)(2,1)S(1)}, bf16[256,256]{1,0:T(8,128)(2,1)S(1)}, u32[]{:S(2)}, u32[]{:S(2)}) collective-permute-start(bf16[256,256]{1,0:T(8,128)(2,1)S(1)} %get-tuple-element.54), channel_id=1, source_target_pairs={{0,224},{8,232},{16,240},{24,248},{32,0},{40,8},{48,16},{56,24},{6... | collective-permute-start | bytes 393224 | tf_op jit(solution)/shard_map/ppermute | solution.py:43
  73.6 6.2 %collective-permute-start.16 = (bf16[256,256]{1,0:T(8,128)(2,1)S(1)}, bf16[256,256]{1,0:T(8,128)(2,1)S(1)}, u32[]{:S(2)}, u32[]{:S(2)}) collective-permute-start(bf16[256,256]{1,0:T(8,128)(2,1)S(1)} %get-tuple-element.55), channel_id=1, source_target_pairs={{0,32},{8,40},{16,48},{24,56},{32,64},{40,72},{48,80},{56,88},{64,... | collective-permute-start | bytes 393224 | tf_op jit(solution)/shard_map/ppermute | solution.py:43
  73.9 2.2 %copy-start = (bf16[4096,512]{1,0:T(8,128)(2,1)S(1)}, bf16[4096,512]{1,0:T(8,128)(2,1)}, u32[]{:S(2)}) copy-start(bf16[4096,512]{1,0:T(8,128)(2,1)} %refs_6_.1) | copy-start | bytes 12582916
  76.1 3.7 %copy-start.1 = (bf16[4096,128]{1,0:T(8,128)(2,1)S(1)}, bf16[4096,128]{1,0:T(8,128)(2,1)}, u32[]{:S(2)}) copy-start(bf16[4096,128]{1,0:T(8,128)(2,1)} %wk_ref.1) | copy-start | bytes 3145732
  76.1 3.7 %copy-start.2 = (bf16[4096,128]{1,0:T(8,128)(2,1)S(1)}, bf16[4096,128]{1,0:T(8,128)(2,1)}, u32[]{:S(2)}) copy-start(bf16[4096,128]{1,0:T(8,128)(2,1)} %wv_ref.1) | copy-start | bytes 3145732
  76.1 3.7 %copy-start.3 = (f32[8,128]{1,0:T(8,128)S(1)}, f32[8,128]{1,0:T(8,128)}, u32[]{:S(2)}) copy-start(f32[8,128]{1,0:T(8,128)} %shard_map.106.refs_10_) | copy-start | bytes 12292
  80.6 2.7 %collective-permute-start.20 = (bf16[4,512,256]{2,1,0:T(8,128)(2,1)S(1)}, bf16[4,512,256]{2,1,0:T(8,128)(2,1)S(1)}, u32[]{:S(2)}, u32[]{:S(2)}) collective-permute-start(bf16[4,512,256]{2,1,0:T(8,128)(2,1)S(1)} %get-tuple-element.62), channel_id=1, source_target_pairs={{0,1},{1,0},{2,3},{3,2},{4,5},{5,4},{6,7},{7,6},{8,9},{9,8},{10,11... | collective-permute-start | bytes 3145736 | tf_op jit(solution)/shard_map/ppermute | solution.py:62
  83.6 10.8 %collective-permute-start.21 = (bf16[512,256]{1,0:T(8,128)(2,1)S(1)}, bf16[512,256]{1,0:T(8,128)(2,1)S(1)}, u32[]{:S(2)}, u32[]{:S(2)}) collective-permute-start(bf16[512,256]{1,0:T(8,128)(2,1)S(1)} %get-tuple-element.65), channel_id=1, source_target_pairs={{0,4},{1,5},{2,6},{3,7},{4,0},{5,1},{6,2},{7,3},{8,12},{9,13},{10,... | collective-permute-start | bytes 786440 | tf_op jit(solution)/shard_map/ppermute | solution.py:57
  86.7 12.4 %collective-permute-start.22 = (bf16[512,256]{1,0:T(8,128)(2,1)S(1)}, bf16[512,256]{1,0:T(8,128)(2,1)S(1)}, u32[]{:S(2)}, u32[]{:S(2)}) collective-permute-start(bf16[512,256]{1,0:T(8,128)(2,1)S(1)} %get-tuple-element.64), channel_id=1, source_target_pairs={{0,2},{1,3},{2,4},{3,5},{4,6},{5,7},{6,0},{7,1},{8,10},{9,11},{10,... | collective-permute-start | bytes 786440 | tf_op jit(solution)/shard_map/ppermute | solution.py:57
  87.3 12.0 %collective-permute-start.23 = (bf16[512,256]{1,0:T(8,128)(2,1)S(1)}, bf16[512,256]{1,0:T(8,128)(2,1)S(1)}, u32[]{:S(2)}, u32[]{:S(2)}) collective-permute-start(bf16[512,256]{1,0:T(8,128)(2,1)S(1)} %get-tuple-element.63), channel_id=1, source_target_pairs={{0,6},{1,7},{2,0},{3,1},{4,2},{5,3},{6,4},{7,5},{8,14},{9,15},{10,... | collective-permute-start | bytes 786440 | tf_op jit(solution)/shard_map/ppermute | solution.py:57

commit v5 on v4

--- a/solution.py
+++ b/solution.py
@@ -335,7 +335,7 @@
 
 def query_kernel(*refs):
     dqs = refs[0:4]
-    cos_ref, sin_ref, wq_ref, out_ref, x_ref = refs[4:]
+    cos_ref, sin_ref, wq_ref, keep_ref, send_ref, x_ref = refs[4:]
     cosine = cos_ref[...]
     sine = sin_ref[...]
     for head in range(REPEAT):
@@ -344,34 +344,30 @@
         for ref in dqs[1:]:
             total = total + ref[rows, :].astype(F32)
         x_ref[rows, :] = rotate(total, cosine, sine).astype(BF)
-    for i in range(2 * NX):
-        out_ref[i] = dot(wq_ref[block_rows(i), :], x_ref[...], NN)
-
-
-def add_terms(part_ref, x_ref, wk_ref, wv_ref, i):
-    rows = block_rows(i)
-    return (
-        part_ref[i]
-        + dot(wk_ref[rows, :], x_ref[0:128, :], NN)
-        + dot(wv_ref[rows, :], x_ref[128:256, :], NN)
-    )
-
-
-def send_kernel(*refs):
+    for i in range(NX):
+        send_ref[i] = dot(wq_ref[block_rows(i), :], x_ref[...], NN).astype(BF)
+        keep_ref[i] = dot(wq_ref[block_rows(NX + i), :], x_ref[...], NN)
+
+
+def key_kernel(*refs):
     dkvs = refs[0:5]
-    cos_ref, sin_ref, part_ref, wk_ref, wv_ref, _, x_out, out_ref = refs[5:]
+    cos_ref, sin_ref, _, x_out = refs[5:]
     total = dkvs[0][...]
     for ref in dkvs[1:]:
         total = total + ref[...].astype(F32)
     x_out[0:128, :] = rotate(total[:, 0:128].T, cos_ref[...], sin_ref[...]).astype(BF)
     x_out[128:256, :] = total[:, 128:256].T.astype(BF)
+
+
+def sum_kernel(keep_ref, came_ref, x_ref, x_other_ref, wk_ref, wv_ref, wk_other_ref, wv_other_ref, *outs):
     for i in range(NX):
-        out_ref[i] = add_terms(part_ref, x_out, wk_ref, wv_ref, i).astype(BF)
-
-
-def keep_kernel(x_ref, part_ref, wk_ref, wv_ref, out_ref):
-    for i in range(NX):
-        out_ref[i] = add_terms(part_ref, x_ref, wk_ref, wv_ref, NX + i)
+        rows = block_rows(NX + i)
+        total = keep_ref[i] + came_ref[i].astype(F32)
+        total = total + dot(wk_ref[rows, :], x_ref[0:128, :], NN)
+        total = total + dot(wv_ref[rows, :], x_ref[128:256, :], NN)
+        total = total + dot(wk_other_ref[rows, :], x_other_ref[0:128, :], NN)
+        total = total + dot(wv_other_ref[rows, :], x_other_ref[128:256, :], NN)
+        outs[i][...] = total.astype(outs[i].dtype)
 
 
 def merge_kernel(up1, down1, up2, down2, from_up, from_down, *outs):
@@ -426,6 +422,8 @@
         cost_estimate=pl.CostEstimate(flops=8_000_000_000, bytes_accessed=8192, transcendentals=0),
     )(mark)
 
+    key_other = swap_core(w_key)
+    value_other = swap_core(w_value)
     left = move_y(pack, 1)
     right = move_y(pack, -1)
     up1 = move_z(kv, 1)
@@ -467,37 +465,34 @@
     cosine = jnp.cos(angles)
     sine = jnp.sin(angles)
 
-    part = pl.pallas_call(
+    kept, to_send = pl.pallas_call(
         query_kernel,
-        out_shape=whole((2 * NX, 512, ROWS), F32),
+        out_shape=(whole((NX, 512, ROWS), F32), whole((NX, 512, ROWS), BF)),
         in_specs=[VM] * 7,
-        out_specs=VM,
+        out_specs=(VM, VM),
         scratch_shapes=[pltpu.VMEM((512, ROWS), BF)],
         compiler_params=pltpu.CompilerParams(vmem_limit_bytes=20 * MIB),
         cost_estimate=pl.CostEstimate(
             flops=1_100_000_000, bytes_accessed=8_000_000, transcendentals=0
         ),
     )(*dqs, cosine, sine, w_query)
-    grads, to_send = pl.pallas_call(
-        send_kernel,
-        out_shape=(whole((256, ROWS), BF), whole((NX, 512, ROWS), BF)),
-        in_specs=[VM] * 10 + [ANY],
-        out_specs=(VM, VM),
+    terms = swap_core(to_send)
+    grads = pl.pallas_call(
+        key_kernel,
+        out_shape=whole((256, ROWS), BF),
+        in_specs=[VM] * 7 + [ANY],
+        out_specs=VM,
+        compiler_params=pltpu.CompilerParams(vmem_limit_bytes=8 * MIB),
+    )(*dkvs, cosine, sine, mark)
+    others = swap_core(grads)
+    parts = pl.pallas_call(
+        sum_kernel,
+        out_shape=(whole((512, ROWS), F32),) + (whole((512, ROWS), BF),) * (NX - 1),
+        in_specs=[VM] * 8,
+        out_specs=(VM,) * NX,
         compiler_params=pltpu.CompilerParams(vmem_limit_bytes=20 * MIB),
-    )(*dkvs, cosine, sine, part, w_key, w_value, mark)
-    got = swap_core(to_send)
-    kept = pl.pallas_call(
-        keep_kernel,
-        out_shape=whole((NX, 512, ROWS), F32),
-        in_specs=[VM] * 4,
-        out_specs=VM,
-        compiler_params=pltpu.CompilerParams(vmem_limit_bytes=20 * MIB),
-        cost_estimate=pl.CostEstimate(
-            flops=800_000_000, bytes_accessed=4_000_000, transcendentals=0
-        ),
-    )(grads, part, w_key, w_value)
-    parts = [kept[i] + got[i].astype(F32) for i in range(4)]
-    came = [move_x(parts[i].astype(BF), i) for i in (2, 1, 3)]
+    )(kept, terms, grads, others, w_key, w_value, key_other, value_other)
+    came = [move_x(parts[i], i) for i in (2, 1, 3)]
     return pl.pallas_call(
         final_kernel,
         out_shape=whole((ROWS, 512), BF),

time: 102 us -> 116 us (1.14)
  the two profiles are of different devices: /device:TPU:8 before, /device:TPU:1 now
where the time goes in v5:
time: 116 us
  starting transfers between devices  53.5 us (46%)
  Pallas kernels  32 us (28%)
  waiting for transfers between devices  24.3 us (21%)
  local copies, waits for them, and re-layouts  5.82 us (5%)
    ppermute x13, starting transfers between devices, move_z(): return lax.ppermute(value, 'seq', pairs)  29.4 us
    pallas_call x3, Pallas kernels, attend(): pl.pallas_call(functools.partial(attn_kernel, sizes, len(kvs), has_dq, ha...  20.4 us
    ppermute x4, starting transfers between devices, swap_core(): return lax.ppermute(value, 'tp', pairs)  10.4 us
    ppermute x3, waiting for transfers between devices, move_x(): return lax.ppermute(value, 'tp', pairs)  9.93 us
    ppermute x13, waiting for transfers between devices, move_z(): return lax.ppermute(value, 'seq', pairs)  9.76 us
    ppermute x7, starting transfers between devices, move_y(): return lax.ppermute(value, 'seq', pairs)  8.11 us
    unnamed x22, local copies, waits for them, and re-layouts  5.78 us
    ppermute x3, starting transfers between devices, move_x(): return lax.ppermute(value, 'tp', pairs)  5.5 us
  transfers between devices with their start and end apart: 27, of which 9 were waited for; matrix products, arithmetic and copies ran while one was open for 0% of the time, Pallas kernels for 10%

profile of v5, /device:TPU:1, one launch (start us, length us, event | category | flops | bytes accessed | tf_op | source)
XLA Modules:
  0.0 116.1 jit_solution(18016729279314790866)
XLA Ops:
  0.0 3.0 %shard_map.100 = (bf16[288,1024]{1,0:T(8,128)(2,1)}, bf16[272,256]{1,0:T(8,128)(2,1)}, f32[8,128]{1,0:T(8,128)}) custom-call(s32[256]{0:T(256)} %pos_hbm.1, bf16[256,512]{1,0:T(8,128)(2,1)} %q_hbm.1, bf16[256,512]{1,0:T(8,128)(2,1)} %do_hbm.1, bf16[256,512]{1,0:T(8,128)(2,1)} %o_hbm.1, f32[4,256]{1,0:T(4,128)} %lse_hbm.1, bf16[256,128]{1,0:T(8,128)(2,1)} %k_hbm.1, ...), custom_call_target="tpu_custom_call" | custom-call | tf_op jit(solution)/shard_map/pallas_call | solution.py:399
  3.1 2.2 %collective-permute-start = (bf16[288,1024]{1,0:T(8,128)(2,1)}, bf16[288,1024]{1,0:T(8,128)(2,1)S(1)}, u32[]{:S(2)}, u32[]{:S(2)}) collective-permute-start(bf16[288,1024]{1,0:T(8,128)(2,1)} %get-tuple-element.38.refs_0_), channel_id=1, source_target_pairs={{0,8},{8,16},{16,24},{24,0},{32,40},{40,48},{48,56},{56,32},{64,72... | collective-permute-start | bytes 1769480 | tf_op jit(solution)/shard_map/ppermute | solution.py:50
  5.2 1.5 %collective-permute-start.1 = (bf16[288,1024]{1,0:T(8,128)(2,1)}, bf16[288,1024]{1,0:T(8,128)(2,1)S(1)}, u32[]{:S(2)}, u32[]{:S(2)}) collective-permute-start(bf16[288,1024]{1,0:T(8,128)(2,1)} %get-tuple-element.38.refs_0_), channel_id=1, source_target_pairs={{0,24},{8,0},{16,8},{24,16},{32,56},{40,32},{48,40},{56,48},{64,88... | collective-permute-start | bytes 1769480 | tf_op jit(solution)/shard_map/ppermute | solution.py:50
  6.8 3.0 %collective-permute-start.4 = (bf16[272,256]{1,0:T(8,128)(2,1)}, bf16[272,256]{1,0:T(8,128)(2,1)S(1)}, u32[]{:S(2)}, u32[]{:S(2)}) collective-permute-start(bf16[272,256]{1,0:T(8,128)(2,1)} %get-tuple-element.39.refs_3_.refs_2_), channel_id=1, source_target_pairs={{0,64},{8,72},{16,80},{24,88},{32,96},{40,104},{48,112},{56,120},{... | collective-permute-start | bytes 417800 | tf_op jit(solution)/shard_map/ppermute | solution.py:43
  9.8 3.0 %collective-permute-start.6 = (bf16[272,256]{1,0:T(8,128)(2,1)}, bf16[272,256]{1,0:T(8,128)(2,1)S(1)}, u32[]{:S(2)}, u32[]{:S(2)}) collective-permute-start(bf16[272,256]{1,0:T(8,128)(2,1)} %get-tuple-element.39.refs_3_.refs_2_), channel_id=1, source_target_pairs={{0,192},{8,200},{16,208},{24,216},{32,224},{40,232},{48,240},{56,2... | collective-permute-start | bytes 417800 | tf_op jit(solution)/shard_map/ppermute | solution.py:43
  12.8 1.9 %collective-permute-start.10 = (bf16[272,256]{1,0:T(8,128)(2,1)}, bf16[272,256]{1,0:T(8,128)(2,1)S(1)}, u32[]{:S(2)}, u32[]{:S(2)}) collective-permute-start(bf16[272,256]{1,0:T(8,128)(2,1)} %get-tuple-element.39.refs_3_.refs_2_), channel_id=1, source_target_pairs={{0,224},{8,232},{16,240},{24,248},{32,0},{40,8},{48,16},{56,24},{6... | collective-permute-start | bytes 417800 | tf_op jit(solution)/shard_map/ppermute | solution.py:43
  14.7 1.9 %collective-permute-done.4.refs_6_.refs_5_ = bf16[272,256]{1,0:T(8,128)(2,1)S(1)} collective-permute-done((bf16[272,256]{1,0:T(8,128)(2,1)}, bf16[272,256]{1,0:T(8,128)(2,1)S(1)}, u32[]{:S(2)}, u32[]{:S(2)}) %collective-permute-start.4) | collective-permute-done | bytes 139296 | tf_op jit(solution)/shard_map/ppermute | solution.py:43
  16.6 3.8 %collective-permute-start.9 = (bf16[272,256]{1,0:T(8,128)(2,1)}, bf16[272,256]{1,0:T(8,128)(2,1)S(1)}, u32[]{:S(2)}, u32[]{:S(2)}) collective-permute-start(bf16[272,256]{1,0:T(8,128)(2,1)} %get-tuple-element.39.refs_3_.refs_2_), channel_id=1, source_target_pairs={{0,32},{8,40},{16,48},{24,56},{32,64},{40,72},{48,80},{56,88},{64,... | collective-permute-start | bytes 417800 | tf_op jit(solution)/shard_map/ppermute | solution.py:43
  20.4 0.9 collective-permute-start.5
  21.4 3.1 %collective-permute-start.8 = (bf16[272,256]{1,0:T(8,128)(2,1)S(1)}, bf16[272,256]{1,0:T(8,128)(2,1)S(1)}, u32[]{:S(2)}, u32[]{:S(2)}) collective-permute-start(bf16[272,256]{1,0:T(8,128)(2,1)S(1)} %collective-permute-done.4.refs_6_.refs_5_), channel_id=1, source_target_pairs={{0,64},{8,72},{16,80},{24,88},{32,96},{40,104},{48,112},{56,120},{... | collective-permute-start | bytes 417800 | tf_op jit(solution)/shard_map/ppermute | solution.py:43
  24.5 1.0 collective-permute-start.7
  25.5 0.8 collective-permute-start.2
  26.4 1.9 %collective-permute-start.3 = (bf16[144,1024]{1,0:T(8,128)(2,1)S(1)}, bf16[144,1024]{1,0:T(8,128)(2,1)S(1)}, u32[]{:S(2)}, u32[]{:S(2)}) collective-permute-start(bf16[144,1024]{1,0:T(8,128)(2,1)S(1)} %slice.9), channel_id=1, source_target_pairs={{0,24},{8,0},{16,8},{24,16},{32,56},{40,32},{48,40},{56,48},{64,88... | collective-permute-start | bytes 884744 | tf_op jit(solution)/shard_map/ppermute | solution.py:50
  28.3 1.1 copy-done.7
  29.4 0.9 copy-done.8
  30.3 7.8 %shard_map.101 = (f32[512,256]{1,0:T(8,128)S(1)}, f32[512,256]{1,0:T(8,128)S(1)}, f32[512,256]{1,0:T(8,128)S(1)}, f32[256,256]{1,0:T(8,128)S(1)}, f32[256,256]{1...) custom-call(bf16[288,1024]{1,0:T(8,128)(2,1)S(1)} %copy-done.7, ...), custom_call_target="tpu_custom_call" | custom-call | flops 5100000256 | bytes 4000000 | tf_op jit(solution)/shard_map/pallas_call | solution.py:294
  38.1 8.7 %shard_map.102 = (f32[512,256]{1,0:T(8,128)S(1)}, bf16[512,256]{1,0:T(8,128)(2,1)S(1)}, bf16[512,256]{1,0:T(8,128)(2,1)S(1)}, f32[512,256]{1,0:T(8,128)S(1)}, bf...) custom-call(bf16[288,1024]{1,0:T(8,128)(2,1)S(1)} %copy-done.7, ...), custom_call_target="tpu_custom_call" | custom-call | flops 4080000000 | bytes 4000000 | tf_op jit(solution)/shard_map/pallas_call | solution.py:294
  46.9 3.9 %shard_map.103 = (bf16[512,256]{1,0:T(8,128)(2,1)S(1)}, f32[256,256]{1,0:T(8,128)S(1)}, f32[256,256]{1,0:T(8,128)S(1)}, f32[256,256]{1,0:T(8,128)S(1)}, f32[256,256]{1,0:T(8,128)S(1)}, /*index=5*/f32[256,256]{1,0:T(8,128)S(1)}) custom-call(bf16[144,1024]{1,0:T(8,128)(2,1)S(1)} %collective-permute-done.2.refs_3_.refs_0_, ...), custom_call_target="tpu_custom_call" | custom-call | flops 1700000000 | bytes 4000000 | tf_op jit(solution)/shard_map/pallas_call | solution.py:294
  50.9 1.1 collective-permute-start.11
  52.0 0.4 collective-permute-start.12
  52.5 2.3 %collective-permute-start.15 = (bf16[384,256]{1,0:T(8,128)(2,1)S(1)}, bf16[384,256]{1,0:T(8,128)(2,1)S(1)}, u32[]{:S(2)}, u32[]{:S(2)}) collective-permute-start(bf16[384,256]{1,0:T(8,128)(2,1)S(1)} %get-tuple-element.60), channel_id=1, source_target_pairs={{0,192},{8,200},{16,208},{24,216},{32,224},{40,232},{48,240},{56,2... | collective-permute-start | bytes 589832 | tf_op jit(solution)/shard_map/ppermute | solution.py:43
  54.9 0.3 multiply_sine_fusion
  55.2 2.5 %collective-permute-done.13.refs_3_ = bf16[512,256]{1,0:T(8,128)(2,1)S(1)} collective-permute-done((bf16[512,256]{1,0:T(8,128)(2,1)S(1)}, bf16[512,256]{1,0:T(8,128)(2,1)S(1)}, u32[]{:S(2)}, u32[]{:S(2)}) %collective-permute-start.13) | collective-permute-done | bytes 262176 | tf_op jit(solution)/shard_map/ppermute | solution.py:50
  57.7 6.3 %collective-permute-start.22 = (bf16[4096,128]{1,0:T(8,128)(2,1)S(1)}, bf16[4096,128]{1,0:T(8,128)(2,1)}, u32[]{:S(2)}, u32[]{:S(2)}) collective-permute-start(bf16[4096,128]{1,0:T(8,128)(2,1)S(1)} %copy-done.1), channel_id=1, source_target_pairs={{0,1},{1,0},{2,3},{3,2},{4,5},{5,4},{6,7},{7,6},{8,9},{9,8},{10,11... | collective-permute-start | bytes 3145736 | tf_op jit(solution)/shard_map/ppermute | solution.py:62
  64.1 1.2 %collective-permute-done.12.refs_2_ = bf16[512,256]{1,0:T(8,128)(2,1)S(1)} collective-permute-done((bf16[512,256]{1,0:T(8,128)(2,1)S(1)}, bf16[512,256]{1,0:T(8,128)(2,1)S(1)}, u32[]{:S(2)}, u32[]{:S(2)}) %collective-permute-start.12) | collective-permute-done | bytes 262176 | tf_op jit(solution)/shard_map/ppermute | solution.py:50
  65.2 2.3 %shard_map.104 = (f32[4,512,256]{2,1,0:T(8,128)S(1)}, bf16[4,512,256]{2,1,0:T(8,128)(2,1)}) custom-call(f32[512,256]{1,0:T(8,128)S(1)} %get-tuple-element.43.refs_0_, bf16[512,256]{1,0:T(8,128)(2,1)S(1)} %collective-permute-done.11.refs_1_, bf16[512,256]{1,0:T(8,128)(2,1)S(1)} %collective-permute-done.12.refs_2_, ...), custom_call_target="tpu_custom_call" | custom-call | flops 1100000000 | bytes 8000000 | tf_op jit(solution)/shard_map/pallas_call | solution.py:468
  67.5 1.5 %collective-permute-start.14 = (bf16[4,512,256]{2,1,0:T(8,128)(2,1)}, bf16[4,512,256]{2,1,0:T(8,128)(2,1)}, u32[]{:S(2)}, u32[]{:S(2)}) collective-permute-start(bf16[4,512,256]{2,1,0:T(8,128)(2,1)} %get-tuple-element.54), channel_id=1, source_target_pairs={{0,1},{1,0},{2,3},{3,2},{4,5},{5,4},{6,7},{7,6},{8,9},{9,8},{10,11... | collective-permute-start | bytes 3145736 | tf_op jit(solution)/shard_map/ppermute | solution.py:62
  69.0 0.8 shard_map.105
  69.8 2.3 %collective-permute-start.17 = (bf16[256,256]{1,0:T(8,128)(2,1)S(1)}, bf16[256,256]{1,0:T(8,128)(2,1)S(1)}, u32[]{:S(2)}, u32[]{:S(2)}) collective-permute-start(bf16[256,256]{1,0:T(8,128)(2,1)S(1)} %get-tuple-element.62), channel_id=1, source_target_pairs={{0,192},{8,200},{16,208},{24,216},{32,224},{40,232},{48,240},{56,2... | collective-permute-start | bytes 393224 | tf_op jit(solution)/shard_map/ppermute | solution.py:43
  72.2 2.8 %collective-permute-done.17.refs_1_ = bf16[256,256]{1,0:T(8,128)(2,1)S(1)} collective-permute-done((bf16[256,256]{1,0:T(8,128)(2,1)S(1)}, bf16[256,256]{1,0:T(8,128)(2,1)S(1)}, u32[]{:S(2)}, u32[]{:S(2)}) %collective-permute-start.17) | collective-permute-done | bytes 131104 | tf_op jit(solution)/shard_map/ppermute | solution.py:43
  75.0 0.6 copy-done.2
  75.6 7.6 %collective-permute-start.19 = (bf16[256,256]{1,0:T(8,128)(2,1)}, bf16[256,256]{1,0:T(8,128)(2,1)}, u32[]{:S(2)}, u32[]{:S(2)}) collective-permute-start(bf16[256,256]{1,0:T(8,128)(2,1)} %get-tuple-element.64), channel_id=1, source_target_pairs={{0,224},{8,232},{16,240},{24,248},{32,0},{40,8},{48,16},{56,24},{6... | collective-permute-start | bytes 393224 | tf_op jit(solution)/shard_map/ppermute | solution.py:43
  83.2 0.7 copy-done.4
  84.1 1.7 %collective-permute-done.19.refs_3_ = bf16[256,256]{1,0:T(8,128)(2,1)} collective-permute-done((bf16[256,256]{1,0:T(8,128)(2,1)}, bf16[256,256]{1,0:T(8,128)(2,1)}, u32[]{:S(2)}, u32[]{:S(2)}) %collective-permute-start.19) | collective-permute-done | bytes 131104 | tf_op jit(solution)/shard_map/ppermute | solution.py:43
  85.8 3.4 %collective-permute-done.20.refs_4_ = bf16[256,256]{1,0:T(8,128)(2,1)} collective-permute-done((bf16[256,256]{1,0:T(8,128)(2,1)}, bf16[256,256]{1,0:T(8,128)(2,1)}, u32[]{:S(2)}, u32[]{:S(2)}) %collective-permute-start.20) | collective-permute-done | bytes 131104 | tf_op jit(solution)/shard_map/ppermute | solution.py:43
  89.2 0.9 copy-done.3
  90.1 0.9 copy-done.5
  91.0 0.7 copy-done.6
  91.7 1.1 shard_map.107.x_ref
  92.8 2.6 %collective-permute-start.21 = (bf16[256,256]{1,0:T(8,128)(2,1)S(1)}, bf16[256,256]{1,0:T(8,128)(2,1)S(1)}, u32[]{:S(2)}, u32[]{:S(2)}) collective-permute-start(bf16[256,256]{1,0:T(8,128)(2,1)S(1)} %shard_map.107.x_ref), channel_id=1, source_target_pairs={{0,1},{1,0},{2,3},{3,2},{4,5},{5,4},{6,7},{7,6},{8,9},{9,8},{10,11... | collective-permute-start | bytes 393224 | tf_op jit(solution)/shard_map/ppermute | solution.py:62
  95.4 1.0 collective-permute-done.21.x_other_ref
  96.4 3.4 %shard_map.108 = (f32[512,256]{1,0:T(8,128)S(1)}, bf16[512,256]{1,0:T(8,128)(2,1)S(1)}, bf16[512,256]{1,0:T(8,128)(2,1)S(1)}, bf16[512,256]{1,0:T(8,128)(2,1)S(1)}) custom-call(f32[4,512,256]{2,1,0:T(8,128)S(1)} %get-tuple-element.53.keep_ref, bf16[4,512,256]{2,1,0:T(8,128)(2,1)} %collective-permute-done.14.came_ref, bf16[256,256]{1,0:T(8,128)(2,1)S(1)} %shard_map.107.x_ref, ...), custom_call_target="tpu_custom_call" | custom-call | tf_op jit(solution)/shard_map/pallas_call | solution.py:488
  99.8 2.8 %collective-permute-start.24 = (bf16[512,256]{1,0:T(8,128)(2,1)S(1)}, bf16[512,256]{1,0:T(8,128)(2,1)S(1)}, u32[]{:S(2)}, u32[]{:S(2)}) collective-permute-start(bf16[512,256]{1,0:T(8,128)(2,1)S(1)} %get-tuple-element.68), channel_id=1, source_target_pairs={{0,4},{1,5},{2,6},{3,7},{4,0},{5,1},{6,2},{7,3},{8,12},{9,13},{10,... | collective-permute-start | bytes 786440 | tf_op jit(solution)/shard_map/ppermute | solution.py:57
  102.6 0.3 collective-permute-start.25
  102.9 2.4 %collective-permute-start.26 = (bf16[512,256]{1,0:T(8,128)(2,1)S(1)}, bf16[512,256]{1,0:T(8,128)(2,1)S(1)}, u32[]{:S(2)}, u32[]{:S(2)}) collective-permute-start(bf16[512,256]{1,0:T(8,128)(2,1)S(1)} %get-tuple-element.70), channel_id=1, source_target_pairs={{0,6},{1,7},{2,0},{3,1},{4,2},{5,3},{6,4},{7,5},{8,14},{9,15},{10,... | collective-permute-start | bytes 786440 | tf_op jit(solution)/shard_map/ppermute | solution.py:57
  105.3 3.6 %collective-permute-done.24.a_ref = bf16[512,256]{1,0:T(8,128)(2,1)S(1)} collective-permute-done((bf16[512,256]{1,0:T(8,128)(2,1)S(1)}, bf16[512,256]{1,0:T(8,128)(2,1)S(1)}, u32[]{:S(2)}, u32[]{:S(2)}) %collective-permute-start.24) | collective-permute-done | bytes 262176 | tf_op jit(solution)/shard_map/ppermute | solution.py:57
  108.9 6.3 %collective-permute-done.25.b_ref = bf16[512,256]{1,0:T(8,128)(2,1)S(1)} collective-permute-done((bf16[512,256]{1,0:T(8,128)(2,1)S(1)}, bf16[512,256]{1,0:T(8,128)(2,1)S(1)}, u32[]{:S(2)}, u32[]{:S(2)}) %collective-permute-start.25) | collective-permute-done | bytes 262176 | tf_op jit(solution)/shard_map/ppermute | solution.py:57
  115.2 0.9 shard_map.109
  (43 shorter events, 0.8 us)
Async XLA Ops:
  3.1 17.4 %collective-permute-start = (bf16[288,1024]{1,0:T(8,128)(2,1)}, bf16[288,1024]{1,0:T(8,128)(2,1)S(1)}, u32[]{:S(2)}, u32[]{:S(2)}) collective-permute-start(bf16[288,1024]{1,0:T(8,128)(2,1)} %get-tuple-element.38.refs_0_), channel_id=1, source_target_pairs={{0,8},{8,16},{16,24},{24,0},{32,40},{40,48},{48,56},{56,32},{64,72... | collective-permute-start | bytes 1769480 | tf_op jit(solution)/shard_map/ppermute | solution.py:50
  5.2 19.2 %collective-permute-start.1 = (bf16[288,1024]{1,0:T(8,128)(2,1)}, bf16[288,1024]{1,0:T(8,128)(2,1)S(1)}, u32[]{:S(2)}, u32[]{:S(2)}) collective-permute-start(bf16[288,1024]{1,0:T(8,128)(2,1)} %get-tuple-element.38.refs_0_), channel_id=1, source_target_pairs={{0,24},{8,0},{16,8},{24,16},{32,56},{40,32},{48,40},{56,48},{64,88... | collective-permute-start | bytes 1769480 | tf_op jit(solution)/shard_map/ppermute | solution.py:50
  6.8 9.8 %collective-permute-start.4 = (bf16[272,256]{1,0:T(8,128)(2,1)}, bf16[272,256]{1,0:T(8,128)(2,1)S(1)}, u32[]{:S(2)}, u32[]{:S(2)}) collective-permute-start(bf16[272,256]{1,0:T(8,128)(2,1)} %get-tuple-element.39.refs_3_.refs_2_), channel_id=1, source_target_pairs={{0,64},{8,72},{16,80},{24,88},{32,96},{40,104},{48,112},{56,120},{... | collective-permute-start | bytes 417800 | tf_op jit(solution)/shard_map/ppermute | solution.py:43
  9.8 11.6 %collective-permute-start.6 = (bf16[272,256]{1,0:T(8,128)(2,1)}, bf16[272,256]{1,0:T(8,128)(2,1)S(1)}, u32[]{:S(2)}, u32[]{:S(2)}) collective-permute-start(bf16[272,256]{1,0:T(8,128)(2,1)} %get-tuple-element.39.refs_3_.refs_2_), channel_id=1, source_target_pairs={{0,192},{8,200},{16,208},{24,216},{32,224},{40,232},{48,240},{56,2... | collective-permute-start | bytes 417800 | tf_op jit(solution)/shard_map/ppermute | solution.py:43
  12.8 12.7 %collective-permute-start.10 = (bf16[272,256]{1,0:T(8,128)(2,1)}, bf16[272,256]{1,0:T(8,128)(2,1)S(1)}, u32[]{:S(2)}, u32[]{:S(2)}) collective-permute-start(bf16[272,256]{1,0:T(8,128)(2,1)} %get-tuple-element.39.refs_3_.refs_2_), channel_id=1, source_target_pairs={{0,224},{8,232},{16,240},{24,248},{32,0},{40,8},{48,16},{56,24},{6... | collective-permute-start | bytes 417800 | tf_op jit(solution)/shard_map/ppermute | solution.py:43
  16.6 9.8 %collective-permute-start.9 = (bf16[272,256]{1,0:T(8,128)(2,1)}, bf16[272,256]{1,0:T(8,128)(2,1)S(1)}, u32[]{:S(2)}, u32[]{:S(2)}) collective-permute-start(bf16[272,256]{1,0:T(8,128)(2,1)} %get-tuple-element.39.refs_3_.refs_2_), channel_id=1, source_target_pairs={{0,32},{8,40},{16,48},{24,56},{32,64},{40,72},{48,80},{56,88},{64,... | collective-permute-start | bytes 417800 | tf_op jit(solution)/shard_map/ppermute | solution.py:43
  20.4 17.6 %collective-permute-start.5 = (bf16[272,256]{1,0:T(8,128)(2,1)S(1)}, bf16[272,256]{1,0:T(8,128)(2,1)S(1)}, u32[]{:S(2)}, u32[]{:S(2)}) collective-permute-start(bf16[272,256]{1,0:T(8,128)(2,1)S(1)} %collective-permute-done.4.refs_6_.refs_5_), channel_id=1, source_target_pairs={{0,32},{8,40},{16,48},{24,56},{32,64},{40,72},{48,80},{56,88},{64,... | collective-permute-start | bytes 417800 | tf_op jit(solution)/shard_map/ppermute | solution.py:43
  21.4 16.7 %collective-permute-start.8 = (bf16[272,256]{1,0:T(8,128)(2,1)S(1)}, bf16[272,256]{1,0:T(8,128)(2,1)S(1)}, u32[]{:S(2)}, u32[]{:S(2)}) collective-permute-start(bf16[272,256]{1,0:T(8,128)(2,1)S(1)} %collective-permute-done.4.refs_6_.refs_5_), channel_id=1, source_target_pairs={{0,64},{8,72},{16,80},{24,88},{32,96},{40,104},{48,112},{56,120},{... | collective-permute-start | bytes 417800 | tf_op jit(solution)/shard_map/ppermute | solution.py:43
  24.5 13.6 %collective-permute-start.7 = (bf16[272,256]{1,0:T(8,128)(2,1)S(1)}, bf16[272,256]{1,0:T(8,128)(2,1)S(1)}, u32[]{:S(2)}, u32[]{:S(2)}) collective-permute-start(bf16[272,256]{1,0:T(8,128)(2,1)S(1)} %collective-permute-done.6.refs_7_.refs_6_), channel_id=1, source_target_pairs={{0,224},{8,232},{16,240},{24,248},{32,0},{40,8},{48,16},{56,24},{6... | collective-permute-start | bytes 417800 | tf_op jit(solution)/shard_map/ppermute | solution.py:43
  25.5 12.5 %collective-permute-start.2 = (bf16[144,1024]{1,0:T(8,128)(2,1)S(1)}, bf16[144,1024]{1,0:T(8,128)(2,1)S(1)}, u32[]{:S(2)}, u32[]{:S(2)}) collective-permute-start(bf16[144,1024]{1,0:T(8,128)(2,1)S(1)} %slice.8), channel_id=1, source_target_pairs={{0,8},{8,16},{16,24},{24,0},{32,40},{40,48},{48,56},{56,32},{64,72... | collective-permute-start | bytes 884744 | tf_op jit(solution)/shard_map/ppermute | solution.py:50
  26.4 11.7 %collective-permute-start.3 = (bf16[144,1024]{1,0:T(8,128)(2,1)S(1)}, bf16[144,1024]{1,0:T(8,128)(2,1)S(1)}, u32[]{:S(2)}, u32[]{:S(2)}) collective-permute-start(bf16[144,1024]{1,0:T(8,128)(2,1)S(1)} %slice.9), channel_id=1, source_target_pairs={{0,24},{8,0},{16,8},{24,16},{32,56},{40,32},{48,40},{56,48},{64,88... | collective-permute-start | bytes 884744 | tf_op jit(solution)/shard_map/ppermute | solution.py:50
  28.3 1.1 copy-start.7
  29.4 0.9 copy-start.8
  38.1 8.8 %copy-start.9 = (bf16[272,256]{1,0:T(8,128)(2,1)S(1)}, bf16[272,256]{1,0:T(8,128)(2,1)}, u32[]{:S(2)}) copy-start(bf16[272,256]{1,0:T(8,128)(2,1)} %get-tuple-element.39.refs_3_.refs_2_) | copy-start | bytes 417796
  46.8 5.6 %copy-start.10 = (s32[256]{0:T(256)S(1)}, s32[256]{0:T(256)}, u32[]{:S(2)}) copy-start(s32[256]{0:T(256)} %pos_hbm.1) | copy-start | bytes 3076
  46.8 10.9 %copy-start.1 = (bf16[4096,128]{1,0:T(8,128)(2,1)S(1)}, bf16[4096,128]{1,0:T(8,128)(2,1)}, u32[]{:S(2)}) copy-start(bf16[4096,128]{1,0:T(8,128)(2,1)} %wk_ref.1) | copy-start | bytes 3145732
  46.9 18.4 %copy-start = (bf16[4096,512]{1,0:T(8,128)(2,1)S(1)}, bf16[4096,512]{1,0:T(8,128)(2,1)}, u32[]{:S(2)}) copy-start(bf16[4096,512]{1,0:T(8,128)(2,1)} %refs_6_.1) | copy-start | bytes 12582916
  50.8 6.9 %collective-permute-start.13 = (bf16[512,256]{1,0:T(8,128)(2,1)S(1)}, bf16[512,256]{1,0:T(8,128)(2,1)S(1)}, u32[]{:S(2)}, u32[]{:S(2)}) collective-permute-start(bf16[512,256]{1,0:T(8,128)(2,1)S(1)} %get-tuple-element.52), channel_id=1, source_target_pairs={{0,16},{8,24},{16,0},{24,8},{32,48},{40,56},{48,32},{56,40},{64,80... | collective-permute-start | bytes 786440 | tf_op jit(solution)/shard_map/ppermute | solution.py:50
  50.9 13.1 %collective-permute-start.11 = (bf16[512,256]{1,0:T(8,128)(2,1)S(1)}, bf16[512,256]{1,0:T(8,128)(2,1)S(1)}, u32[]{:S(2)}, u32[]{:S(2)}) collective-permute-start(bf16[512,256]{1,0:T(8,128)(2,1)S(1)} %get-tuple-element.44), channel_id=1, source_target_pairs={{0,24},{8,0},{16,8},{24,16},{32,56},{40,32},{48,40},{56,48},{64,88... | collective-permute-start | bytes 786440 | tf_op jit(solution)/shard_map/ppermute | solution.py:50
  52.0 13.2 %collective-permute-start.12 = (bf16[512,256]{1,0:T(8,128)(2,1)S(1)}, bf16[512,256]{1,0:T(8,128)(2,1)S(1)}, u32[]{:S(2)}, u32[]{:S(2)}) collective-permute-start(bf16[512,256]{1,0:T(8,128)(2,1)S(1)} %get-tuple-element.45), channel_id=1, source_target_pairs={{0,8},{8,16},{16,24},{24,0},{32,40},{40,48},{48,56},{56,32},{64,72... | collective-permute-start | bytes 786440 | tf_op jit(solution)/shard_map/ppermute | solution.py:50
  52.5 16.6 %collective-permute-start.15 = (bf16[384,256]{1,0:T(8,128)(2,1)S(1)}, bf16[384,256]{1,0:T(8,128)(2,1)S(1)}, u32[]{:S(2)}, u32[]{:S(2)}) collective-permute-start(bf16[384,256]{1,0:T(8,128)(2,1)S(1)} %get-tuple-element.60), channel_id=1, source_target_pairs={{0,192},{8,200},{16,208},{24,216},{32,224},{40,232},{48,240},{56,2... | collective-permute-start | bytes 589832 | tf_op jit(solution)/shard_map/ppermute | solution.py:43
  54.8 14.2 %collective-permute-start.16 = (bf16[384,256]{1,0:T(8,128)(2,1)S(1)}, bf16[384,256]{1,0:T(8,128)(2,1)S(1)}, u32[]{:S(2)}, u32[]{:S(2)}) collective-permute-start(bf16[384,256]{1,0:T(8,128)(2,1)S(1)} %get-tuple-element.61), channel_id=1, source_target_pairs={{0,64},{8,72},{16,80},{24,88},{32,96},{40,104},{48,112},{56,120},{... | collective-permute-start | bytes 589832 | tf_op jit(solution)/shard_map/ppermute | solution.py:43
  57.7 37.7 %collective-permute-start.22 = (bf16[4096,128]{1,0:T(8,128)(2,1)S(1)}, bf16[4096,128]{1,0:T(8,128)(2,1)}, u32[]{:S(2)}, u32[]{:S(2)}) collective-permute-start(bf16[4096,128]{1,0:T(8,128)(2,1)S(1)} %copy-done.1), channel_id=1, source_target_pairs={{0,1},{1,0},{2,3},{3,2},{4,5},{5,4},{6,7},{7,6},{8,9},{9,8},{10,11... | collective-permute-start | bytes 3145736 | tf_op jit(solution)/shard_map/ppermute | solution.py:62
  64.0 31.4 %collective-permute-start.23 = (bf16[4096,128]{1,0:T(8,128)(2,1)}, bf16[4096,128]{1,0:T(8,128)(2,1)}, u32[]{:S(2)}, u32[]{:S(2)}) collective-permute-start(bf16[4096,128]{1,0:T(8,128)(2,1)} %wv_ref.1), channel_id=1, source_target_pairs={{0,1},{1,0},{2,3},{3,2},{4,5},{5,4},{6,7},{7,6},{8,9},{9,8},{10,11... | collective-permute-start | bytes 3145736 | tf_op jit(solution)/shard_map/ppermute | solution.py:62
  67.5 28.8 %collective-permute-start.14 = (bf16[4,512,256]{2,1,0:T(8,128)(2,1)}, bf16[4,512,256]{2,1,0:T(8,128)(2,1)}, u32[]{:S(2)}, u32[]{:S(2)}) collective-permute-start(bf16[4,512,256]{2,1,0:T(8,128)(2,1)} %get-tuple-element.54), channel_id=1, source_target_pairs={{0,1},{1,0},{2,3},{3,2},{4,5},{5,4},{6,7},{7,6},{8,9},{9,8},{10,11... | collective-permute-start | bytes 3145736 | tf_op jit(solution)/shard_map/ppermute | solution.py:62
  69.8 5.1 %collective-permute-start.17 = (bf16[256,256]{1,0:T(8,128)(2,1)S(1)}, bf16[256,256]{1,0:T(8,128)(2,1)S(1)}, u32[]{:S(2)}, u32[]{:S(2)}) collective-permute-start(bf16[256,256]{1,0:T(8,128)(2,1)S(1)} %get-tuple-element.62), channel_id=1, source_target_pairs={{0,192},{8,200},{16,208},{24,216},{32,224},{40,232},{48,240},{56,2... | collective-permute-start | bytes 393224 | tf_op jit(solution)/shard_map/ppermute | solution.py:43
  72.1 11.1 %collective-permute-start.18 = (bf16[256,256]{1,0:T(8,128)(2,1)S(1)}, bf16[256,256]{1,0:T(8,128)(2,1)S(1)}, u32[]{:S(2)}, u32[]{:S(2)}) collective-permute-start(bf16[256,256]{1,0:T(8,128)(2,1)S(1)} %get-tuple-element.63), channel_id=1, source_target_pairs={{0,64},{8,72},{16,80},{24,88},{32,96},{40,104},{48,112},{56,120},{... | collective-permute-start | bytes 393224 | tf_op jit(solution)/shard_map/ppermute | solution.py:43
  75.0 0.6 copy-start.2
  75.6 10.2 %collective-permute-start.19 = (bf16[256,256]{1,0:T(8,128)(2,1)}, bf16[256,256]{1,0:T(8,128)(2,1)}, u32[]{:S(2)}, u32[]{:S(2)}) collective-permute-start(bf16[256,256]{1,0:T(8,128)(2,1)} %get-tuple-element.64), channel_id=1, source_target_pairs={{0,224},{8,232},{16,240},{24,248},{32,0},{40,8},{48,16},{56,24},{6... | collective-permute-start | bytes 393224 | tf_op jit(solution)/shard_map/ppermute | solution.py:43
  83.2 0.7 copy-start.4
  83.8 5.3 %collective-permute-start.20 = (bf16[256,256]{1,0:T(8,128)(2,1)}, bf16[256,256]{1,0:T(8,128)(2,1)}, u32[]{:S(2)}, u32[]{:S(2)}) collective-permute-start(bf16[256,256]{1,0:T(8,128)(2,1)} %get-tuple-element.65), channel_id=1, source_target_pairs={{0,32},{8,40},{16,48},{24,56},{32,64},{40,72},{48,80},{56,88},{64,... | collective-permute-start | bytes 393224 | tf_op jit(solution)/shard_map/ppermute | solution.py:43
  89.2 0.9 copy-start.3
  90.1 0.9 copy-start.5
  91.0 0.7 copy-start.6
  92.8 3.6 %collective-permute-start.21 = (bf16[256,256]{1,0:T(8,128)(2,1)S(1)}, bf16[256,256]{1,0:T(8,128)(2,1)S(1)}, u32[]{:S(2)}, u32[]{:S(2)}) collective-permute-start(bf16[256,256]{1,0:T(8,128)(2,1)S(1)} %shard_map.107.x_ref), channel_id=1, source_target_pairs={{0,1},{1,0},{2,3},{3,2},{4,5},{5,4},{6,7},{7,6},{8,9},{9,8},{10,11... | collective-permute-start | bytes 393224 | tf_op jit(solution)/shard_map/ppermute | solution.py:62
  99.8 9.1 %collective-permute-start.24 = (bf16[512,256]{1,0:T(8,128)(2,1)S(1)}, bf16[512,256]{1,0:T(8,128)(2,1)S(1)}, u32[]{:S(2)}, u32[]{:S(2)}) collective-permute-start(bf16[512,256]{1,0:T(8,128)(2,1)S(1)} %get-tuple-element.68), channel_id=1, source_target_pairs={{0,4},{1,5},{2,6},{3,7},{4,0},{5,1},{6,2},{7,3},{8,12},{9,13},{10,... | collective-permute-start | bytes 786440 | tf_op jit(solution)/shard_map/ppermute | solution.py:57
  102.6 12.6 %collective-permute-start.25 = (bf16[512,256]{1,0:T(8,128)(2,1)S(1)}, bf16[512,256]{1,0:T(8,128)(2,1)S(1)}, u32[]{:S(2)}, u32[]{:S(2)}) collective-permute-start(bf16[512,256]{1,0:T(8,128)(2,1)S(1)} %get-tuple-element.69), channel_id=1, source_target_pairs={{0,2},{1,3},{2,4},{3,5},{4,6},{5,7},{6,0},{7,1},{8,10},{9,11},{10,... | collective-permute-start | bytes 786440 | tf_op jit(solution)/shard_map/ppermute | solution.py:57
  102.9 12.3 %collective-permute-start.26 = (bf16[512,256]{1,0:T(8,128)(2,1)S(1)}, bf16[512,256]{1,0:T(8,128)(2,1)S(1)}, u32[]{:S(2)}, u32[]{:S(2)}) collective-permute-start(bf16[512,256]{1,0:T(8,128)(2,1)S(1)} %get-tuple-element.70), channel_id=1, source_target_pairs={{0,6},{1,7},{2,0},{3,1},{4,2},{5,3},{6,4},{7,5},{8,14},{9,15},{10,... | collective-permute-start | bytes 786440 | tf_op jit(solution)/shard_map/ppermute | solution.py:57
